TPU v7x, 32 devices: a whole 2x2x4 slice. The times are simulated.
32 devices in a mesh: ctx: 16 (over z, y, x), fsdp: 2 (over core).
Axes of the slice: x: 2, y: 2, z: 4, core: 2. Of those that a mesh axis runs over, the one named last changes fastest.
Arguments:
- tokens: bfloat16 [4, 2048, 576], P('fsdp', 'ctx'), may hold values from -6 to 6
- positions: int32 [4, 2048], P('fsdp', 'ctx'), may hold values from 0 to 2047, as said below
- norm_attn: bfloat16 [2, 576], P(None, 'fsdp'), may hold values from 0.5 to 1.5
- w_query: bfloat16 [2, 576, 576], P(None, 'fsdp'), may hold values from -0.25 to 0.25
- w_key: bfloat16 [2, 576, 192], P(None, 'fsdp'), may hold values from -0.25 to 0.25
- w_value: bfloat16 [2, 576, 192], P(None, 'fsdp'), may hold values from -0.25 to 0.25
- w_out: bfloat16 [2, 576, 576], P(None, 'fsdp'), may hold values from -2 to 2
- norm_ffn: bfloat16 [2, 576], P(None, 'fsdp'), may hold values from 0.5 to 1.5
- w_gate: bfloat16 [2, 576, 1536], P(None, 'fsdp'), may hold values from -0.25 to 0.25
- w_up: bfloat16 [2, 576, 1536], P(None, 'fsdp'), may hold values from -0.25 to 0.25
- w_down: bfloat16 [2, 1536, 576], P(None, 'fsdp'), may hold values from -0.15625 to 0.15625
- cotangent: bfloat16 [4, 2048, 576], P('fsdp', 'ctx'), may hold values from -6 to 6
Outputs:
- output: bfloat16 [4, 2048, 576], P('fsdp', 'ctx')
- grad_tokens: float32 [4, 2048, 576], P('fsdp', 'ctx')
- grad_norm_attn: float32 [2, 576], P(None, 'fsdp')
- grad_query: float32 [2, 576, 576], P(None, 'fsdp')
- grad_key: float32 [2, 576, 192], P(None, 'fsdp')
- grad_value: float32 [2, 576, 192], P(None, 'fsdp')
- grad_out: float32 [2, 576, 576], P(None, 'fsdp')
- grad_norm_ffn: float32 [2, 576], P(None, 'fsdp')
- grad_gate: float32 [2, 576, 1536], P(None, 'fsdp')
- grad_up: float32 [2, 576, 1536], P(None, 'fsdp')
- grad_down: float32 [2, 1536, 576], P(None, 'fsdp')
Inputs may be any that keep to these rules, and one draw needn't show every extreme that they name: For each sequence the 2048 positions are 0 .. 2047 once each; index c of ctx holds, in order, the two runs of 64 consecutive positions of blocks b and 31 - b, with b a permutation over the devices drawn per sequence.
All inputs are finite; a program needn't handle non-finite values.
Results may differ from a plain program's by a relative error of at most 0.02.
Values may be sent and summed in bfloat16 or wider, within the bound.
A program may use at most 320 MiB of HBM per device.

v0:
```python
import jax
import jax.numpy as jnp
from jax import lax
from jax.sharding import PartitionSpec as P

HEADS = 9
KV_HEADS = 3
HEAD = 64


EPS = 1e-05
ROPE_BASE = 100000.0


def rotate(tensor, positions_row, direction_sign):
    half_size = tensor.shape[-1] // 2
    frequency = jnp.exp(
        jnp.arange(half_size, dtype=jnp.float32) * (-jnp.log(ROPE_BASE) / half_size)
    )
    angles = positions_row.astype(jnp.float32)[..., None] * frequency
    cosine = jnp.cos(angles)[..., None, :]
    sine_part = direction_sign * jnp.sin(angles)[..., None, :]
    first_half = tensor[..., :half_size]
    second_half = tensor[..., half_size:]
    return jnp.concatenate(
        [
            first_half * cosine - second_half * sine_part,
            second_half * cosine + first_half * sine_part,
        ],
        axis=-1,
    )


def normalize(values, gain):
    return values * lax.rsqrt(jnp.mean(values * values, axis=-1, keepdims=True) + EPS) * gain


def normalize_back(values, gain, incoming):
    inverse = lax.rsqrt(jnp.mean(values * values, axis=-1, keepdims=True) + EPS)
    scaled = incoming * gain
    grad_values = inverse * scaled - values * (inverse * inverse * inverse) * jnp.mean(
        scaled * values, axis=-1, keepdims=True
    )
    grad_gain = jnp.sum(incoming * values * inverse, axis=(0, 1))
    return (grad_values, grad_gain)


def scores_of(queries, keys_all, query_places, key_places):
    raw_scores = jnp.einsum(
        "qhge,khe->hgqk", queries, keys_all, preferred_element_type=jnp.float32
    ) * queries.shape[-1] ** (-0.5)
    visible = key_places[None, :] <= query_places[:, None]
    return jnp.where(visible[None, None], raw_scores, -1e30)


def attend(operands):
    queries, keys_all, values_all, query_places, key_places = operands
    scores = scores_of(queries, keys_all, query_places, key_places)
    row_top = jnp.max(scores, axis=-1, keepdims=True)
    exponent = jnp.exp(scores - row_top)
    row_total = jnp.sum(exponent, axis=-1, keepdims=True)
    probabilities = (exponent / row_total).astype(jnp.bfloat16)
    mixed = jnp.einsum(
        "hgqk,khe->qhge", probabilities, values_all, preferred_element_type=jnp.float32
    )
    return (mixed, row_top + jnp.log(row_total))


def attend_back(operands):
    queries, keys_all, values_all, query_places, key_places, log_total, grad_mixed = operands
    score_scale = queries.shape[-1] ** (-0.5)
    scores = scores_of(queries, keys_all, query_places, key_places)
    probabilities = jnp.exp(scores - log_total)
    grad_probs = jnp.einsum(
        "qhge,khe->hgqk", grad_mixed, values_all, preferred_element_type=jnp.float32
    )
    grad_scores = (
        probabilities * (grad_probs - jnp.sum(probabilities * grad_probs, axis=-1, keepdims=True))
    ).astype(jnp.bfloat16)
    grad_queries = (
        jnp.einsum("hgqk,khe->qhge", grad_scores, keys_all, preferred_element_type=jnp.float32)
        * score_scale
    )
    grad_keys = (
        jnp.einsum("hgqk,qhge->khe", grad_scores, queries, preferred_element_type=jnp.float32)
        * score_scale
    )
    grad_values = jnp.einsum(
        "hgqk,qhge->khe",
        probabilities.astype(jnp.bfloat16),
        grad_mixed,
        preferred_element_type=jnp.float32,
    )
    return (grad_queries, grad_keys, grad_values)


def layer_forward(inputs, positions, places, weights):
    gain_attn, w_query, w_key, w_value, w_out, gain_ffn, w_gate, w_up, w_down = weights
    seq_count, row_count, model_width = inputs.shape
    normed = normalize(inputs, gain_attn).astype(jnp.bfloat16)
    query_pre = jnp.einsum("srd,de->sre", normed, w_query, preferred_element_type=jnp.float32)
    key_pre = jnp.einsum("srd,de->sre", normed, w_key, preferred_element_type=jnp.float32)
    value_pre = jnp.einsum("srd,de->sre", normed, w_value, preferred_element_type=jnp.float32)
    queries = rotate(query_pre.reshape(seq_count, row_count, HEADS, HEAD), positions, 1.0).astype(
        jnp.bfloat16
    )
    queries = queries.reshape(seq_count, row_count, KV_HEADS, HEADS // KV_HEADS, HEAD)
    keys_own = rotate(key_pre.reshape(seq_count, row_count, KV_HEADS, HEAD), positions, 1.0).astype(
        jnp.bfloat16
    )
    keys_own = keys_own.reshape(seq_count, row_count, KV_HEADS * HEAD)
    values_own = value_pre.astype(jnp.bfloat16)
    keys_all, values_all = (
        lax.all_gather(keys_own, "ctx", axis=1, tiled=True),
        lax.all_gather(values_own, "ctx", axis=1, tiled=True),
    )
    length = keys_all.shape[1]
    mixed, log_total = lax.map(
        attend,
        (
            queries,
            keys_all.reshape(seq_count, length, KV_HEADS, HEAD),
            values_all.reshape(seq_count, length, KV_HEADS, HEAD),
            positions,
            places,
        ),
    )
    mixed_low = mixed.reshape(seq_count, row_count, model_width).astype(jnp.bfloat16)
    middle = inputs + jnp.einsum(
        "srd,de->sre", mixed_low, w_out, preferred_element_type=jnp.float32
    )
    normed_ffn = normalize(middle, gain_ffn).astype(jnp.bfloat16)
    gate_pre = jnp.einsum("srd,df->srf", normed_ffn, w_gate, preferred_element_type=jnp.float32)
    up_pre = jnp.einsum("srd,df->srf", normed_ffn, w_up, preferred_element_type=jnp.float32)
    hidden = (jax.nn.silu(gate_pre) * up_pre).astype(jnp.bfloat16)
    result = middle + jnp.einsum("srf,fd->srd", hidden, w_down, preferred_element_type=jnp.float32)
    record = (
        inputs,
        normed,
        queries,
        keys_own,
        values_own,
        keys_all,
        values_all,
        log_total,
        mixed_low,
        middle,
        normed_ffn,
        gate_pre,
        up_pre,
        hidden,
    )
    return (result, record)


def layer_backward(gradient, record, weights, positions, places):
    gain_attn, w_query, w_key, w_value, w_out, gain_ffn, w_gate, w_up, w_down = weights
    (
        inputs,
        normed,
        queries,
        keys_own,
        values_own,
        kept_keys,
        kept_values,
        log_total,
        mixed_low,
        middle,
        normed_ffn,
        gate_pre,
        up_pre,
        hidden,
    ) = record
    seq_count, row_count, model_width = inputs.shape
    grad_low = gradient.astype(jnp.bfloat16)
    grad_wdown = jnp.einsum("srf,srd->fd", hidden, grad_low, preferred_element_type=jnp.float32)
    grad_hidden = jnp.einsum("srd,fd->srf", grad_low, w_down, preferred_element_type=jnp.float32)
    sigmoid_gate = jax.nn.sigmoid(gate_pre)
    grad_gate = (
        grad_hidden * up_pre * sigmoid_gate * (1.0 + gate_pre * (1.0 - sigmoid_gate))
    ).astype(jnp.bfloat16)
    grad_up = (grad_hidden * gate_pre * sigmoid_gate).astype(jnp.bfloat16)
    grad_wgate = jnp.einsum(
        "srd,srf->df", normed_ffn, grad_gate, preferred_element_type=jnp.float32
    )
    grad_wup = jnp.einsum("srd,srf->df", normed_ffn, grad_up, preferred_element_type=jnp.float32)
    grad_normed_ffn = jnp.einsum(
        "srf,df->srd", grad_gate, w_gate, preferred_element_type=jnp.float32
    ) + jnp.einsum("srf,df->srd", grad_up, w_up, preferred_element_type=jnp.float32)
    grad_middle_norm, grad_gain_ffn = normalize_back(middle, gain_ffn, grad_normed_ffn)
    grad_middle = gradient + grad_middle_norm
    branch_low = grad_middle.astype(jnp.bfloat16)
    grad_wout = jnp.einsum("srd,sre->de", mixed_low, branch_low, preferred_element_type=jnp.float32)
    grad_mixed = jnp.einsum(
        "sre,de->srd", branch_low, w_out, preferred_element_type=jnp.float32
    ).astype(jnp.bfloat16)
    grad_mixed = grad_mixed.reshape(seq_count, row_count, KV_HEADS, HEADS // KV_HEADS, HEAD)
    keys_all, values_all = (
        lax.all_gather(keys_own, "ctx", axis=1, tiled=True),
        lax.all_gather(values_own, "ctx", axis=1, tiled=True),
    )
    length = keys_all.shape[1]
    grad_queries, grad_keys_all, grad_values_all = lax.map(
        attend_back,
        (
            queries,
            keys_all.reshape(seq_count, length, KV_HEADS, HEAD),
            values_all.reshape(seq_count, length, KV_HEADS, HEAD),
            positions,
            places,
            log_total,
            grad_mixed,
        ),
    )
    grad_keys, grad_values = (
        lax.psum_scatter(
            grad_keys_all.reshape(seq_count, length, KV_HEADS * HEAD),
            "ctx",
            scatter_dimension=1,
            tiled=True,
        ),
        lax.psum_scatter(
            grad_values_all.reshape(seq_count, length, KV_HEADS * HEAD),
            "ctx",
            scatter_dimension=1,
            tiled=True,
        ),
    )
    grad_query_pre = (
        rotate(grad_queries.reshape(seq_count, row_count, HEADS, HEAD), positions, -1.0)
        .reshape(seq_count, row_count, model_width)
        .astype(jnp.bfloat16)
    )
    grad_key_pre = (
        rotate(grad_keys.reshape(seq_count, row_count, KV_HEADS, HEAD), positions, -1.0)
        .reshape(seq_count, row_count, KV_HEADS * HEAD)
        .astype(jnp.bfloat16)
    )
    grad_value_pre = grad_values.astype(jnp.bfloat16)
    grad_wquery = jnp.einsum(
        "srd,sre->de", normed, grad_query_pre, preferred_element_type=jnp.float32
    )
    grad_wkey = jnp.einsum("srd,sre->de", normed, grad_key_pre, preferred_element_type=jnp.float32)
    grad_wvalue = jnp.einsum(
        "srd,sre->de", normed, grad_value_pre, preferred_element_type=jnp.float32
    )
    grad_normed = jnp.einsum(
        "sre,de->srd", grad_query_pre, w_query, preferred_element_type=jnp.float32
    )
    grad_normed = grad_normed + jnp.einsum(
        "sre,de->srd", grad_key_pre, w_key, preferred_element_type=jnp.float32
    )
    grad_normed = grad_normed + jnp.einsum(
        "sre,de->srd", grad_value_pre, w_value, preferred_element_type=jnp.float32
    )
    grad_input_norm, grad_gain_attn = normalize_back(inputs, gain_attn, grad_normed)
    layer_grads = (
        grad_gain_attn,
        grad_wquery,
        grad_wkey,
        grad_wvalue,
        grad_wout,
        grad_gain_ffn,
        grad_wgate,
        grad_wup,
        grad_wdown,
    )
    return (grad_middle + grad_input_norm, layer_grads)


def body(
    tokens,
    positions,
    norm_attn,
    w_query,
    w_key,
    w_value,
    w_out,
    norm_ffn,
    w_gate,
    w_up,
    w_down,
    cotangent,
):
    layer_count = norm_attn.shape[0]
    places = lax.all_gather(positions, "ctx", axis=1, tiled=True)
    current = tokens.astype(jnp.float32)
    records = []
    gathered_weights = []
    for layer_index in range(layer_count):
        weights = (
            lax.all_gather(norm_attn[layer_index], "fsdp", axis=0, tiled=True),
            lax.all_gather(w_query[layer_index], "fsdp", axis=0, tiled=True),
            lax.all_gather(w_key[layer_index], "fsdp", axis=0, tiled=True),
            lax.all_gather(w_value[layer_index], "fsdp", axis=0, tiled=True),
            lax.all_gather(w_out[layer_index], "fsdp", axis=0, tiled=True),
            lax.all_gather(norm_ffn[layer_index], "fsdp", axis=0, tiled=True),
            lax.all_gather(w_gate[layer_index], "fsdp", axis=0, tiled=True),
            lax.all_gather(w_up[layer_index], "fsdp", axis=0, tiled=True),
            lax.all_gather(w_down[layer_index], "fsdp", axis=0, tiled=True),
        )
        current, record = layer_forward(current, positions, places, weights)
        records.append(record)
        gathered_weights.append(weights)
    output = current.astype(jnp.bfloat16)
    gradient = cotangent.astype(jnp.float32)
    collected = []
    for layer_index in reversed(range(layer_count)):
        weights = (
            lax.all_gather(norm_attn[layer_index], "fsdp", axis=0, tiled=True),
            lax.all_gather(w_query[layer_index], "fsdp", axis=0, tiled=True),
            lax.all_gather(w_key[layer_index], "fsdp", axis=0, tiled=True),
            lax.all_gather(w_value[layer_index], "fsdp", axis=0, tiled=True),
            lax.all_gather(w_out[layer_index], "fsdp", axis=0, tiled=True),
            lax.all_gather(norm_ffn[layer_index], "fsdp", axis=0, tiled=True),
            lax.all_gather(w_gate[layer_index], "fsdp", axis=0, tiled=True),
            lax.all_gather(w_up[layer_index], "fsdp", axis=0, tiled=True),
            lax.all_gather(w_down[layer_index], "fsdp", axis=0, tiled=True),
        )
        gradient, layer_grads = layer_backward(
            gradient, records[layer_index], weights, positions, places
        )
        shares = (
            lax.psum_scatter(
                layer_grads[0].astype(jnp.bfloat16), "fsdp", scatter_dimension=0, tiled=True
            ).astype(jnp.float32),
            lax.psum_scatter(
                layer_grads[1].astype(jnp.bfloat16), "fsdp", scatter_dimension=0, tiled=True
            ).astype(jnp.float32),
            lax.psum_scatter(
                layer_grads[2].astype(jnp.bfloat16), "fsdp", scatter_dimension=0, tiled=True
            ).astype(jnp.float32),
            lax.psum_scatter(
                layer_grads[3].astype(jnp.bfloat16), "fsdp", scatter_dimension=0, tiled=True
            ).astype(jnp.float32),
            lax.psum_scatter(
                layer_grads[4].astype(jnp.bfloat16), "fsdp", scatter_dimension=0, tiled=True
            ).astype(jnp.float32),
            lax.psum_scatter(
                layer_grads[5].astype(jnp.bfloat16), "fsdp", scatter_dimension=0, tiled=True
            ).astype(jnp.float32),
            lax.psum_scatter(
                layer_grads[6].astype(jnp.bfloat16), "fsdp", scatter_dimension=0, tiled=True
            ).astype(jnp.float32),
            lax.psum_scatter(
                layer_grads[7].astype(jnp.bfloat16), "fsdp", scatter_dimension=0, tiled=True
            ).astype(jnp.float32),
            lax.psum_scatter(
                layer_grads[8].astype(jnp.bfloat16), "fsdp", scatter_dimension=0, tiled=True
            ).astype(jnp.float32),
        )
        totals = lax.psum(
            (
                shares[0],
                shares[1],
                shares[2],
                shares[3],
                shares[4],
                shares[5],
                shares[6],
                shares[7],
                shares[8],
            ),
            "ctx",
        )
        collected.insert(0, totals)
    stacked = tuple(
        (jnp.stack([entry_totals[member] for entry_totals in collected]) for member in range(9))
    )
    return (
        output,
        gradient,
        stacked[0],
        stacked[1],
        stacked[2],
        stacked[3],
        stacked[4],
        stacked[5],
        stacked[6],
        stacked[7],
        stacked[8],
    )


def solution(mesh):
    in_specs = (
        P("fsdp", "ctx", None),
        P("fsdp", "ctx"),
        P(None, "fsdp"),
        P(None, "fsdp", None),
        P(None, "fsdp", None),
        P(None, "fsdp", None),
        P(None, "fsdp", None),
        P(None, "fsdp"),
        P(None, "fsdp", None),
        P(None, "fsdp", None),
        P(None, "fsdp", None),
        P("fsdp", "ctx", None),
    )
    out_specs = (
        P("fsdp", "ctx", None),
        P("fsdp", "ctx", None),
        P(None, "fsdp"),
        P(None, "fsdp", None),
        P(None, "fsdp", None),
        P(None, "fsdp", None),
        P(None, "fsdp", None),
        P(None, "fsdp"),
        P(None, "fsdp", None),
        P(None, "fsdp", None),
        P(None, "fsdp", None),
    )
    return jax.shard_map(body, mesh=mesh, in_specs=in_specs, out_specs=out_specs, check_vma=False)
```

profile of v0, /device:TPU:10, one launch (start us, length us, event | category | flops | bytes accessed | tf_op | source)
XLA Modules:
  0.0 1768.8 jit_solution(10200862059027686231)
XLA Ops:
  31.3 30.2 %all_gather.94 = s32[2,2048]{1,0:T(2,128)S(1)} all-gather(s32[2,128]{1,0:T(2,128)S(1)} %copy-done.116), channel_id=1, replica_groups=mesh['ctx'=16,'fsdp'=2] {'ctx'}, dimensions={1}, use_global_device_ids=true | all-gather | bytes 17408 | tf_op jit(solution)/shard_map/all_gather | solution.py:286
  74.8 57.7 %all-gather.31.cloned.1.call-done = bf16[2,2048,192]{1,2,0:T(8,128)(2,1)} async-done(((bf16[2,128,192]{1,2,0:T(8,128)(2,1)}), bf16[2,2048,192]{1,2,0:T(8,128)(2,1)}) %all-gather.31.cloned.1.call-update) | async-done | bytes 1572880 | tf_op jit(solution)/shard_map/all_gather | solution.py:114
  132.5 15.5 while.52
  162.7 8.7 all-gather.41.cloned.1.call-done
  190.5 53.1 %all-gather.33.cloned.1.call-done = bf16[2,2048,192]{1,2,0:T(8,128)(2,1)} async-done(((bf16[2,128,192]{1,2,0:T(8,128)(2,1)}), bf16[2,2048,192]{1,2,0:T(8,128)(2,1)}) %all-gather.33.cloned.1.call-update) | async-done | bytes 1572880 | tf_op jit(solution)/shard_map/all_gather | solution.py:115
  243.7 58.3 %all-gather.35.cloned.1.call-done = bf16[2,2048,192]{1,2,0:T(8,128)(2,1)} async-done(((bf16[2,128,192]{1,2,0:T(8,128)(2,1)}), bf16[2,2048,192]{1,2,0:T(8,128)(2,1)}) %all-gather.35.cloned.1.call-update) | async-done | bytes 1572880 | tf_op jit(solution)/shard_map/all_gather | solution.py:114
  302.0 15.5 while.53
  342.7 63.7 %while.54 = (s32[]{:T(128)}, f32[2,128,3,3,64]{1,4,3,2,0:T(8,128)}, f32[2,2048,3,64]{1,3,2,0:T(8,128)}, f32[2,2048,3,64]{1,3,2,0:T(8,128)}, bf16[2,2048,3,64]{1,...) while((s32[]{:T(128)}, f32[2,128,3,3,64]{1,4,3,2,0:T(8,128)}, ...), condition=%wide.region_15.16_spmd, body=%wide.region_13.15_spmd.sunk | while | flops 1546066816 | bytes 160072944 | solution.py:203
  350.6 11.1 fusion.326
  382.4 11.1 fusion.326
  419.8 120.3 %reduce-scatter.19.cloned.1.call-done = f32[2,128,192]{1,2,0:T(8,128)} async-done(((f32[2,2048,192]{1,2,0:T(8,128)}), f32[2,128,192]{1,2,0:T(8,128)}) %reduce-scatter.19.cloned.1.call-update) | async-done | bytes 196624 | tf_op jit(solution)/shard_map/reduce_scatter | solution.py:216
  542.7 134.7 %reduce-scatter.21.cloned.1.call-done = f32[2,128,192]{1,2,0:T(8,128)} async-done(((f32[2,2048,192]{1,2,0:T(8,128)}), f32[2,128,192]{1,2,0:T(8,128)}) %reduce-scatter.21.cloned.1.call-update) | async-done | bytes 196624 | tf_op jit(solution)/shard_map/reduce_scatter | solution.py:222
  695.2 65.1 %while.55 = (s32[]{:T(128)}, f32[2,128,3,3,64]{1,4,3,2,0:T(8,128)}, f32[2,2048,3,64]{1,3,2,0:T(8,128)}, f32[2,2048,3,64]{1,3,2,0:T(8,128)}, bf16[2,2048,3,64]{1,...) while((s32[]{:T(128)}, f32[2,128,3,3,64]{1,4,3,2,0:T(8,128)}, ...), condition=%wide.region_22.23_spmd, body=%wide.region_20.22_spmd.sunk | while | flops 1546066816 | bytes 160072944 | solution.py:203
  703.1 11.7 fusion.341
  736.1 11.2 fusion.341
  794.2 11.0 reduce-scatter.43.cloned.1.call-done
  807.7 136.5 %reduce-scatter.23.cloned.1.call-done = f32[2,128,192]{1,2,0:T(8,128)} async-done(((f32[2,2048,192]{1,2,0:T(8,128)}), f32[2,128,192]{1,2,0:T(8,128)}) %reduce-scatter.23.cloned.1.call-update) | async-done | bytes 196624 | tf_op jit(solution)/shard_map/reduce_scatter | solution.py:216
  946.3 9.0 reduce-scatter.47.cloned.1.call-done
  957.8 136.5 %reduce-scatter.25.cloned.1.call-done = f32[2,128,192]{1,2,0:T(8,128)} async-done(((f32[2,2048,192]{1,2,0:T(8,128)}), f32[2,128,192]{1,2,0:T(8,128)}) %reduce-scatter.25.cloned.1.call-update) | async-done | bytes 196624 | tf_op jit(solution)/shard_map/reduce_scatter | solution.py:222
  1096.3 8.9 reduce-scatter.51.cloned.1.call-done
  1107.8 9.1 reduce-scatter.31.cloned.1.call-done
  1118.5 10.1 reduce-scatter.35.cloned.1.call-done
  1139.3 33.4 %all-reduce.8 = (f32[1,288]{1,0:T(1,128)S(1)}, f32[1,288]{1,0:T(1,128)S(1)}, f32[1,288]{1,0:T(1,128)S(1)}, f32[1,288]{1,0:T(1,128)S(1)}) all-reduce(f32[1,288]{1,0:T(1,128)S(1)} %stack.82, f32[1,288]{1,0:T(1,128)S(1)} %stack.81, f32[1,288]{1,0:T(1,128)S(1)} %stack.97, ...), channel_id=1, replica_groups=mesh['ctx'=16,'fsdp'=2] {'ctx'}, use_global_device_ids=true, to_apply=%region_31.32 | all-reduce | flops 1152 | bytes 9216 | tf_op jit(solution)/shard_map/psum | solution.py:352
  1174.9 574.1 %all-reduce.14.cloned.1.call-done = (f32[1,288,576]{2,1,0:T(8,128)}, f32[1,288,576]{2,1,0:T(8,128)}, f32[1,288,192]{2,1,0:T(8,128)}, f32[1,288,192]{2,1,0:T(8,12...) async-done(((f32[1,288,576]{2,1,0:T(8,128)}, ...) | async-done | bytes 14155792 | tf_op jit(solution)/shard_map/psum | solution.py:352
  (541 shorter events, 314.2 us)
Async XLA Ops:
  18.8 113.7 %all-gather.31.cloned.1.call-start = ((), (), s32[]{:S(2)}) async-start(), calls=%async_computation.19 | async-start | bytes 1671168 | tf_op jit(solution)/shard_map/all_gather | solution.py:114
  24.8 124.5 %all-gather.37.cloned.1.call-start = ((), (), s32[]{:S(2)}) async-start(), calls=%async_computation.40 | async-start | bytes 2654208 | tf_op jit(solution)/shard_map/all_gather | solution.py:298
  26.2 132.4 %all-gather.39.cloned.1.call-start = ((), (), s32[]{:S(2)}) async-start(), calls=%async_computation.41 | async-start | bytes 2654208 | tf_op jit(solution)/shard_map/all_gather | solution.py:299
  29.2 142.2 %all-gather.41.cloned.1.call-start = ((), (), s32[]{:S(2)}) async-start(), calls=%async_computation.42 | async-start | bytes 2654208 | tf_op jit(solution)/shard_map/all_gather | solution.py:300
  30.6 155.9 %all-gather.47.cloned.1.call-start = ((), (), s32[]{:S(2)}) async-start(), calls=%async_computation.45 | async-start | bytes 2654208 | tf_op jit(solution)/shard_map/all_gather | solution.py:300
  31.2 212.5 %all-gather.33.cloned.1.call-start = ((), (), s32[]{:S(2)}) async-start(), calls=%async_computation.20 | async-start | bytes 1671168 | tf_op jit(solution)/shard_map/all_gather | solution.py:115
  175.2 126.8 %all-gather.35.cloned.1.call-start = ((), (), s32[]{:S(2)}) async-start(), calls=%async_computation.21 | async-start | bytes 1671168 | tf_op jit(solution)/shard_map/all_gather | solution.py:114
  179.8 138.4 %all-gather.45.cloned.1.call-start = ((), (), s32[]{:S(2)}) async-start(), calls=%async_computation.44 | async-start | bytes 2654208 | tf_op jit(solution)/shard_map/all_gather | solution.py:299
  180.5 147.6 %all-gather.43.cloned.1.call-start = ((), (), s32[]{:S(2)}) async-start(), calls=%async_computation.43 | async-start | bytes 2654208 | tf_op jit(solution)/shard_map/all_gather | solution.py:298
  181.1 359.0 %reduce-scatter.19.cloned.1.call-start = ((), (), s32[]{:S(2)}) async-start(), calls=%async_computation.22 | async-start | bytes 3342336 | tf_op jit(solution)/shard_map/reduce_scatter | solution.py:216
  406.5 270.9 %reduce-scatter.21.cloned.1.call-start = ((), (), s32[]{:S(2)}) async-start(), calls=%async_computation.23 | async-start | bytes 3342336 | tf_op jit(solution)/shard_map/reduce_scatter | solution.py:222
  407.1 365.1 %reduce-scatter.29.cloned.1.call-start = ((), (), s32[]{:S(2)}) async-start(), calls=%async_computation.27 | async-start | bytes 1105920 | tf_op jit(solution)/shard_map/reduce_scatter | solution.py:327
  409.0 367.0 %reduce-scatter.41.cloned.1.call-start = ((), (), s32[]{:S(2)}) async-start(), calls=%async_computation.33 | async-start | bytes 1105920 | tf_op jit(solution)/shard_map/reduce_scatter | solution.py:336
  410.4 367.5 %reduce-scatter.53.cloned.1.call-start = ((), (), s32[]{:S(2)}) async-start(), calls=%async_computation.39 | async-start | bytes 2654208 | tf_op jit(solution)/shard_map/reduce_scatter | solution.py:348
  413.5 367.0 %reduce-scatter.45.cloned.1.call-start = ((), (), s32[]{:S(2)}) async-start(), calls=%async_computation.35 | async-start | bytes 2654208 | tf_op jit(solution)/shard_map/reduce_scatter | solution.py:342
  416.6 366.5 %reduce-scatter.49.cloned.1.call-start = ((), (), s32[]{:S(2)}) async-start(), calls=%async_computation.37 | async-start | bytes 2654208 | tf_op jit(solution)/shard_map/reduce_scatter | solution.py:345
  419.8 366.0 %reduce-scatter.33.cloned.1.call-start = ((), (), s32[]{:S(2)}) async-start(), calls=%async_computation.29 | async-start | bytes 442368 | tf_op jit(solution)/shard_map/reduce_scatter | solution.py:330
  768.2 176.0 %reduce-scatter.23.cloned.1.call-start = ((), (), s32[]{:S(2)}) async-start(), calls=%async_computation.24 | async-start | bytes 3342336 | tf_op jit(solution)/shard_map/reduce_scatter | solution.py:216
  769.0 186.3 %reduce-scatter.47.cloned.1.call-start = ((), (), s32[]{:S(2)}) async-start(), calls=%async_computation.36 | async-start | bytes 2654208 | tf_op jit(solution)/shard_map/reduce_scatter | solution.py:345
  771.3 323.0 %reduce-scatter.25.cloned.1.call-start = ((), (), s32[]{:S(2)}) async-start(), calls=%async_computation.25 | async-start | bytes 3342336 | tf_op jit(solution)/shard_map/reduce_scatter | solution.py:222
  772.1 333.2 %reduce-scatter.51.cloned.1.call-start = ((), (), s32[]{:S(2)}) async-start(), calls=%async_computation.38 | async-start | bytes 2654208 | tf_op jit(solution)/shard_map/reduce_scatter | solution.py:348
  775.9 340.9 %reduce-scatter.31.cloned.1.call-start = ((), (), s32[]{:S(2)}) async-start(), calls=%async_computation.28 | async-start | bytes 442368 | tf_op jit(solution)/shard_map/reduce_scatter | solution.py:330
  946.2 182.3 %reduce-scatter.35.cloned.1.call-start = ((), (), s32[]{:S(2)}) async-start(), calls=%async_computation.30 | async-start | bytes 442368 | tf_op jit(solution)/shard_map/reduce_scatter | solution.py:333
  1096.3 652.8 %all-reduce.14.cloned.1.call-start = ((), (), s32[]{:S(2)}) async-start(), calls=%async_computation.46 | async-start | bytes 29491200 | tf_op jit(solution)/shard_map/psum | solution.py:352
  (131 other events, 2696.2 us)
Sparse Core Ops, SparseCore 0:
  18.9 55.8 all-gather.28
  77.5 54.9 all-gather.30
  134.7 10.6 all-gather.36
  147.4 11.2 all-gather.38
  160.0 11.2 all-gather.40
  173.3 11.4 all-gather.46
  188.1 55.5 all-gather.32
  247.0 54.9 all-gather.34
  304.1 10.6 all-gather.44
  316.8 11.2 all-gather.42
  406.5 133.5 reduce-scatter.18
  545.5 131.7 reduce-scatter.20
  689.3 9.1 reduce-scatter.40
  700.7 10.4 reduce-scatter.52
  713.9 10.5 reduce-scatter.44
  726.6 10.5 reduce-scatter.48
  739.9 8.8 reduce-scatter.32
  771.5 9.1 reduce-scatter.26
  783.0 9.2 reduce-scatter.38
  794.5 10.5 reduce-scatter.42
  810.7 133.4 reduce-scatter.22
  946.3 8.8 reduce-scatter.46
  960.8 133.4 reduce-scatter.24
  1136.1 612.8 all-reduce.13
  (5 shorter events, 40.7 us)
where the time goes:
time: 1780 us; the launch traced here: 1770 us
  waiting for transfers between devices  1350 us (76%)
  matrix products  171 us (10%)
  other arithmetic  109 us (6%)
  blocking collectives  88 us (5%)
  local copies, waits for them, and re-layouts  34.3 us (2%)
    psum x1, waiting for transfers between devices, body(): lax.psum((shares[0], shares[1], shares[2], shares[3], shares[4], shares[5...  574 us
    reduce_scatter x2, waiting for transfers between devices, layer_backward(): lax.psum_scatter(grad_values_all.reshape(seq_count, length, KV_HEADS * HE...  271 us
    reduce_scatter x2, waiting for transfers between devices, layer_backward(): lax.psum_scatter(grad_keys_all.reshape(seq_count, length, KV_HEADS * HEAD...  257 us
    all_gather x2, waiting for transfers between devices, layer_forward(): lax.all_gather(keys_own, 'ctx', axis=1, tiled=True)  116 us
    all_gather x2, waiting for transfers between devices, layer_forward(): lax.all_gather(values_own, 'ctx', axis=1, tiled=True)  54.6 us
    convert_element_type x4, other arithmetic, attend_back(): grad_scores = (probabilities * (grad_probs - jnp.sum(probabilities * grad...  45 us
    another operation x20, other arithmetic, body(): jnp.stack([entry_totals[member] for entry_totals in collected])  41.6 us
  transfers between devices with their start and end apart: 29, of which 18 were waited for; matrix products, arithmetic and copies ran while one was open for 12% of the time, Pallas kernels for 0%

commit v1 on v0

--- a/solution.py
+++ b/solution.py
@@ -1,6 +1,345 @@
+import functools, itertools
 import jax
 import jax.numpy as jnp
 from jax import lax
+from jax.experimental import pallas as pl
+from jax.experimental.pallas import tpu as pltpu
+
+CTX, FSDP = "ctx", "fsdp"
+MESH = pl.DeviceIdType.MESH
+
+
+def factors(n):
+    known = {16: (4, 2, 2), 64: (2, 4, 4, 2)}
+    if n in known:
+        return known[n]
+    out, p = [], 2
+    while n > 1:
+        while n % p == 0:
+            out.append(p)
+            n //= p
+        p += 1
+    return tuple(out) or (1,)
+
+
+class Grid:
+    def __init__(self, n):
+        self.n = n
+        self.dims = factors(n)
+        strides, s = [], 1
+        for d in reversed(self.dims):
+            strides.insert(0, s)
+            s *= d
+        self.strides = tuple(strides)
+        self.all = list(itertools.product(*[range(d) for d in self.dims]))
+        self.ident = {d: i for i, d in enumerate(self.all)}
+
+    def locate(self):
+        me = lax.axis_index(CTX)
+        self.me = me
+        self.at = [lax.rem(me // s, d) for s, d in zip(self.strides, self.dims)]
+
+    def index(self, delta):
+        out = 0
+        for c, d, n, s in zip(self.at, delta, self.dims, self.strides):
+            out = out + (lax.rem(c + d, n) if d else c) * s
+        return out
+
+    def peer(self, axis, j):
+        return self.index(tuple(j if a == axis else 0 for a in range(len(self.dims))))
+
+    def orders(self):
+        rest = list(range(1, len(self.dims)))
+        return [[0] + rest, [0] + rest[::-1]]
+
+
+def entry_barrier(g, fsdp):
+    sem = pltpu.get_barrier_semaphore()
+    count = 0
+    f = lax.axis_index(FSDP)
+    for a, d in enumerate(g.dims):
+        for j in range(1, d):
+            pl.semaphore_signal(sem, inc=1, device_id=(g.peer(a, j), f), device_id_type=MESH)
+            count += 1
+    if fsdp:
+        pl.semaphore_signal(sem, inc=1, device_id=(g.me, 1 - f), device_id_type=MESH)
+        count += 1
+    pl.semaphore_wait(sem, count)
+
+
+class Gather:
+    def __init__(self, g, order, own, slot, send, recv):
+        self.g, self.order, self.own, self.slot, self.send, self.recv = g, order, own, slot, send, recv
+        self.copies = {}
+
+    def _copy(self, delta, axis, j, src):
+        g = self.g
+        label = tuple((g.dims[a] - j) % g.dims[a] if a == axis else delta[a] for a in range(len(g.dims)))
+        i = g.ident[label]
+        c = pltpu.make_async_remote_copy(
+            src_ref=src, dst_ref=self.slot(g.index(delta)), send_sem=self.send.at[i], recv_sem=self.recv.at[i],
+            device_id=(g.peer(axis, j), lax.axis_index(FSDP)), device_id_type=MESH)
+        self.copies[label] = c
+        return c
+
+    def forward(self, delta, stage, src):
+        for k in range(stage, len(self.order)):
+            a = self.order[k]
+            for j in range(1, self.g.dims[a]):
+                self._copy(delta, a, j, src).start()
+
+    def begin(self):
+        self.forward((0,) * len(self.g.dims), 0, self.own)
+
+    def labels(self, stage):
+        g, order = self.g, self.order
+        done = set(order[:stage])
+        out = []
+        for d in g.all:
+            if d[order[stage]] and all(d[a] == 0 for a in order[stage + 1:]):
+                out.append(d)
+        return out
+
+    def arrive(self, label, stage):
+        i = self.g.ident[label]
+        here = self.slot(self.g.index(label))
+        self.copies[label].wait_recv()
+        self.forward(label, stage + 1, here)
+
+    def end(self):
+        for c in self.copies.values():
+            c.wait_send()
+
+
+def gather_kernel(g, x_ref, o_ref, send, recv, local):
+    g.locate()
+    entry_barrier(g, False)
+    parts = x_ref.shape[0]
+    ords = g.orders()
+    gs = []
+    for p in range(parts):
+        gs.append(Gather(g, ords[p % len(ords)], x_ref.at[p], (lambda p: lambda i: o_ref.at[p, i])(p), send.at[p], recv.at[p]))
+    for q in gs:
+        q.begin()
+    mine = [pltpu.make_async_copy(x_ref.at[p], o_ref.at[p, g.me], local.at[p]) for p in range(parts)]
+    for m in mine:
+        m.start()
+    for stage in range(len(g.dims)):
+        lists = [q.labels(stage) for q in gs]
+        for i in range(max(map(len, lists))):
+            for q, l in zip(gs, lists):
+                if i < len(l):
+                    q.arrive(l[i], stage)
+    for m in mine:
+        m.wait()
+    for q in gs:
+        q.end()
+
+
+def all_gather_ctx(x, n, cid):
+    g = Grid(n)
+    parts, rows, cols = x.shape
+    return pl.pallas_call(
+        functools.partial(gather_kernel, g),
+        out_shape=jax.ShapeDtypeStruct((parts, n, rows, cols), x.dtype),
+        in_specs=[pl.BlockSpec(memory_space=pltpu.VMEM)],
+        out_specs=pl.BlockSpec(memory_space=pltpu.VMEM),
+        scratch_shapes=[pltpu.SemaphoreType.DMA((parts, n)), pltpu.SemaphoreType.DMA((parts, n)), pltpu.SemaphoreType.DMA((parts,))],
+        compiler_params=pltpu.CompilerParams(collective_id=cid, has_side_effects=True, vmem_limit_bytes=60 << 20),
+        name="ctx_gather",
+    )(x)
+
+
+def add_into(out, refs):
+    rows = out.shape[0]
+    step = max(s for s in range(16, 129, 16) if rows % s == 0)
+
+    def some(i, carry):
+        at = pl.ds(pl.multiple_of(i * step, step), step)
+        out[at] = sum(r[at].astype(jnp.float32) for r in refs).astype(out.dtype)
+        return carry
+
+    lax.fori_loop(0, rows // step, some, 0)
+
+
+class Reduce:
+    def __init__(self, g, order, src, acc, land, send, recv):
+        self.g, self.order, self.src, self.acc, self.land, self.send, self.recv = g, order, src, acc, land, send, recv
+        self.copies = {}
+        self.fresh = set(g.all)
+
+    def held(self, delta):
+        return self.src(self.g.index(delta)) if delta in self.fresh else self.acc(self.g.ident[delta])
+
+    def live(self, stage):
+        gone = set(self.order[:stage])
+        return [d for d in self.g.all if all(d[a] == 0 for a in gone)]
+
+    def send_block(self, d, stage):
+        g, a = self.g, self.order[stage]
+        i = g.ident[d]
+        c = pltpu.make_async_remote_copy(
+            src_ref=self.held(d), dst_ref=self.land(i), send_sem=self.send.at[i], recv_sem=self.recv.at[i],
+            device_id=(g.peer(a, d[a]), lax.axis_index(FSDP)), device_id_type=MESH)
+        self.copies[d] = c
+        c.start()
+
+    def weight(self, d, stage):
+        return sum(1 for a in self.order[stage:] if d[a])
+
+    def add(self, d, stage, out=None):
+        g, a = self.g, self.order[stage]
+        refs = [self.held(d)]
+        for j in range(1, g.dims[a]):
+            label = tuple(j if b == a else d[b] for b in range(len(d)))
+            self.copies[label].wait_recv()
+            refs.append(self.land(g.ident[label]))
+        add_into(self.acc(g.ident[d]) if out is None else out, refs)
+        if out is None:
+            self.fresh.discard(d)
+
+    def end(self):
+        for c in self.copies.values():
+            c.wait_send()
+
+
+def run_reduces(g, rs, outs):
+    last = len(g.dims) - 1
+    for r in rs:
+        first = [d for d in g.all if d[r.order[0]]]
+        first.sort(key=lambda d: -r.weight(d, 0))
+        r.pending = first
+    for i in range(max(len(r.pending) for r in rs)):
+        for r in rs:
+            if i < len(r.pending):
+                r.send_block(r.pending[i], 0)
+    for stage in range(len(g.dims)):
+        lists = []
+        for r in rs:
+            l = [d for d in r.live(stage + 1)]
+            l.sort(key=lambda d: -r.weight(d, stage + 1))
+            lists.append(l)
+        for i in range(max(map(len, lists))):
+            for r, l, o in zip(rs, lists, outs):
+                if i < len(l):
+                    if stage == last:
+                        r.add(l[i], stage, o)
+                    else:
+                        r.add(l[i], stage)
+                        if l[i][r.order[stage + 1]]:
+                            r.send_block(l[i], stage + 1)
+
+
+def scatter_kernel(g, x_ref, o_ref, acc, land, send, recv):
+    g.locate()
+    entry_barrier(g, False)
+    parts = x_ref.shape[0]
+    ords = [o[::-1] for o in g.orders()]
+    rs = []
+    for p in range(parts):
+        rs.append(Reduce(g, ords[p % 2], (lambda p: lambda i: x_ref.at[p, i])(p), (lambda p: lambda i: acc.at[p, i])(p),
+                         (lambda p: lambda i: land.at[p, i])(p), send.at[p], recv.at[p]))
+    run_reduces(g, rs, [o_ref.at[p] for p in range(parts)])
+    for r in rs:
+        r.end()
+
+
+def reduce_scatter_ctx(x, n, cid):
+    g = Grid(n)
+    parts, _, rows, cols = x.shape
+    return pl.pallas_call(
+        functools.partial(scatter_kernel, g),
+        out_shape=jax.ShapeDtypeStruct((parts, rows, cols), jnp.float32),
+        in_specs=[pl.BlockSpec(memory_space=pltpu.VMEM)],
+        out_specs=pl.BlockSpec(memory_space=pltpu.VMEM),
+        scratch_shapes=[pltpu.VMEM((parts, n, rows, cols), x.dtype), pltpu.VMEM((parts, n, rows, cols), x.dtype),
+                        pltpu.SemaphoreType.DMA((parts, n)), pltpu.SemaphoreType.DMA((parts, n))],
+        compiler_params=pltpu.CompilerParams(collective_id=cid, has_side_effects=True, vmem_limit_bytes=60 << 20),
+        name="ctx_reduce",
+    )(x)
+
+
+def reduce_all_kernel(g, x_ref, o_ref, acc, land, pair, fsum, send, recv, gsend, grecv, psend, precv):
+    g.locate()
+    entry_barrier(g, True)
+    f = lax.axis_index(FSDP)
+    parts = x_ref.shape[1]
+    n = g.n
+    gords = g.orders()
+    ords = [o[::-1] for o in gords]
+    pairs = {}
+    rs, gs = [], []
+    for p in range(parts):
+        rs.append(Reduce(g, ords[p % 2], (lambda p: lambda i: fsum.at[p, i])(p), (lambda p: lambda i: acc.at[p, i])(p),
+                         (lambda p: lambda i: land.at[p, i])(p), send.at[p], recv.at[p]))
+        gs.append(Gather(g, gords[p % 2], o_ref.at[p, g.me], (lambda p: lambda i: o_ref.at[p, i])(p), gsend.at[p], grecv.at[p]))
+    seq = []
+    for r in rs:
+        l = sorted(g.all, key=lambda d: -r.weight(d, 0) - (10 if d[r.order[0]] else 0))
+        seq.append(l)
+    for i in range(n):
+        for p in range(parts):
+            d = seq[p][i]
+            k = g.index(d)
+            c = pltpu.make_async_remote_copy(
+                src_ref=x_ref.at[1 - f, p, k], dst_ref=pair.at[p, k], send_sem=psend.at[p, g.ident[d]], recv_sem=precv.at[p, g.ident[d]],
+                device_id=(g.me, 1 - f), device_id_type=MESH)
+            c.start()
+            pairs[p, d] = c
+    for i in range(n):
+        for p in range(parts):
+            d = seq[p][i]
+            k = g.index(d)
+            pairs[p, d].wait_recv()
+            add_into(fsum.at[p, k], [x_ref.at[f, p, k], pair.at[p, k]])
+            if d[rs[p].order[0]]:
+                rs[p].send_block(d, 0)
+    last = len(g.dims) - 1
+    for stage in range(len(g.dims)):
+        lists = []
+        for r in rs:
+            l = [d for d in r.live(stage + 1)]
+            l.sort(key=lambda d: -r.weight(d, stage + 1))
+            lists.append(l)
+        for i in range(max(map(len, lists))):
+            for p, (r, l) in enumerate(zip(rs, lists)):
+                if i < len(l):
+                    if stage == last:
+                        r.add(l[i], stage, o_ref.at[p, g.me])
+                        gs[p].begin()
+                    else:
+                        r.add(l[i], stage)
+                        if l[i][r.order[stage + 1]]:
+                            r.send_block(l[i], stage + 1)
+    for stage in range(len(g.dims)):
+        lists = [q.labels(stage) for q in gs]
+        for i in range(max(map(len, lists))):
+            for q, l in zip(gs, lists):
+                if i < len(l):
+                    q.arrive(l[i], stage)
+    for c in pairs.values():
+        c.wait_send()
+    for r in rs:
+        r.end()
+    for q in gs:
+        q.end()
+
+
+def reduce_all(x, n, cid):
+    g = Grid(n)
+    _, parts, _, rows, cols = x.shape
+    blk = (parts, n, rows, cols)
+    return pl.pallas_call(
+        functools.partial(reduce_all_kernel, g),
+        out_shape=jax.ShapeDtypeStruct(blk, x.dtype),
+        in_specs=[pl.BlockSpec(memory_space=pltpu.VMEM)],
+        out_specs=pl.BlockSpec(memory_space=pltpu.VMEM),
+        scratch_shapes=[pltpu.VMEM(blk, x.dtype)] * 4 + [pltpu.SemaphoreType.DMA((parts, n))] * 6,
+        compiler_params=pltpu.CompilerParams(collective_id=cid, has_side_effects=True, vmem_limit_bytes=64 << 20),
+        name="grad_reduce",
+    )(x)
+
+
 from jax.sharding import PartitionSpec as P
 
 HEADS = 9
@@ -94,7 +433,7 @@
     return (grad_queries, grad_keys, grad_values)
 
 
-def layer_forward(inputs, positions, places, weights):
+def layer_forward(inputs, positions, places, weights, layer_index):
     gain_attn, w_query, w_key, w_value, w_out, gain_ffn, w_gate, w_up, w_down = weights
     seq_count, row_count, model_width = inputs.shape
     normed = normalize(inputs, gain_attn).astype(jnp.bfloat16)
@@ -110,10 +449,10 @@
     )
     keys_own = keys_own.reshape(seq_count, row_count, KV_HEADS * HEAD)
     values_own = value_pre.astype(jnp.bfloat16)
-    keys_all, values_all = (
-        lax.all_gather(keys_own, "ctx", axis=1, tiled=True),
-        lax.all_gather(values_own, "ctx", axis=1, tiled=True),
-    )
+    devices = lax.axis_size("ctx")
+    both = all_gather_ctx(jnp.concatenate([keys_own, values_own], axis=-1), devices, 2 + layer_index)
+    both = both.reshape(seq_count, devices * row_count, 2 * KV_HEADS * HEAD)
+    keys_all, values_all = both[..., : KV_HEADS * HEAD], both[..., KV_HEADS * HEAD :]
     length = keys_all.shape[1]
     mixed, log_total = lax.map(
         attend,
@@ -153,7 +492,7 @@
     return (result, record)
 
 
-def layer_backward(gradient, record, weights, positions, places):
+def layer_backward(gradient, record, weights, positions, places, layer_index):
     gain_attn, w_query, w_key, w_value, w_out, gain_ffn, w_gate, w_up, w_down = weights
     (
         inputs,
@@ -195,10 +534,7 @@
         "sre,de->srd", branch_low, w_out, preferred_element_type=jnp.float32
     ).astype(jnp.bfloat16)
     grad_mixed = grad_mixed.reshape(seq_count, row_count, KV_HEADS, HEADS // KV_HEADS, HEAD)
-    keys_all, values_all = (
-        lax.all_gather(keys_own, "ctx", axis=1, tiled=True),
-        lax.all_gather(values_own, "ctx", axis=1, tiled=True),
-    )
+    keys_all, values_all = kept_keys, kept_values
     length = keys_all.shape[1]
     grad_queries, grad_keys_all, grad_values_all = lax.map(
         attend_back,
@@ -212,20 +548,16 @@
             grad_mixed,
         ),
     )
-    grad_keys, grad_values = (
-        lax.psum_scatter(
+    devices = lax.axis_size("ctx")
+    both = jnp.concatenate(
+        [
             grad_keys_all.reshape(seq_count, length, KV_HEADS * HEAD),
-            "ctx",
-            scatter_dimension=1,
-            tiled=True,
-        ),
-        lax.psum_scatter(
             grad_values_all.reshape(seq_count, length, KV_HEADS * HEAD),
-            "ctx",
-            scatter_dimension=1,
-            tiled=True,
-        ),
-    )
+        ],
+        axis=-1,
+    ).astype(jnp.bfloat16)
+    both = reduce_scatter_ctx(both.reshape(seq_count, devices, row_count, -1), devices, 4 + layer_index)
+    grad_keys, grad_values = both[..., : KV_HEADS * HEAD], both[..., KV_HEADS * HEAD :]
     grad_query_pre = (
         rotate(grad_queries.reshape(seq_count, row_count, HEADS, HEAD), positions, -1.0)
         .reshape(seq_count, row_count, model_width)
@@ -266,6 +598,51 @@
         grad_wdown,
     )
     return (grad_middle + grad_input_norm, layer_grads)
+
+
+def pair_kernel(*refs):
+    count = len(refs) // 2 - 1
+    srcs, dsts, send, recv = refs[:count], refs[count : 2 * count], refs[-2], refs[-1]
+    c, f = lax.axis_index(CTX), lax.axis_index(FSDP)
+    sem = pltpu.get_barrier_semaphore()
+    pl.semaphore_signal(sem, inc=1, device_id=(c, 1 - f), device_id_type=MESH)
+    pl.semaphore_wait(sem, 1)
+    copies = [
+        pltpu.make_async_remote_copy(
+            src_ref=s, dst_ref=d, send_sem=send.at[i], recv_sem=recv.at[i], device_id=(c, 1 - f), device_id_type=MESH
+        )
+        for i, (s, d) in enumerate(zip(srcs, dsts))
+    ]
+    for x in copies:
+        x.start()
+    for x in copies:
+        x.wait()
+
+
+def pair_exchange(arrays, cid):
+    any_space = pl.BlockSpec(memory_space=pl.ANY)
+    return pl.pallas_call(
+        pair_kernel,
+        out_shape=[jax.ShapeDtypeStruct(a.shape, a.dtype) for a in arrays],
+        in_specs=[any_space] * len(arrays),
+        out_specs=[any_space] * len(arrays),
+        scratch_shapes=[pltpu.SemaphoreType.DMA((len(arrays),))] * 2,
+        compiler_params=pltpu.CompilerParams(collective_id=cid, has_side_effects=True),
+        name="pair_exchange",
+    )(*arrays)
+
+
+def tiled(grad):
+    rows, cols = grad.shape[0] // 2, grad.shape[1]
+    wide = -(-cols // 128) * 128
+    grad = jnp.pad(grad.astype(jnp.bfloat16), ((0, 0), (0, wide - cols)))
+    grad = grad.reshape(2, rows, wide // 128, 128).transpose(0, 2, 1, 3)
+    return grad.reshape(2, -1, 16, 128)
+
+
+def untiled(tiles, rows, cols):
+    wide = -(-cols // 128)
+    return tiles.reshape(wide, rows, 128).transpose(1, 0, 2).reshape(rows, wide * 128)[:, :cols].astype(jnp.float32)
 
 
 def body(
@@ -283,103 +660,54 @@
     cotangent,
 ):
     layer_count = norm_attn.shape[0]
+    devices = lax.axis_size("ctx")
     places = lax.all_gather(positions, "ctx", axis=1, tiled=True)
+    own = (norm_attn, w_query, w_key, w_value, w_out, norm_ffn, w_gate, w_up, w_down)
+    other = pair_exchange(own, 0)
+    first = lax.axis_index("fsdp") == 0
+    full = [
+        jnp.where(first, jnp.concatenate([o, t], axis=1), jnp.concatenate([t, o], axis=1)) for o, t in zip(own, other)
+    ]
     current = tokens.astype(jnp.float32)
     records = []
-    gathered_weights = []
     for layer_index in range(layer_count):
-        weights = (
-            lax.all_gather(norm_attn[layer_index], "fsdp", axis=0, tiled=True),
-            lax.all_gather(w_query[layer_index], "fsdp", axis=0, tiled=True),
-            lax.all_gather(w_key[layer_index], "fsdp", axis=0, tiled=True),
-            lax.all_gather(w_value[layer_index], "fsdp", axis=0, tiled=True),
-            lax.all_gather(w_out[layer_index], "fsdp", axis=0, tiled=True),
-            lax.all_gather(norm_ffn[layer_index], "fsdp", axis=0, tiled=True),
-            lax.all_gather(w_gate[layer_index], "fsdp", axis=0, tiled=True),
-            lax.all_gather(w_up[layer_index], "fsdp", axis=0, tiled=True),
-            lax.all_gather(w_down[layer_index], "fsdp", axis=0, tiled=True),
-        )
-        current, record = layer_forward(current, positions, places, weights)
+        weights = tuple(w[layer_index] for w in full)
+        current, record = layer_forward(current, positions, places, weights, layer_index)
         records.append(record)
-        gathered_weights.append(weights)
     output = current.astype(jnp.bfloat16)
     gradient = cotangent.astype(jnp.float32)
     collected = []
     for layer_index in reversed(range(layer_count)):
-        weights = (
-            lax.all_gather(norm_attn[layer_index], "fsdp", axis=0, tiled=True),
-            lax.all_gather(w_query[layer_index], "fsdp", axis=0, tiled=True),
-            lax.all_gather(w_key[layer_index], "fsdp", axis=0, tiled=True),
-            lax.all_gather(w_value[layer_index], "fsdp", axis=0, tiled=True),
-            lax.all_gather(w_out[layer_index], "fsdp", axis=0, tiled=True),
-            lax.all_gather(norm_ffn[layer_index], "fsdp", axis=0, tiled=True),
-            lax.all_gather(w_gate[layer_index], "fsdp", axis=0, tiled=True),
-            lax.all_gather(w_up[layer_index], "fsdp", axis=0, tiled=True),
-            lax.all_gather(w_down[layer_index], "fsdp", axis=0, tiled=True),
+        weights = tuple(w[layer_index] for w in full)
+        gradient, layer_grads = layer_backward(
+            gradient, records[layer_index], weights, positions, places, layer_index
         )
-        gradient, layer_grads = layer_backward(
-            gradient, records[layer_index], weights, positions, places
-        )
-        shares = (
-            lax.psum_scatter(
-                layer_grads[0].astype(jnp.bfloat16), "fsdp", scatter_dimension=0, tiled=True
-            ).astype(jnp.float32),
-            lax.psum_scatter(
-                layer_grads[1].astype(jnp.bfloat16), "fsdp", scatter_dimension=0, tiled=True
-            ).astype(jnp.float32),
-            lax.psum_scatter(
-                layer_grads[2].astype(jnp.bfloat16), "fsdp", scatter_dimension=0, tiled=True
-            ).astype(jnp.float32),
-            lax.psum_scatter(
-                layer_grads[3].astype(jnp.bfloat16), "fsdp", scatter_dimension=0, tiled=True
-            ).astype(jnp.float32),
-            lax.psum_scatter(
-                layer_grads[4].astype(jnp.bfloat16), "fsdp", scatter_dimension=0, tiled=True
-            ).astype(jnp.float32),
-            lax.psum_scatter(
-                layer_grads[5].astype(jnp.bfloat16), "fsdp", scatter_dimension=0, tiled=True
-            ).astype(jnp.float32),
-            lax.psum_scatter(
-                layer_grads[6].astype(jnp.bfloat16), "fsdp", scatter_dimension=0, tiled=True
-            ).astype(jnp.float32),
-            lax.psum_scatter(
-                layer_grads[7].astype(jnp.bfloat16), "fsdp", scatter_dimension=0, tiled=True
-            ).astype(jnp.float32),
-            lax.psum_scatter(
-                layer_grads[8].astype(jnp.bfloat16), "fsdp", scatter_dimension=0, tiled=True
-            ).astype(jnp.float32),
-        )
-        totals = lax.psum(
-            (
-                shares[0],
-                shares[1],
-                shares[2],
-                shares[3],
-                shares[4],
-                shares[5],
-                shares[6],
-                shares[7],
-                shares[8],
-            ),
-            "ctx",
-        )
-        collected.insert(0, totals)
-    stacked = tuple(
-        (jnp.stack([entry_totals[member] for entry_totals in collected]) for member in range(9))
-    )
-    return (
-        output,
-        gradient,
-        stacked[0],
-        stacked[1],
-        stacked[2],
-        stacked[3],
-        stacked[4],
-        stacked[5],
-        stacked[6],
-        stacked[7],
-        stacked[8],
-    )
+        collected.insert(0, layer_grads)
+    pieces, sizes = [], []
+    for layer_grads in collected:
+        for grad in layer_grads:
+            if grad.ndim == 1:
+                half = jnp.pad(grad.astype(jnp.bfloat16).reshape(2, -1), ((0, 0), (0, 2048 - grad.shape[0] // 2)))
+                piece = half.reshape(2, 1, 16, 128)
+            else:
+                piece = tiled(grad)
+            pieces.append(piece)
+            sizes.append(piece.shape[1])
+    count = sum(sizes)
+    block = -(-count // (2 * devices))
+    pieces.append(jnp.zeros((2, 2 * devices * block - count, 16, 128), jnp.bfloat16))
+    blob = jnp.concatenate(pieces, axis=1).reshape(2, 2, devices, block * 16, 128)
+    total = reduce_all(blob, devices, 1).reshape(-1, 16, 128)
+    results, start = [], 0
+    for size, weight in zip(sizes, own * layer_count):
+        part = total[start : start + size]
+        start += size
+        if weight.ndim == 2:
+            results.append(part.reshape(-1)[: weight.shape[1]].astype(jnp.float32))
+        else:
+            results.append(untiled(part, weight.shape[1], weight.shape[2]))
+    stacked = [jnp.stack(results[k :: len(own)]) for k in range(len(own))]
+    return (output, gradient, *stacked)
 
 
 def solution(mesh):

time: 1780 us -> 796 us (0.45)
  waiting for transfers between devices: 1350 us -> 0 us
  Pallas kernels: 0 us -> 348 us
  local copies, waits for them, and re-layouts: 34.3 us -> 176 us
  blocking collectives: 88 us -> 28.4 us
  matrix products: 171 us -> 133 us
    reduce_scatter x18 -> x0, waiting for transfers between devices: 577 us -> none  [the longest x2 271 us: layer_backward(): lax.psum_scatter(grad_values_all.reshape(seq_count, length, KV_HEADS * HE...]
    psum x1 -> x0, waiting for transfers between devices: 574 us -> none  [body(): lax.psum((shares[0], shares[1], shares[2], shares[3], shares[4], shares[5...]
    pallas_call x0 -> x6, Pallas kernels: none -> 348 us  [the longest x1 192 us: reduce_all(): pl.pallas_call(functools.partial(reduce_all_kernel, g), out_shape=jax.Sha...]
    all_gather x10 -> x0, waiting for transfers between devices: 191 us -> none  [the longest x2 116 us: layer_forward(): lax.all_gather(keys_own, 'ctx', axis=1, tiled=True)]
    unnamed x233 -> x244, local copies, waits for them, and re-layouts: 9.89 us -> 54 us
    another operation x28 -> x13, other arithmetic: 45.8 us -> 11 us  [the longest x9 10.8 us: body(): stacked = [jnp.stack(results[k::len(own)]) for k in range(len(own))]]
    psum x1 -> x0, blocking collectives: 33.4 us -> none  [body(): lax.psum((shares[0], shares[1], shares[2], shares[3], shares[4], shares[5...]
    slice x9 -> x18, local copies, waits for them, and re-layouts: 9.58 us -> 36.4 us  [the longest x4 16.3 us: layer_forward(): both[..., :KV_HEADS * HEAD]]
  transfers between devices with their start and end apart: 29 -> 0, of which waited for: 18 -> 0; matrix products, arithmetic and copies ran while one was open for 12% -> 0% of each run, Pallas kernels for 0% -> 0%
where the time goes in v1:
time: 796 us; the launch traced here: 790 us
  Pallas kernels  348 us (44%)
  local copies, waits for them, and re-layouts  176 us (22%)
  matrix products  133 us (17%)
  other arithmetic  99.4 us (12%)
  blocking collectives  28.4 us (4%)
    pallas_call x1, Pallas kernels, reduce_all(): pl.pallas_call(functools.partial(reduce_all_kernel, g), out_shape=jax.Sha...  192 us
    pallas_call x2, Pallas kernels, all_gather_ctx(): pl.pallas_call(functools.partial(gather_kernel, g), out_shape=jax.ShapeDt...  81.6 us
    pallas_call x2, Pallas kernels, reduce_scatter_ctx(): pl.pallas_call(functools.partial(scatter_kernel, g), out_shape=jax.ShapeD...  61.7 us
    unnamed x244, local copies, waits for them, and re-layouts  54 us
    convert_element_type x4, other arithmetic, attend_back(): grad_scores = (probabilities * (grad_probs - jnp.sum(probabilities * grad...  44.1 us
    all_gather x1, blocking collectives, body(): places = lax.all_gather(positions, 'ctx', axis=1, tiled=True)  28.4 us
    dot_general x4, matrix products, attend_back(): jnp.einsum('qhge,khe->hgqk', grad_mixed, values_all, preferred_element_ty...  23.5 us
    dot_general x4, matrix products, attend_back(): jnp.einsum('hgqk,qhge->khe', grad_scores, queries, preferred_element_type...  20 us

profile of v1, /device:TPU:10, one launch (start us, length us, event | category | flops | bytes accessed | tf_op | source)
XLA Modules:
  0.0 790.0 jit_solution(15462647856765319087)
XLA Ops:
  6.1 12.5 %pair_exchange.1 = (bf16[2,288]{1,0:T(2,128)(2,1)}, bf16[2,288,576]{2,1,0:T(8,128)(2,1)}, bf16[2,288,192]{2,1,0:T(8,128)(2,1)}, bf16[2,288,192]{2,1,0:T(8,128)(2...) custom-call(bf16[2,288]{1,0:T(2,128)(2,1)} %refs_0_.1, ...), custom_call_target="tpu_custom_call" | custom-call | tf_op jit(solution)/shard_map/pair_exchange/pallas_call | solution.py:624
  25.5 45.3 %ctx_gather.2 = bf16[2,16,128,384]{3,2,1,0:T(8,128)(2,1)} custom-call(bf16[2,128,384]{2,1,0:T(8,128)(2,1)} %pad_maximum_fusion.4.x_ref), custom_call_target="tpu_custom_call" | custom-call | tf_op jit(solution)/shard_map/ctx_gather/pallas_call | solution.py:142
  70.8 5.3 fusion.190
  78.9 28.4 %all_gather.3 = s32[2,2048]{1,0:T(2,128)S(1)} all-gather(s32[2,128]{1,0:T(2,128)S(1)} %copy-done.115), channel_id=1, replica_groups=mesh['ctx'=16,'fsdp'=2] {'ctx'}, dimensions={1}, use_global_device_ids=true | all-gather | bytes 17408 | tf_op jit(solution)/shard_map/all_gather | solution.py:664
  120.8 14.5 %while.52 = (s32[]{:T(128)}, bf16[2,128,3,3,64]{1,4,3,2,0:T(8,128)(2,1)}, f32[2,3,3,128,1]{3,2,1,4,0:T(4,128)S(1)}, bf16[2,2048,3,64]{1,3,2,0:T(8,128)(2,1)S(1)}...) while((s32[]{:T(128)}, ...), condition=%wide.region_4.5_spmd, body=%wide.region_1.4_spmd.sunk | while | flops 632552320 | bytes 33807528 | solution.py:457
  139.2 5.6 maximum_select_fusion.1
  157.7 36.3 %ctx_gather.3 = bf16[2,16,128,384]{3,2,1,0:T(8,128)(2,1)} custom-call(bf16[2,128,384]{2,1,0:T(8,128)(2,1)} %pad_maximum_fusion.5.x_ref), custom_call_target="tpu_custom_call" | custom-call | tf_op jit(solution)/shard_map/ctx_gather/pallas_call | solution.py:142
  194.0 5.3 fusion.189
  210.1 13.4 %while.53 = (s32[]{:T(128)}, bf16[2,128,3,3,64]{1,4,3,2,0:T(8,128)(2,1)S(1)}, f32[2,3,3,128,1]{3,2,1,4,0:T(4,128)S(1)}, bf16[2,2048,3,64]{1,3,2,0:T(8,128)(2,1)}...) while((s32[]{:T(128)}, ...), condition=%wide.region_10.11_spmd, body=%wide.region_7.10_spmd.sunk | while | flops 632552320 | bytes 37739660 | solution.py:457
  241.4 63.2 %while.54 = (s32[]{:T(128)}, f32[2,128,3,3,64]{1,4,3,2,0:T(8,128)}, bf16[2,2048,3,64]{1,3,2,0:T(8,128)(2,1)}, bf16[2,2048,3,64]{1,3,2,0:T(8,128)(2,1)}, bf16[2,2...) while((s32[]{:T(128)}, f32[2,128,3,3,64]{1,4,3,2,0:T(8,128)}, ...), condition=%wide.region_15.16_spmd, body=%wide.region_13.15_spmd.sunk | while | flops 1546066816 | bytes 175015248 | solution.py:539
  243.3 5.9 fusion.298
  249.2 11.0 %fusion.299 = bf16[3,3,128,2048]{2,3,1,0:T(8,128)(2,1)} fusion(f32[3,2048,128,3]{2,1,3,0:T(8,128)} %get-tuple-element.685, f32[3,2048,128,3]{2,1,3,0:T(8,128)} %copy-done, f32[3,3,128]{2,1,0:T(4,128)S(1)} %get-tuple-element.686, f32[3,3,128]{2,1,0:T(4,128)S(1)} %dynamic-slice_bitcast_fusion.4, pred[128,2048]{0,1:T(8,128)(4,1)S(1)} %broadcast_compare_fusion.10), kind=kLoop, calls=%fused_computation.52.clone.1 | loop fusion | flops 14155776 | bytes 23864320 | tf_op jit(solution)/shard_map/while/body/eval_jaxpr/convert_element_type | solution.py:418
  274.9 5.9 fusion.298
  280.8 11.0 %fusion.299 = bf16[3,3,128,2048]{2,3,1,0:T(8,128)(2,1)} fusion(f32[3,2048,128,3]{2,1,3,0:T(8,128)} %get-tuple-element.685, f32[3,2048,128,3]{2,1,3,0:T(8,128)} %copy-done, f32[3,3,128]{2,1,0:T(4,128)S(1)} %get-tuple-element.686, f32[3,3,128]{2,1,0:T(4,128)S(1)} %dynamic-slice_bitcast_fusion.4, pred[128,2048]{0,1:T(8,128)(4,1)S(1)} %broadcast_compare_fusion.10), kind=kLoop, calls=%fused_computation.52.clone.1 | loop fusion | flops 14155776 | bytes 23864320 | tf_op jit(solution)/shard_map/while/body/eval_jaxpr/convert_element_type | solution.py:418
  322.1 31.7 %ctx_reduce.2 = f32[2,128,384]{2,1,0:T(8,128)} custom-call(bf16[2,16,128,384]{3,2,1,0:T(8,128)(2,1)} %pad_maximum_fusion.x_ref), custom_call_target="tpu_custom_call" | custom-call | tf_op jit(solution)/shard_map/ctx_reduce/pallas_call | solution.py:250
  372.5 63.5 %while.55 = (s32[]{:T(128)}, f32[2,128,3,3,64]{1,4,3,2,0:T(8,128)}, bf16[2,2048,3,64]{1,3,2,0:T(8,128)(2,1)}, bf16[2,2048,3,64]{1,3,2,0:T(8,128)(2,1)}, bf16[2,2...) while((s32[]{:T(128)}, f32[2,128,3,3,64]{1,4,3,2,0:T(8,128)}, ...), condition=%wide.region_20.21_spmd, body=%wide.region_18.20_spmd.sunk | while | flops 1546066816 | bytes 172655920 | solution.py:539
  374.8 5.9 fusion.313
  380.8 11.0 %fusion.314 = bf16[3,3,128,2048]{2,3,1,0:T(8,128)(2,1)} fusion(f32[3,2048,128,3]{2,1,3,0:T(8,128)} %get-tuple-element.698, f32[3,2048,128,3]{2,1,3,0:T(8,128)} %copy-done.2, f32[3,3,128]{2,1,0:T(4,128)S(1)} %get-tuple-element.699, f32[3,3,128]{2,1,0:T(4,128)S(1)} %dynamic-slice_bitcast_fusion.5, pred[128,2048]{0,1:T(8,128)(4,1)S(1)} %broadcast_compare_fusion.11), kind=kLoop, calls=%fused_computation.100.clone.1 | loop fusion | flops 14155776 | bytes 23864320 | tf_op jit(solution)/shard_map/while/body/eval_jaxpr/convert_element_type | solution.py:418
  406.4 5.9 fusion.313
  412.3 11.0 %fusion.314 = bf16[3,3,128,2048]{2,3,1,0:T(8,128)(2,1)} fusion(f32[3,2048,128,3]{2,1,3,0:T(8,128)} %get-tuple-element.698, f32[3,2048,128,3]{2,1,3,0:T(8,128)} %copy-done.2, f32[3,3,128]{2,1,0:T(4,128)S(1)} %get-tuple-element.699, f32[3,3,128]{2,1,0:T(4,128)S(1)} %dynamic-slice_bitcast_fusion.5, pred[128,2048]{0,1:T(8,128)(4,1)S(1)} %broadcast_compare_fusion.11), kind=kLoop, calls=%fused_computation.100.clone.1 | loop fusion | flops 14155776 | bytes 23864320 | tf_op jit(solution)/shard_map/while/body/eval_jaxpr/convert_element_type | solution.py:418
  453.5 30.0 %ctx_reduce.3 = f32[2,128,384]{2,1,0:T(8,128)} custom-call(bf16[2,16,128,384]{3,2,1,0:T(8,128)(2,1)} %pad_maximum_fusion.1.x_ref), custom_call_target="tpu_custom_call" | custom-call | tf_op jit(solution)/shard_map/ctx_reduce/pallas_call | solution.py:250
  518.6 5.8 copy.302
  554.7 5.7 copy.314
  562.7 192.3 %grad_reduce.1 = bf16[2,16,928,128]{3,2,1,0:T(8,128)(2,1)} custom-call(bf16[2,2,16,928,128]{4,3,2,1,0:T(8,128)(2,1)} %bitcast.837), custom_call_target="tpu_custom_call" | custom-call | tf_op jit(solution)/shard_map/grad_reduce/pallas_call | solution.py:332
  (573 shorter events, 313.7 us)
Async XLA Ops:
  6.0 12.6 %copy-start.70 = (bf16[2,288,192]{2,1,0:T(8,128)(2,1)S(1)}, bf16[2,288,192]{2,1,0:T(8,128)(2,1)}, u32[]{:S(2)}) copy-start(bf16[2,288,192]{2,1,0:T(8,128)(2,1)} %refs_2_.1) | copy-start | bytes 663556
  6.0 12.6 %copy-start.71 = (bf16[2,288,192]{2,1,0:T(8,128)(2,1)S(1)}, bf16[2,288,192]{2,1,0:T(8,128)(2,1)}, u32[]{:S(2)}) copy-start(bf16[2,288,192]{2,1,0:T(8,128)(2,1)} %refs_3_.1) | copy-start | bytes 663556
  6.0 14.2 %copy-start.110 = (bf16[2,288]{1,0:T(2,128)(2,1)S(1)}, bf16[2,288]{1,0:T(2,128)(2,1)}, u32[]{:S(2)}) copy-start(bf16[2,288]{1,0:T(2,128)(2,1)} %refs_0_.1) | copy-start | bytes 3460
  6.0 14.2 %copy-start.111 = (bf16[2,288]{1,0:T(2,128)(2,1)S(1)}, bf16[2,288]{1,0:T(2,128)(2,1)}, u32[]{:S(2)}) copy-start(bf16[2,288]{1,0:T(2,128)(2,1)} %refs_5_.1) | copy-start | bytes 3460
  6.0 15.1 %copy-start.21 = (bf16[2,128,576]{1,2,0:T(8,128)(2,1)S(1)}, bf16[2,128,576]{1,2,0:T(8,128)(2,1)}, u32[]{:S(2)}) copy-start(bf16[2,128,576]{1,2,0:T(8,128)(2,1)} %param.20) | copy-start | bytes 884740
  20.2 50.6 %copy-start.38 = (bf16[2,576,192]{2,1,0:T(8,128)(2,1)}, bf16[2,576,192]{2,1,0:T(8,128)(2,1)S(1)}, u32[]{:S(2)}) copy-start(bf16[2,576,192]{2,1,0:T(8,128)(2,1)S(1)} %get-tuple-element.448) | copy-start | bytes 1327108
  20.2 50.6 %copy-start.61 = (bf16[2,576,192]{2,1,0:T(8,128)(2,1)}, bf16[2,576,192]{2,1,0:T(8,128)(2,1)S(1)}, u32[]{:S(2)}) copy-start(bf16[2,576,192]{2,1,0:T(8,128)(2,1)S(1)} %get-tuple-element.449) | copy-start | bytes 1327108
  21.1 97.9 %copy-start.97 = (f32[576]{0:T(1024)}, f32[576]{0:T(1024)S(1)}, u32[]{:S(2)}) copy-start(f32[576]{0:T(1024)S(1)} %get-tuple-element.287) | copy-start | bytes 6916
  21.1 134.6 %copy-start.99 = (f32[576]{0:T(1024)}, f32[576]{0:T(1024)S(1)}, u32[]{:S(2)}) copy-start(f32[576]{0:T(1024)S(1)} %get-tuple-element.286) | copy-start | bytes 6916
  21.8 97.2 %copy-start.103 = (f32[2,128]{1,0:T(2,128)}, f32[2,128]{1,0:T(2,128)S(1)}, u32[]{:S(2)}) copy-start(f32[2,128]{1,0:T(2,128)S(1)} %get-tuple-element.425) | copy-start | bytes 3076
  24.5 185.4 %copy-start.59 = (f32[2,128,32]{1,2,0:T(8,128)}, f32[2,128,32]{1,2,0:T(8,128)S(1)}, u32[]{:S(2)}) copy-start(f32[2,128,32]{1,2,0:T(8,128)S(1)} %get-tuple-element.423) | copy-start | bytes 98308
  135.4 9.4 %copy-start.6 = (bf16[2,128,3,3,64]{1,4,3,2,0:T(8,128)(2,1)}, bf16[2,128,3,3,64]{1,4,3,2,0:T(8,128)(2,1)S(1)}, u32[]{:S(2)}) copy-start(bf16[2,128,3,3,64]{1,4,3,2,0:T(8,128)(2,1)S(1)} %get-tuple-element.828) | copy-start | bytes 884740
  135.4 9.4 %copy-start.8 = (bf16[2,2048,3,64]{1,3,2,0:T(8,128)(2,1)}, bf16[2,2048,3,64]{1,3,2,0:T(8,128)(2,1)S(1)}, u32[]{:S(2)}) copy-start(bf16[2,2048,3,64]{1,3,2,0:T(8,128)(2,1)S(1)} %get-tuple-element.830) | copy-start | bytes 4718596
  135.4 9.5 %copy-start.95 = (f32[2,3,3,128,1]{3,2,1,4,0:T(4,128)}, f32[2,3,3,128,1]{3,2,1,4,0:T(4,128)S(1)}, u32[]{:S(2)}) copy-start(f32[2,3,3,128,1]{3,2,1,4,0:T(4,128)S(1)} %get-tuple-element.798) | copy-start | bytes 27652
  138.3 14.1 %copy-start.65 = (f32[2,128,576]{1,2,0:T(8,128)}, f32[2,128,576]{1,2,0:T(8,128)S(1)}, u32[]{:S(2)}) copy-start(f32[2,128,576]{1,2,0:T(8,128)S(1)} %get-tuple-element.433) | copy-start | bytes 1769476
  155.7 38.3 %copy-start.105 = (f32[2,128]{1,0:T(2,128)}, f32[2,128]{1,0:T(2,128)S(1)}, u32[]{:S(2)}) copy-start(f32[2,128]{1,0:T(2,128)S(1)} %get-tuple-element.429) | copy-start | bytes 3076
  155.9 52.5 %copy-start.19 = (bf16[2,128,576]{1,2,0:T(8,128)(2,1)}, bf16[2,128,576]{1,2,0:T(8,128)(2,1)S(1)}, u32[]{:S(2)}) copy-start(bf16[2,128,576]{1,2,0:T(8,128)(2,1)S(1)} %multiply_convert_fusion.7) | copy-start | bytes 884740
  235.3 126.1 %copy-start.23 = (f32[2,128,576]{1,2,0:T(8,128)}, f32[2,128,576]{1,2,0:T(8,128)S(1)}, u32[]{:S(2)}) copy-start(f32[2,128,576]{1,2,0:T(8,128)S(1)} %subtract_add_fusion.2) | copy-start | bytes 1769476
  322.1 35.2 %copy-start.60 = (f32[2,128,32]{1,2,0:T(8,128)S(1)}, f32[2,128,32]{1,2,0:T(8,128)}, u32[]{:S(2)}) copy-start(f32[2,128,32]{1,2,0:T(8,128)} %copy-done.59) | copy-start | bytes 98308
  322.1 35.2 %copy-start.80 = (f32[2,128,32]{1,2,0:T(8,128)S(1)}, f32[2,128,32]{1,2,0:T(8,128)}, u32[]{:S(2)}) copy-start(f32[2,128,32]{1,2,0:T(8,128)} %get-tuple-element.421) | copy-start | bytes 98308
  322.1 36.3 %copy-start.39 = (bf16[2,576,192]{2,1,0:T(8,128)(2,1)S(1)}, bf16[2,576,192]{2,1,0:T(8,128)(2,1)}, u32[]{:S(2)}) copy-start(bf16[2,576,192]{2,1,0:T(8,128)(2,1)} %copy-done.38) | copy-start | bytes 1327108
  322.1 37.8 %copy-start.17 = (bf16[2,576,576]{2,1,0:T(8,128)(2,1)S(1)}, bf16[2,576,576]{2,1,0:T(8,128)(2,1)}, u32[]{:S(2)}) copy-start(bf16[2,576,576]{2,1,0:T(8,128)(2,1)} %copy-done.16) | copy-start | bytes 3981316
  453.5 33.0 %copy-start.40 = (bf16[2,576,192]{2,1,0:T(8,128)(2,1)S(1)}, bf16[2,576,192]{2,1,0:T(8,128)(2,1)}, u32[]{:S(2)}) copy-start(bf16[2,576,192]{2,1,0:T(8,128)(2,1)} %copy-done.38) | copy-start | bytes 1327108
  453.5 34.4 %copy-start.18 = (bf16[2,576,576]{2,1,0:T(8,128)(2,1)S(1)}, bf16[2,576,576]{2,1,0:T(8,128)(2,1)}, u32[]{:S(2)}) copy-start(bf16[2,576,576]{2,1,0:T(8,128)(2,1)} %copy-done.16) | copy-start | bytes 3981316
  (109 other events, 394.3 us)

commit v2 on v0

v2 whole, which is shorter than its diff:
```python
import functools, itertools
import jax
import jax.numpy as jnp
from jax import lax
from jax.experimental import pallas as pl
from jax.experimental.pallas import tpu as pltpu
from jax.sharding import PartitionSpec as P

CTX, FSDP = "ctx", "fsdp"
MESH = pl.DeviceIdType.MESH
PARTS = 2


def factors(n):
    known = {16: (4, 2, 2), 64: (2, 4, 4, 2)}
    if n in known:
        return known[n]
    out, p = [], 2
    while n > 1:
        while n % p == 0:
            out.append(p)
            n //= p
        p += 1
    return tuple(out) or (1,)


class Grid:
    def __init__(self, n):
        self.n = n
        self.dims = factors(n)
        strides, s = [], 1
        for d in reversed(self.dims):
            strides.insert(0, s)
            s *= d
        self.strides = tuple(strides)
        self.all = list(itertools.product(*[range(d) for d in self.dims]))
        self.ident = {d: i for i, d in enumerate(self.all)}

    def locate(self):
        me = lax.axis_index(CTX)
        self.me = me
        self.at = [lax.rem(me // s, d) for s, d in zip(self.strides, self.dims)]

    def index(self, delta):
        out = 0
        for c, d, n, s in zip(self.at, delta, self.dims, self.strides):
            out = out + (c if isinstance(d, int) and d == 0 else lax.rem(c + d, n)) * s
        return out

    def slot(self, delta):
        return sum(d * s for d, s in zip(delta, self.strides))

    def peer(self, axis, j):
        return self.index(tuple(j if a == axis else 0 for a in range(len(self.dims))))

    def orders(self):
        rest = list(range(1, len(self.dims)))
        return [[0] + rest, [0] + rest[::-1]]


def put(x, d, a):
    return tuple(x if i == a else v for i, v in enumerate(d))


def entry_barrier(g, fsdp):
    sem = pltpu.get_barrier_semaphore()
    count = 0
    f = lax.axis_index(FSDP)
    for a, d in enumerate(g.dims):
        for j in range(1, d):
            pl.semaphore_signal(sem, inc=1, device_id=(g.peer(a, j), f), device_id_type=MESH)
            count += 1
    if fsdp:
        pl.semaphore_signal(sem, inc=1, device_id=(g.me, 1 - f), device_id_type=MESH)
        count += 1
    pl.semaphore_wait(sem, count)


class Gather:
    def __init__(self, g, order, own, slot, send, recv):
        self.g, self.order, self.own, self.slot, self.send, self.recv = g, order, own, slot, send, recv
        self.sent = []

    def copy(self, src, index, axis, step, label, way):
        g = self.g
        i = g.slot(label)
        return pltpu.make_async_remote_copy(
            src_ref=src, dst_ref=self.slot(index), send_sem=self.send.at[way, i], recv_sem=self.recv.at[i],
            device_id=(g.peer(axis, step % g.dims[axis]), lax.axis_index(FSDP)), device_id_type=MESH)

    def start(self, copy, cond):
        self.sent.append((copy, cond))
        if cond is None:
            copy.start()
        else:
            pl.when(cond)(copy.start)

    def spread(self, delta, stage, src):
        g = self.g
        index = g.index(delta)
        for a in self.order[stage:]:
            n, c = g.dims[a], g.at[a]
            if n > 2:
                self.start(self.copy(src, index, a, 1, put(n - 1, delta, a), 0), c < n - 1)
                self.start(self.copy(src, index, a, -1, put(1, delta, a), 1), c > 0)
            else:
                for j in range(1, n):
                    self.start(self.copy(src, index, a, j, put(n - j, delta, a), 0), None)

    def begin(self):
        self.spread((0,) * len(self.g.dims), 0, self.own)

    def labels(self, stage):
        g, a = self.g, self.order[stage]
        n = g.dims[a]
        before = [range(g.dims[i]) if i in self.order[:stage] else range(1) for i in range(len(g.dims))]
        out = []
        if n > 2:
            c = g.at[a]
            near = [sorted((s for s in range(n) if s != k), key=lambda s: abs(s - k)) for k in range(n)]
            steps = []
            for t in range(n - 1):
                v = (near[0][t]) % n
                for k in range(1, n):
                    v = jnp.where(c == k, (near[k][t] - k) % n, v)
                steps.append(v)
        else:
            steps = list(range(1, n))
        for s in steps:
            for d in itertools.product(*before):
                out.append(put(s, d, a))
        return out

    def arrive(self, label, stage):
        g, a = self.g, self.order[stage]
        n, c = g.dims[a], g.at[a]
        index = g.index(label)
        here = self.slot(index)
        pltpu.make_async_remote_copy(
            src_ref=here, dst_ref=here, send_sem=self.send.at[0, 0], recv_sem=self.recv.at[g.slot(label)],
            device_id=(g.peer(a, 1), lax.axis_index(FSDP)), device_id_type=MESH).wait_recv()
        if n > 2:
            k = label[a]
            below = c + k >= n
            up = jnp.logical_and(below, c < n - 1)
            down = jnp.logical_and(jnp.logical_not(below), c > 0)
            self.start(self.copy(here, index, a, 1, put(k - 1, label, a), 0), up)
            self.start(self.copy(here, index, a, -1, put(k + 1, label, a), 1), down)
        self.spread(label, stage + 1, here)

    def end(self):
        for copy, cond in self.sent:
            if cond is None:
                copy.wait_send()
            else:
                pl.when(cond)(copy.wait_send)


def run_gathers(g, gs, stages=None):
    for stage in range(len(g.dims)):
        lists = [q.labels(stage) for q in gs]
        for i in range(max(map(len, lists))):
            for q, l in zip(gs, lists):
                if i < len(l):
                    q.arrive(l[i], stage)


def add_into(out, refs):
    rows = out.shape[0]
    step = max(s for s in range(16, 129, 16) if rows % s == 0)

    def some(i, carry):
        at = pl.ds(pl.multiple_of(i * step, step), step)
        out[at] = sum(r[at].astype(jnp.float32) for r in refs).astype(out.dtype)
        return carry

    lax.fori_loop(0, rows // step, some, 0)


def chosen(table, c):
    v = table[0]
    for k in range(1, len(table)):
        v = jnp.where(c == k, table[k], v)
    return v


class Reduce:
    def __init__(self, g, order, own, acc, land, send, recv):
        self.g, self.order, self.own, self.acc, self.land, self.send, self.recv = g, order, own, acc, land, send, recv
        self.sent = []
        self.stage = 0

    def held(self, delta):
        ref = self.own if self.stage == 0 else self.acc
        return ref(self.g.index(delta))

    def ship(self, src, label, axis, step, way, at_label):
        g = self.g
        copy = pltpu.make_async_remote_copy(
            src_ref=src, dst_ref=self.land.at[way, g.slot(at_label)], send_sem=self.send.at[g.slot(label)],
            recv_sem=self.recv.at[way, g.slot(at_label)],
            device_id=(g.peer(axis, step), lax.axis_index(FSDP)), device_id_type=MESH)
        copy.start()
        self.sent.append(copy)

    def landed(self, way, label):
        g = self.g
        ref = self.land.at[way, g.slot(label)]
        pltpu.make_async_remote_copy(
            src_ref=ref, dst_ref=ref, send_sem=self.send.at[0], recv_sem=self.recv.at[way, g.slot(label)],
            device_id=(g.peer(self.order[0], 1), lax.axis_index(FSDP)), device_id_type=MESH).wait_recv()
        return ref

    def labels(self, stage):
        gone = self.order[:stage]
        ranges = [range(1) if i in gone else range(n) for i, n in enumerate(self.g.dims)]
        far = lambda d: -sum(1 for i in self.order[stage:] if d[i])
        return sorted(itertools.product(*ranges), key=far)

    def steps(self, stage):
        g, a = self.g, self.order[stage]
        n, c = g.dims[a], g.at[a]
        keep = [d for d in self.labels(stage) if d[a] == 0]
        out = []
        if n == 2:
            if stage == 0:
                out += [functools.partial(self.swap, put(1, d, a), a) for d in keep]
            out += [functools.partial(self.take, d, stage) for d in keep]
        else:
            if stage == 0:
                out.append(self.copy_all)
            far = [sorted((k for k in range(1, n)), key=lambda k: -abs((p + k) % n - p)) for p in range(n)]
            for t in range(n - 1):
                k = chosen([far[p][t] for p in range(n)], c)
                out += [functools.partial(self.pass_on, put(k, d, a), stage) for d in keep]
            out += [functools.partial(self.close, d, stage) for d in keep]
        return out

    def copy_all(self):
        for d in self.g.all:
            i = self.g.index(d)
            add_into(self.acc(i), [self.own(i)])
        self.stage = 1

    def swap(self, d, axis):
        self.ship(self.held(d), d, axis, 1, 0, put(1, d, axis))

    def next_ship(self, d, stage):
        if stage + 1 < len(self.order):
            a = self.order[stage + 1]
            if self.g.dims[a] == 2 and d[a]:
                self.ship(self.acc(self.g.index(d)), d, a, 1, 0, d)

    def take(self, d, stage):
        a = self.order[stage]
        i = self.g.index(d)
        ref = self.own(i) if stage == 0 and self.stage == 0 else self.acc(i)
        add_into(self.acc(i), [ref, self.landed(0, put(1, d, a))])
        self.next_ship(d, stage)

    def pass_on(self, d, stage):
        g, a = self.g, self.order[stage]
        n, c = g.dims[a], g.at[a]
        k = d[a]
        up = c + k < n
        way = jnp.where(up, 0, 1)
        kept = self.acc(g.index(d))

        @pl.when(jnp.where(up, c > 0, c < n - 1))
        def _():
            add_into(kept, [kept, self.landed(way, d)])

        self.ship(kept, d, a, jnp.where(up, 1, n - 1), way, put(jnp.where(up, k - 1, lax.rem(k + 1, n)), d, a))

    def close(self, d, stage):
        g, a = self.g, self.order[stage]
        n, c = g.dims[a], g.at[a]
        kept = self.acc(g.index(d))

        @pl.when(c > 0)
        def _():
            add_into(kept, [kept, self.landed(0, d)])

        @pl.when(c < n - 1)
        def _():
            add_into(kept, [kept, self.landed(1, d)])

        self.next_ship(d, stage)

    def end(self):
        for copy in self.sent:
            copy.wait_send()


def interleave(lists):
    for i in range(max(map(len, lists))):
        for l in lists:
            if i < len(l):
                yield l[i]


def scatter_kernel(g, x_ref, o_ref, acc, land, send, recv):
    g.locate()
    entry_barrier(g, False)
    rows = x_ref.shape[1] // 2
    rs = []
    for p, order in enumerate(g.orders()):
        at = pl.ds(p * rows, rows)
        own = (lambda at: lambda i: x_ref.at[i, at])(at)
        kept = (lambda at: lambda i: acc.at[i, at])(at)
        rs.append(Reduce(g, order[::-1], own, kept, land.at[p], send.at[p], recv.at[p]))
    for stage in range(len(g.dims)):
        for step in interleave([r.steps(stage) for r in rs]):
            step()
        for r in rs:
            r.stage = 1
    o_ref[...] = acc[g.me].astype(jnp.float32)
    for r in rs:
        r.end()


def reduce_scatter_ctx(x, n, cid):
    g = Grid(n)
    _, rows, cols = x.shape
    dma = pltpu.SemaphoreType.DMA
    return pl.pallas_call(
        functools.partial(scatter_kernel, g),
        out_shape=jax.ShapeDtypeStruct((rows, cols), jnp.float32),
        in_specs=[pl.BlockSpec(memory_space=pltpu.VMEM)],
        out_specs=pl.BlockSpec(memory_space=pltpu.VMEM),
        scratch_shapes=[
            pltpu.VMEM((n, rows, cols), x.dtype),
            pltpu.VMEM((2, 2, n, rows // 2, cols), x.dtype),
            dma((2, n)),
            dma((2, 2, n)),
        ],
        compiler_params=pltpu.CompilerParams(collective_id=cid, has_side_effects=True, vmem_limit_bytes=60 << 20),
        name="ctx_reduce",
    )(x)


def reduce_all_kernel(g, x_ref, o_ref, own, kept, land, send, recv, gsend, grecv, psend, precv, lsem):
    g.locate()
    entry_barrier(g, True)
    f = lax.axis_index(FSDP)
    parts = x_ref.shape[1]
    orders = g.orders()
    rs, gs, local = [], [], []
    for p in range(parts):
        order = orders[p % 2]
        at = (lambda p: lambda i: kept.at[p, i])(p)
        rs.append(Reduce(g, order[::-1], at, at, land.at[p], send.at[p], recv.at[p]))
        gs.append(Gather(g, order, o_ref.at[p, g.me], (lambda p: lambda i: o_ref.at[p, i])(p), gsend.at[p], grecv.at[p]))
        c = pltpu.make_async_copy(x_ref.at[f, p], own.at[p], lsem.at[p])
        c.start()
        local.append(c)
    turns = [sorted(g.all, key=lambda d, a=r.order[0], r=r: (d[a] == 0, -sum(1 for v in d if v))) for r in rs]
    pairs = {}
    for i in range(g.n):
        for p in range(parts):
            d = turns[p][i]
            k = g.index(d)
            c = pltpu.make_async_remote_copy(
                src_ref=x_ref.at[1 - f, p, k], dst_ref=kept.at[p, k], send_sem=psend.at[p, g.slot(d)],
                recv_sem=precv.at[p, g.slot(d)], device_id=(g.me, 1 - f), device_id_type=MESH)
            c.start()
            pairs[p, d] = c
    for c in local:
        c.wait()
    first = [r.steps(0) for r in rs]
    for i in range(g.n):
        for p, r in enumerate(rs):
            d = turns[p][i]
            k = g.index(d)
            pairs[p, d].wait_recv()
            add_into(kept.at[p, k], [kept.at[p, k], own.at[p, k]])
            a = r.order[0]
            if g.dims[a] == 2 and d[a]:
                r.swap(d, a)
    for r in rs:
        r.stage = 1
    for stage in range(len(g.dims)):
        lists = []
        for r, steps in zip(rs, first):
            if stage == 0:
                lists.append([s for s in steps if getattr(s, "func", s).__name__ in ("take", "pass_on", "close")])
            else:
                lists.append(r.steps(stage))
        for step in interleave(lists):
            step()
    for p, q in enumerate(gs):
        add_into(o_ref.at[p, g.me], [kept.at[p, g.me]])
        q.begin()
    run_gathers(g, gs)
    for c in pairs.values():
        c.wait_send()
    for r in rs:
        r.end()
    for q in gs:
        q.end()


def reduce_all(x, n, cid):
    g = Grid(n)
    _, parts, _, rows, cols = x.shape
    blk = (parts, n, rows, cols)
    dma = pltpu.SemaphoreType.DMA
    return pl.pallas_call(
        functools.partial(reduce_all_kernel, g),
        out_shape=jax.ShapeDtypeStruct(blk, x.dtype),
        in_specs=[pl.BlockSpec(memory_space=pl.ANY)],
        out_specs=pl.BlockSpec(memory_space=pltpu.VMEM),
        scratch_shapes=[
            pltpu.VMEM(blk, x.dtype),
            pltpu.VMEM(blk, x.dtype),
            pltpu.VMEM((parts, 2, n, rows, cols), x.dtype),
            dma((parts, n)),
            dma((parts, 2, n)),
            dma((parts, 2, n)),
            dma((parts, n)),
            dma((parts, n)),
            dma((parts, n)),
            dma((parts,)),
        ],
        compiler_params=pltpu.CompilerParams(collective_id=cid, has_side_effects=True, vmem_limit_bytes=64 << 20),
        name="grad_reduce",
    )(x)


def gather_kernel(g, count, spots, *refs):
    k = 2 if count else 1
    xs, ws = refs[:k], picked(refs[k : k + count], spots)
    refs = refs[k + count :]
    os, fulls = refs[:k], refs[k : k + len(spots)]
    refs = refs[k + len(spots) :]
    send, recv, local = refs[:3]
    g.locate()
    entry_barrier(g, bool(count))
    rows = xs[0].shape[0] // 2
    gs = []
    for p, order in enumerate(g.orders()):
        at = pl.ds(p * rows, rows)
        slot = (lambda at: lambda i: os[0].at[i, at])(at)
        gs.append(Gather(g, order, xs[0].at[at], slot, send.at[p], recv.at[p]))
    if count:
        gs.append(Gather(g, g.orders()[0], xs[1], lambda i: os[1].at[i], send.at[2], recv.at[2]))
    for q in gs:
        q.begin()
    mine = [pltpu.make_async_copy(x, o.at[g.me], local.at[i]) for i, (x, o) in enumerate(zip(xs, os))]
    for c in mine:
        c.start()
    swap = Swap(ws, fulls, *refs[3:]) if count else None
    if count:
        swap.begin()
    run_gathers(g, gs)
    for c in mine:
        c.wait()
    if count:
        swap.end()
    for q in gs:
        q.end()


class Swap:
    def __init__(self, srcs, dsts, send, recv, load, store, *stages):
        c, f = lax.axis_index(CTX), lax.axis_index(FSDP)
        self.remote, self.loads, self.stores = [], [], []
        for i, (s, d, v) in enumerate(zip(srcs, dsts, stages)):
            self.remote.append(
                pltpu.make_async_remote_copy(
                    src_ref=s, dst_ref=d.at[f], send_sem=send.at[i], recv_sem=recv.at[i], device_id=(c, 1 - f),
                    device_id_type=MESH))
            self.loads.append(pltpu.make_async_copy(s, v, load.at[i]))
            self.stores.append(pltpu.make_async_copy(v, d.at[f], store.at[i]))

    def begin(self):
        for c in self.remote + self.loads:
            c.start()
        for a, b in zip(self.loads, self.stores):
            a.wait()
            b.start()

    def end(self):
        for c in self.stores + self.remote:
            c.wait()

    @staticmethod
    def scratch(picks):
        return [pltpu.SemaphoreType.DMA((len(picks),))] * 4 + [pltpu.VMEM(shape_of(a, l), a.dtype) for a, l in picks]


def distinct(picks):
    arrays, places = [], []
    for a, l in picks:
        spot = next((i for i, b in enumerate(arrays) if b is a), None)
        if spot is None:
            spot = len(arrays)
            arrays.append(a)
        places.append((spot, l))
    return arrays, places


def picked(refs, places):
    return [refs[i] if l is None else refs[i].at[l] for i, l in places]


def shape_of(a, l):
    return a.shape if l is None else a.shape[1:]


def all_gather_ctx(x, n, cid, places=None, weights=()):
    g = Grid(n)
    arrays, spots = distinct(weights)
    count = len(arrays)
    xs = [x] if places is None else [x, places]
    dma = pltpu.SemaphoreType.DMA
    vmem, anywhere = pl.BlockSpec(memory_space=pltpu.VMEM), pl.BlockSpec(memory_space=pl.ANY)
    parts = len(xs) + 1
    return pl.pallas_call(
        functools.partial(gather_kernel, g, count, spots),
        out_shape=[jax.ShapeDtypeStruct((n, *v.shape), v.dtype) for v in xs]
        + [jax.ShapeDtypeStruct((2, *shape_of(a, l)), a.dtype) for a, l in weights],
        in_specs=[vmem] * len(xs) + [anywhere] * count,
        out_specs=[vmem] * len(xs) + [anywhere] * len(weights),
        scratch_shapes=[dma((parts, 2, n)), dma((parts, n)), dma((2,))] + (Swap.scratch(weights) if count else []),
        compiler_params=pltpu.CompilerParams(collective_id=cid, has_side_effects=True, vmem_limit_bytes=60 << 20),
        name="ctx_gather",
    )(*xs, *arrays)


def exchange_kernel(count, spots, *refs):
    srcs, dsts = picked(refs[:count], spots), refs[count : count + len(spots)]
    c, f = lax.axis_index(CTX), lax.axis_index(FSDP)
    sem = pltpu.get_barrier_semaphore()
    pl.semaphore_signal(sem, inc=1, device_id=(c, 1 - f), device_id_type=MESH)
    pl.semaphore_wait(sem, 1)
    swap = Swap(srcs, dsts, *refs[count + len(spots) :])
    swap.begin()
    swap.end()


def exchange(picks, cid):
    arrays, spots = distinct(picks)
    anywhere = pl.BlockSpec(memory_space=pl.ANY)
    return pl.pallas_call(
        functools.partial(exchange_kernel, len(arrays), spots),
        out_shape=[jax.ShapeDtypeStruct((2, *shape_of(a, l)), a.dtype) for a, l in picks],
        in_specs=[anywhere] * len(arrays),
        out_specs=[anywhere] * len(picks),
        scratch_shapes=Swap.scratch(picks),
        compiler_params=pltpu.CompilerParams(collective_id=cid, has_side_effects=True),
        name="exchange",
    )(*arrays)


HEADS = 9
KV_HEADS = 3
HEAD = 64
GROUP = HEADS // KV_HEADS
EPS = 1e-05
ROPE_BASE = 100000.0
F32, BF16 = jnp.float32, jnp.bfloat16
CHUNK = 256
ROOM = 62 << 20


def nn(a, b):
    return lax.dot_general(a, b, (((1,), (0,)), ((), ())), preferred_element_type=F32)


def nt(a, b):
    return lax.dot_general(a, b, (((1,), (1,)), ((), ())), preferred_element_type=F32)


def tn(a, b):
    return lax.dot_general(a, b, (((0,), (0,)), ((), ())), preferred_element_type=F32)


def rms(v, gain):
    return v * lax.rsqrt(jnp.mean(v * v, axis=-1, keepdims=True) + EPS) * gain


def rms_back(v, gain, e):
    r = lax.rsqrt(jnp.mean(v * v, axis=-1, keepdims=True) + EPS)
    eg = e * gain
    dv = r * eg - v * (r * r * r) * jnp.mean(eg * v, axis=-1, keepdims=True)
    return dv, jnp.sum(e * v * r, axis=0, keepdims=True)


def rope(t, cos, sin):
    width = t.shape[1]
    out = []
    for lo in range(0, width, 128):
        w = min(128, width - lo)
        u = t[:, lo : lo + w]
        if w == 128:
            lane = lax.broadcasted_iota(jnp.int32, u.shape, 1) % HEAD
            other = jnp.where(lane < HEAD // 2, pltpu.roll(u, 128 - HEAD // 2, 1), pltpu.roll(u, HEAD // 2, 1))
        else:
            other = jnp.concatenate([u[:, HEAD // 2 :], u[:, : HEAD // 2]], axis=1)
        out.append((lo, w, u * cos[:, :w] + other * sin[:, :w]))
    return out


def call(kernel, outs, args, name, scratch=(), prefetch=0, blob=None):
    vmem = pl.BlockSpec(memory_space=pltpu.VMEM)
    smem = pl.BlockSpec(memory_space=pltpu.SMEM)
    anywhere = pl.BlockSpec(memory_space=pl.ANY)
    if blob is not None:
        new = isinstance(blob, tuple)
        return pl.pallas_call(
            kernel,
            out_shape=[jax.ShapeDtypeStruct(s, t) for s, t in outs] + [jax.ShapeDtypeStruct(blob if new else blob.shape, BF16)],
            in_specs=[vmem] * len(args) + ([] if new else [anywhere]),
            out_specs=[vmem] * len(outs) + [anywhere],
            scratch_shapes=list(scratch),
            input_output_aliases={} if new else {len(args): len(outs)},
            compiler_params=pltpu.CompilerParams(vmem_limit_bytes=ROOM),
            name=name,
        )(*args, *([] if new else [blob]))
    return pl.pallas_call(
        kernel,
        out_shape=[jax.ShapeDtypeStruct(s, t) for s, t in outs],
        in_specs=[smem] * prefetch + [vmem] * (len(args) - prefetch),
        out_specs=[vmem] * len(outs),
        scratch_shapes=list(scratch),
        compiler_params=pltpu.CompilerParams(vmem_limit_bytes=ROOM),
        name=name,
    )(*args)


def pre_kernel(x_ref, gain_ref, wq_ref, wk_ref, wv_ref, cos_ref, sin_ref, a_ref, q_ref, kv_ref):
    a = rms(x_ref[...].astype(F32), gain_ref[...]).astype(BF16)
    a_ref[...] = a
    cos, sin = cos_ref[...], sin_ref[...]
    for lo, w, piece in rope(nn(a, wq_ref[...]), cos, sin):
        q_ref[:, lo : lo + w] = piece.astype(BF16)
    keys = jnp.concatenate([piece for _, _, piece in rope(nn(a, wk_ref[...]), cos, sin)], axis=1)
    kv_ref[...] = jnp.concatenate([keys, nn(a, wv_ref[...])], axis=1).astype(BF16)


def pre(x, gain, wq, wk, wv, cos, sin):
    m, d = x.shape
    e = wk.shape[1]
    return call(pre_kernel, [((m, d), BF16), ((m, d), BF16), ((m, 2 * e), BF16)], (x, gain, wq, wk, wv, cos, sin), "pre")


def half_of(u, src, dst):
    if src != dst:
        u = pltpu.roll(u, HEAD, 1)
    lane = lax.broadcasted_iota(jnp.int32, u.shape, 1)
    return jnp.where((lane < HEAD) if dst == 0 else (lane >= HEAD), u, 0.0)


def head_chunk(ref, s, h):
    lo = (h // 2) * 128
    width = ref.shape[-1]
    if lo + 128 <= width:
        return ref[s, :, lo : lo + 128].astype(F32)
    u = ref[s, :, lo:width].astype(F32)
    return jnp.concatenate([u, jnp.zeros_like(u)], axis=1)


def pack_heads(ref, s, dst, g, half, scale):
    rows = ref.shape[1] // 2
    for i in range(GROUP):
        h = g * GROUP + i
        u = half_of(head_chunk(ref, s, h) * scale, h % 2, half).astype(BF16)
        for part in range(2):
            dst[g * 2 + part, i * rows : (i + 1) * rows, :] = u[part * rows : (part + 1) * rows]


def sort_rows(block_ref, s, src, dst, n, rows):
    def one(j, carry):
        b = block_ref[j, s, 0] // rows
        dst[pl.ds(pl.multiple_of(b * rows, rows), rows), :] = src[j, s, 0:rows, :]
        dst[pl.ds(pl.multiple_of((2 * n - 1 - b) * rows, rows), rows), :] = src[j, s, rows : 2 * rows, :]
        return carry

    lax.fori_loop(0, n, one, 0)


def visible(c, block, rows, shape):
    key = lax.broadcasted_iota(jnp.int32, shape, 0) + c * CHUNK
    query = lax.broadcasted_iota(jnp.int32, shape, 1) % rows + block * rows
    return key <= query


def key_lanes(g):
    return (g // 2) * 128, g % 2


def value_lanes(g):
    return ((KV_HEADS + g) // 2) * 128, (KV_HEADS + g) % 2


def attend_kernel(n, block_ref, mine_ref, q_ref, kv_ref, o_ref, lse_ref, sorted_ref, qp_ref, st_ref):
    rows = q_ref.shape[1] // 2
    wide = GROUP * rows

    def sequence(s, carry):
        sort_rows(block_ref, s, kv_ref, sorted_ref, n, rows)
        for g in range(KV_HEADS):
            pack_heads(q_ref, s, qp_ref, g, key_lanes(g)[1], HEAD**-0.5)
        low = mine_ref[s, 0] // rows
        for g in range(KV_HEADS):
            klo, _ = key_lanes(g)
            vlo, vhalf = value_lanes(g)
            for part in range(2):
                block = low if part == 0 else 2 * n - 1 - low
                last = block * rows // CHUNK
                qp = qp_ref[g * 2 + part]

                def score(c, top, masked):
                    at = pl.ds(pl.multiple_of(c * CHUNK, CHUNK), CHUNK)
                    st = nt(sorted_ref[at, klo : klo + 128], qp)
                    if masked:
                        st = jnp.where(visible(c, block, rows, st.shape), st, -1e30)
                    st_ref[at, :] = st
                    return jnp.maximum(top, jnp.max(st.reshape(CHUNK // 8, 8, wide), axis=0))

                top = lax.fori_loop(0, last, lambda c, t: score(c, t, False), jnp.full((8, wide), -1e30, F32))
                top = jnp.max(score(last, top, True), axis=0, keepdims=True)

                def mix(c, state):
                    total, acc = state
                    at = pl.ds(pl.multiple_of(c * CHUNK, CHUNK), CHUNK)
                    p = jnp.exp(st_ref[at, :] - top)
                    total = total + jnp.sum(p.reshape(CHUNK // 8, 8, wide), axis=0)
                    return total, acc + tn(sorted_ref[at, vlo : vlo + 128], p.astype(BF16))

                total, acc = lax.fori_loop(0, last + 1, mix, (jnp.zeros((8, wide), F32), jnp.zeros((128, wide), F32)))
                total = jnp.sum(total, axis=0, keepdims=True)
                lse_ref[s, g * 2 + part] = top + jnp.log(total)
                out = (acc[vhalf * HEAD : (vhalf + 1) * HEAD] / total).T
                for i in range(GROUP):
                    h = g * GROUP + i
                    o_ref[s, part * rows : (part + 1) * rows, h * HEAD : (h + 1) * HEAD] = out[i * rows : (i + 1) * rows]
        return carry

    lax.fori_loop(0, q_ref.shape[0], sequence, 0)


def attend(blocks, mine, q, kv):
    seqs, r, d = q.shape
    n = kv.shape[0]
    wide = GROUP * r // 2
    scratch = [
        pltpu.VMEM((n * r, kv.shape[-1]), BF16),
        pltpu.VMEM((2 * KV_HEADS, wide, 128), BF16),
        pltpu.VMEM((n * r, wide), F32),
    ]
    outs = [((seqs, r, d), F32), ((seqs, 2 * KV_HEADS, 1, wide), F32)]
    return call(functools.partial(attend_kernel, n), outs, (blocks, mine, q, kv), "attend", scratch, 2)


def attend_back_kernel(
    n, block_ref, mine_ref, q_ref, kv_ref, do_ref, o_ref, lse_ref, dq_ref, dkv_ref, sorted_ref, qp_ref, dop_ref, acc_ref, delta_ref
):
    rows = q_ref.shape[1] // 2
    wide = GROUP * rows

    def sequence(s, carry):
        sort_rows(block_ref, s, kv_ref, sorted_ref, n, rows)
        for g in range(KV_HEADS):
            pack_heads(q_ref, s, qp_ref, g, key_lanes(g)[1], HEAD**-0.5)
            pack_heads(do_ref, s, dop_ref, g, value_lanes(g)[1], 1.0)
        acc_ref[...] = jnp.zeros_like(acc_ref)
        low = mine_ref[s, 0] // rows
        for g in range(KV_HEADS):
            klo, khalf = key_lanes(g)
            vlo, vhalf = value_lanes(g)
            pieces = []
            for part in range(2):
                block = low if part == 0 else 2 * n - 1 - low
                last = block * rows // CHUNK
                qp, dop = qp_ref[g * 2 + part], dop_ref[g * 2 + part]
                lse = lse_ref[s, g * 2 + part]
                sums = []
                for i in range(GROUP):
                    h = g * GROUP + i
                    lanes = slice(h * HEAD, (h + 1) * HEAD)
                    at = slice(part * rows, (part + 1) * rows)
                    both = do_ref[s, at, lanes].astype(F32) * o_ref[s, at, lanes]
                    sums.append(jnp.sum(both, axis=1, keepdims=True))
                delta_ref[...] = jnp.concatenate(sums, axis=0) + jnp.zeros((wide, 128), F32)
                delta = delta_ref[...].T[0:1]

                def step(c, dq, masked):
                    at = pl.ds(pl.multiple_of(c * CHUNK, CHUNK), CHUNK)
                    keys = sorted_ref[at, klo : klo + 128]
                    p = jnp.exp(nt(keys, qp) - lse)
                    if masked:
                        p = jnp.where(visible(c, block, rows, p.shape), p, 0.0)
                    dp = nt(sorted_ref[at, vlo : vlo + 128], dop)
                    ds = (p * (dp - delta)).astype(BF16)
                    acc_ref[at, vlo : vlo + 128] += nn(p.astype(BF16), dop)
                    acc_ref[at, klo : klo + 128] += nn(ds, qp)
                    return dq + tn(ds, keys)

                dq = lax.fori_loop(0, last, lambda c, t: step(c, t, False), jnp.zeros((wide, 128), F32))
                dq = step(last, dq, True) * HEAD**-0.5
                for i in range(GROUP):
                    h = g * GROUP + i
                    dq_ref[s, part * rows : (part + 1) * rows, h * HEAD : (h + 1) * HEAD] = dq[
                        i * rows : (i + 1) * rows, khalf * HEAD : (khalf + 1) * HEAD
                    ]

        def one(j, carry):
            b = block_ref[j, s, 0] // rows
            dkv_ref[j, s, 0:rows, :] = acc_ref[pl.ds(pl.multiple_of(b * rows, rows), rows), :].astype(BF16)
            dkv_ref[j, s, rows : 2 * rows, :] = acc_ref[
                pl.ds(pl.multiple_of((2 * n - 1 - b) * rows, rows), rows), :
            ].astype(BF16)
            return carry

        lax.fori_loop(0, n, one, 0)
        return carry

    lax.fori_loop(0, q_ref.shape[0], sequence, 0)


def attend_back(blocks, mine, q, kv, do, o, lse):
    seqs, r, d = q.shape
    n = kv.shape[0]
    wide = GROUP * r // 2
    scratch = [
        pltpu.VMEM((n * r, kv.shape[-1]), BF16),
        pltpu.VMEM((2 * KV_HEADS, wide, 128), BF16),
        pltpu.VMEM((2 * KV_HEADS, wide, 128), BF16),
        pltpu.VMEM((n * r, kv.shape[-1]), F32),
        pltpu.VMEM((wide, 128), F32),
    ]
    outs = [((seqs, r, d), F32), (kv.shape, BF16)]
    args = (blocks, mine, q, kv, do, o, lse)
    return call(functools.partial(attend_back_kernel, n), outs, args, "attend_back", scratch, 2)


def post_kernel(o_ref, x_ref, wo_ref, gain_ref, wg_ref, wu_ref, wd_ref, h_ref, b_ref, gate_ref, up_ref, y_ref):
    h = x_ref[...].astype(F32) + nn(o_ref[...].astype(BF16), wo_ref[...])
    h_ref[...] = h
    y_ref[...] = h
    b_ref[...] = rms(h, gain_ref[...]).astype(BF16)

    def some(i, carry):
        at = pl.ds(pl.multiple_of(i * CHUNK, CHUNK), CHUNK)
        b = b_ref[...]
        gate, up = nn(b, wg_ref[:, at]), nn(b, wu_ref[:, at])
        gate_ref[:, at], up_ref[:, at] = gate, up
        m = (gate * jax.nn.sigmoid(gate) * up).astype(BF16)
        y_ref[...] += nn(m, wd_ref[at, :])
        return carry

    lax.fori_loop(0, wg_ref.shape[1] // CHUNK, some, 0)


def post(o, x, wo, gain, wg, wu, wd):
    m, d = x.shape
    ff = wg.shape[1]
    outs = [((m, d), F32), ((m, d), BF16), ((m, ff), F32), ((m, ff), F32), ((m, d), F32)]
    return call(post_kernel, outs, (o, x, wo, gain, wg, wu, wd), "post")


def put_tiles(blob, base, value, count):
    rows = value.shape[0] // 2
    if value.shape[1] < count * 128:
        value = jnp.concatenate([value, jnp.zeros((2 * rows, count * 128 - value.shape[1]), value.dtype)], axis=1)
    for f in range(2):
        for j in range(count):
            piece = value[f * rows : (f + 1) * rows, j * 128 : (j + 1) * 128]
            blob[f, pl.ds(base + j * (rows // 16), rows // 16)] = piece.reshape(rows // 16, 16, 128)


def put_norm(blob, at, dg):
    half = dg.shape[1] // 2
    for f in range(2):
        v = dg[:, f * half : (f + 1) * half]
        v = jnp.concatenate([v, jnp.zeros((1, 384 - half), F32)], axis=1)
        rows = jnp.concatenate([v[:, 0:128], v[:, 128:256], v[:, 256:384], jnp.zeros((13, 128), F32)], axis=0)
        blob[f, at] = rows.astype(BF16)


def wide_of(cols):
    return -(-cols // 128)


def ffn_back_kernel(base, new, *refs):
    dy_ref, h_ref, b_ref, gate_ref, up_ref, o_ref, gain_ref, wo_ref, wg_ref, wu_ref, wd_ref = refs[:11]
    dh_ref, do_ref, out_ref, blob_ref, dyb_ref, db_ref, bt_ref, sem = refs[11 if new else 12 :]
    m, d = h_ref.shape
    ff = wg_ref.shape[1]
    half = d // 2 // 16
    gate_at, up_at = 0, (ff // 128) * half
    down_at = 2 * up_at
    down_rows = ff // 2 // 16
    out_at = down_at + wide_of(d) * down_rows
    norm_at = out_at + wide_of(d) * half
    dyb_ref[...] = dy_ref[...].astype(BF16)
    db_ref[...] = jnp.zeros_like(db_ref)
    bt_ref[...] = b_ref[...].T

    def some(i, carry):
        at = pl.ds(pl.multiple_of(i * CHUNK, CHUNK), CHUNK)
        dyb = dyb_ref[...]
        dm = nt(dyb, wd_ref[at, :])
        gate, up = gate_ref[:, at], up_ref[:, at]
        sig = jax.nn.sigmoid(gate)
        silu = gate * sig
        mid = (silu * up).astype(BF16)
        dgate = (dm * up * sig * (1.0 + gate * (1.0 - sig))).astype(BF16)
        dup = (dm * silu).astype(BF16)
        db_ref[...] += nt(dgate, wg_ref[:, at]) + nt(dup, wu_ref[:, at])
        bt = bt_ref[...]
        put_tiles(blob_ref, gate_at + i * (CHUNK // 128) * half, nn(bt, dgate).astype(BF16), CHUNK // 128)
        put_tiles(blob_ref, up_at + i * (CHUNK // 128) * half, nn(bt, dup).astype(BF16), CHUNK // 128)
        gd = tn(mid, dyb).astype(BF16)
        gd = jnp.concatenate([gd, jnp.zeros((CHUNK, wide_of(d) * 128 - d), BF16)], axis=1)
        per = ff // 2 // CHUNK
        f = i // per
        for j in range(wide_of(d)):
            start = down_at + j * down_rows + (i - f * per) * (CHUNK // 16)
            blob_ref[f, pl.ds(start, CHUNK // 16)] = gd[:, j * 128 : (j + 1) * 128].reshape(CHUNK // 16, 16, 128)
        return carry

    lax.fori_loop(0, ff // CHUNK, some, 0)
    first = pltpu.make_async_copy(blob_ref.at[:, pl.ds(0, out_at)], out_ref.at[:, pl.ds(base, out_at)], sem.at[0])
    first.start()
    dv, dg = rms_back(h_ref[...], gain_ref[...], db_ref[...])
    dh = dy_ref[...].astype(F32) + dv
    dh_ref[...] = dh
    dhb = dh.astype(BF16)
    do_ref[...] = nt(dhb, wo_ref[...]).astype(BF16)
    put_tiles(blob_ref, out_at, tn(o_ref[...].astype(BF16), dhb).astype(BF16), wide_of(d))
    put_norm(blob_ref, norm_at, dg)
    rest = norm_at + 1 - out_at
    second = pltpu.make_async_copy(
        blob_ref.at[:, pl.ds(out_at, rest)], out_ref.at[:, pl.ds(base + out_at, rest)], sem.at[1]
    )
    second.start()
    first.wait()
    second.wait()


def ffn_tiles(d, ff):
    return 2 * (ff // 128) * (d // 32) + wide_of(d) * (ff // 32) + wide_of(d) * (d // 32) + 1


def pre_tiles(d, e):
    return wide_of(d) * (d // 32) + wide_of(2 * e) * (d // 32) + 1


def ffn_back(blob, base, dy, h, b, gate, up, o, gain, wo, wg, wu, wd):
    m, d = h.shape
    ff = wg.shape[1]
    scratch = [
        pltpu.VMEM((2, ffn_tiles(d, ff), 16, 128), BF16),
        pltpu.VMEM((m, d), BF16),
        pltpu.VMEM((m, d), F32),
        pltpu.VMEM((d, m), BF16),
        pltpu.SemaphoreType.DMA((2,)),
    ]
    kernel = functools.partial(ffn_back_kernel, base, isinstance(blob, tuple))
    args = (dy, h, b, gate, up, o, gain, wo, wg, wu, wd)
    return call(kernel, [((m, d), F32), ((m, d), BF16)], args, "ffn_back", scratch, blob=blob)


def pre_back_kernel(base, *refs):
    dq_ref, dkv_ref, a_ref, x_ref, dh_ref, gain_ref, wq_ref, wk_ref, wv_ref, cos_ref, sin_ref = refs[:11]
    dx_ref, out_ref, blob_ref, dqp_ref, sem = refs[12:]
    d = x_ref.shape[1]
    e = wk_ref.shape[1]
    half = d // 2 // 16
    cos, sin = cos_ref[...], -sin_ref[...]
    for lo, w, piece in rope(dq_ref[...], cos, sin):
        dqp_ref[:, lo : lo + w] = piece.astype(BF16)
    dqp = dqp_ref[...]
    dkv = dkv_ref[...]
    dkp = jnp.concatenate([piece for _, _, piece in rope(dkv[:, :e], cos, sin)], axis=1).astype(BF16)
    dvr = dkv[:, e:].astype(BF16)
    da = nt(dqp, wq_ref[...]) + nt(dkp, wk_ref[...]) + nt(dvr, wv_ref[...])
    dv, dg = rms_back(x_ref[...].astype(F32), gain_ref[...], da)
    kv_at = wide_of(d) * half
    norm_at = kv_at + wide_of(2 * e) * half
    put_norm(blob_ref, norm_at, dg)
    left = blob_ref.shape[1] - norm_at - 1
    if left:
        blob_ref[:, pl.ds(norm_at + 1, left)] = jnp.zeros((2, left, 16, 128), BF16)
    at = a_ref[...].T
    put_tiles(blob_ref, 0, nn(at, dqp).astype(BF16), wide_of(d))
    put_tiles(blob_ref, kv_at, jnp.concatenate([nn(at, dkp), nn(at, dvr)], axis=1).astype(BF16), wide_of(2 * e))
    done = pltpu.make_async_copy(blob_ref, out_ref.at[:, pl.ds(base, blob_ref.shape[1])], sem)
    done.start()
    dx_ref[...] = dh_ref[...] + dv
    done.wait()


def pre_back(blob, base, tiles, dq, dkv, a, x, dh, gain, wq, wk, wv, cos, sin):
    m, d = x.shape
    scratch = [pltpu.VMEM((2, tiles, 16, 128), BF16), pltpu.VMEM((m, d), BF16), pltpu.SemaphoreType.DMA(())]
    args = (dq, dkv, a, x, dh, gain, wq, wk, wv, cos, sin)
    return call(functools.partial(pre_back_kernel, base), [((m, d), F32)], args, "pre_back", scratch, blob=blob)


def unpack_kernel(places, blob, *outs):
    g_attn, gq, gk, gv, go, g_ffn, gg, gu, gd = outs
    half, d, e, ff = gq.shape[1], gq.shape[2], gk.shape[2], gg.shape[2]
    t = half // 16

    def take(base, at, rows, cols, out, l, skip=0):
        for lo in range(0, cols, 128):
            w = min(128, cols - lo)
            j = (skip + lo) // 128
            if (skip + lo) % 128 == 0:
                u = blob[pl.ds(base + at + j * (rows // 16), rows // 16)].reshape(rows, 128)[:, :w]
            else:
                u = blob[pl.ds(base + at + j * (rows // 16), rows // 16)].reshape(rows, 128)[:, 64:]
                if w > 64:
                    v = blob[pl.ds(base + at + (j + 1) * (rows // 16), rows // 16)].reshape(rows, 128)[:, : w - 64]
                    u = jnp.concatenate([u.astype(F32), v.astype(F32)], axis=1)
            out[l, :, lo : lo + w] = u.astype(F32)

    def norm(base, at, out, l):
        u = blob[base + at].astype(F32)
        row = jnp.concatenate([u[0:1], u[1:2], u[2:3]], axis=1)
        out[l : l + 1, :] = row[:, :half]

    for l, (ffn, att) in enumerate(places):
        up_at = (ff // 128) * t
        down_at = 2 * up_at
        out_at = down_at + wide_of(d) * (gd.shape[1] // 16)
        take(ffn, 0, half, ff, gg, l)
        take(ffn, up_at, half, ff, gu, l)
        take(ffn, down_at, gd.shape[1], d, gd, l)
        take(ffn, out_at, half, d, go, l)
        norm(ffn, out_at + wide_of(d) * t, g_ffn, l)
        take(att, 0, half, d, gq, l)
        kv_at = wide_of(d) * t
        take(att, kv_at, half, e, gk, l)
        take(att, kv_at, half, e, gv, l, e)
        norm(att, kv_at + wide_of(2 * e) * t, g_attn, l)


def unpack(blob, places, shapes):
    return call(functools.partial(unpack_kernel, places), [(s, F32) for s in shapes], (blob,), "unpack")


def body(tokens, positions, norm_attn, w_query, w_key, w_value, w_out, norm_ffn, w_gate, w_up, w_down, cotangent):
    layers = norm_attn.shape[0]
    n = lax.axis_size(CTX)
    seqs, r, d = tokens.shape
    m = seqs * r
    e, ff = w_key.shape[2], w_gate.shape[2]
    own = (w_query, w_key, w_value, w_out, w_gate, w_up, w_down)
    shards = [(w, l) for l in range(layers) for w in own]
    full = exchange([(norm_attn, None), (norm_ffn, None), *shards[:3]], 0)
    gains = [jnp.swapaxes(v, 0, 1).reshape(layers, 1, d).astype(F32) for v in full[:2]]
    full = full[2:]
    frequency = jnp.exp(jnp.arange(HEAD // 2, dtype=F32) * (-jnp.log(ROPE_BASE) / (HEAD // 2)))
    angles = positions.reshape(m, 1).astype(F32) * frequency
    cos, sin = jnp.cos(angles), jnp.sin(angles)
    cos = jnp.concatenate([cos] * 4, axis=1)
    sin = jnp.concatenate([-sin, sin] * 2, axis=1)
    x = tokens.reshape(m, d)
    kept = []
    weights = []

    def joined(w):
        return w.reshape(2 * w.shape[1], w.shape[2])

    for l in range(layers):
        wq, wk, wv = (joined(w) for w in full[l * len(own) : l * len(own) + 3])
        a, q, kv = pre(x, gains[0][l], wq, wk, wv, cos, sin)
        q = q.reshape(seqs, r, d)
        if l == 0:
            kv, places, *rest = all_gather_ctx(kv, n, 1, positions, shards[3:])
            full = [*full, *rest]
        else:
            (kv,) = all_gather_ctx(kv, n, 1 + l)
        wo, wg, wu, wd = (joined(w) for w in full[l * len(own) + 3 : (l + 1) * len(own)])
        weights.append((wq, wk, wv, wo, wg, wu, wd))
        kv = kv.reshape(n, seqs, r, 2 * e)
        o, lse = attend(places, positions, q, kv)
        h, b, gate, up, y = post(o.reshape(m, d), x, wo, gains[1][l], wg, wu, wd)
        kept.append((x, a, q, kv, o, lse, h, b, gate, up))
        x = y
    output = x.reshape(seqs, r, d).astype(BF16)
    dy = cotangent.reshape(m, d)
    one, two = ffn_tiles(d, ff), pre_tiles(d, e)
    unit = 2 * PARTS * n
    whole = -(-layers * (one + two) // unit) * unit
    blob = (2, whole, 16, 128)
    spots = []
    for l in reversed(range(layers)):
        wq, wk, wv, wo, wg, wu, wd = weights[l]
        x, a, q, kv, o, lse, h, b, gate, up = kept[l]
        start = (layers - 1 - l) * (one + two)
        spots.insert(0, (start, start + one))
        dh, do, blob = ffn_back(blob, start, dy, h, b, gate, up, o.reshape(m, d), gains[1][l], wo, wg, wu, wd)
        dq, dkv = attend_back(places, positions, q, kv, do.reshape(seqs, r, d), o, lse)
        dkv = reduce_scatter_ctx(dkv.reshape(n, m, 2 * e), n, 1 + layers + l)
        tiles = two if l else whole - start - one
        dy, blob = pre_back(
            blob, start + one, tiles, dq.reshape(m, d), dkv, a, x, dh, gains[0][l], wq, wk, wv, cos, sin
        )
    total = reduce_all(blob.reshape(2, PARTS, n, -1, 128), n, 1 + 2 * layers)
    shapes = [norm_attn.shape, *[w.shape for w in own[:4]], norm_ffn.shape, *[w.shape for w in own[4:]]]
    grads = unpack(total.reshape(whole, 16, 128), spots, shapes)
    return (output, dy.reshape(seqs, r, d), *grads)


def solution(mesh):
    in_specs = (
        P("fsdp", "ctx", None),
        P("fsdp", "ctx"),
        P(None, "fsdp"),
        P(None, "fsdp", None),
        P(None, "fsdp", None),
        P(None, "fsdp", None),
        P(None, "fsdp", None),
        P(None, "fsdp"),
        P(None, "fsdp", None),
        P(None, "fsdp", None),
        P(None, "fsdp", None),
        P("fsdp", "ctx", None),
    )
    out_specs = (
        P("fsdp", "ctx", None),
        P("fsdp", "ctx", None),
        P(None, "fsdp"),
        P(None, "fsdp", None),
        P(None, "fsdp", None),
        P(None, "fsdp", None),
        P(None, "fsdp", None),
        P(None, "fsdp"),
        P(None, "fsdp", None),
        P(None, "fsdp", None),
        P(None, "fsdp", None),
    )
    return jax.shard_map(body, mesh=mesh, in_specs=in_specs, out_specs=out_specs, check_vma=False)
```

time: 1780 us -> 538 us (0.30)
  waiting for transfers between devices: 1350 us -> 0 us
  Pallas kernels: 0 us -> 515 us
  matrix products: 171 us -> 0 us
  other arithmetic: 109 us -> 4.02 us
  blocking collectives: 88 us -> 0 us
    reduce_scatter x18 -> x0, waiting for transfers between devices: 577 us -> none  [the longest x2 271 us: layer_backward(): lax.psum_scatter(grad_values_all.reshape(seq_count, length, KV_HEADS * HE...]
    psum x1 -> x0, waiting for transfers between devices: 574 us -> none  [body(): lax.psum((shares[0], shares[1], shares[2], shares[3], shares[4], shares[5...]
    pallas_call x0 -> x19, Pallas kernels: none -> 515 us  [the longest x13 198 us: call(): pl.pallas_call(kernel, out_shape=[jax.ShapeDtypeStruct(s, t) for s, t in...]
    all_gather x10 -> x0, waiting for transfers between devices: 191 us -> none  [the longest x2 116 us: layer_forward(): lax.all_gather(keys_own, 'ctx', axis=1, tiled=True)]
    dot_general x70 -> x0, matrix products: 171 us -> none  [the longest x4 23.3 us: attend_back(): jnp.einsum('qhge,khe->hgqk', grad_mixed, values_all, preferred_element_ty...]
    all_gather x9 -> x0, blocking collectives: 49.6 us -> none  [the longest x1 30.2 us: body(): places = lax.all_gather(positions, 'ctx', axis=1, tiled=True)]
    another operation x28 -> x0, other arithmetic: 45.8 us -> none  [the longest x20 41.6 us: body(): jnp.stack([entry_totals[member] for entry_totals in collected])]
    convert_element_type x14 -> x3, other arithmetic: 45.6 us -> 2.5 us  [the longest x1 1.12 us: body(): output = x.reshape(seqs, r, d).astype(BF16)]
  transfers between devices with their start and end apart: 29 -> 0, of which waited for: 18 -> 0; matrix products, arithmetic and copies ran while one was open for 12% -> 0% of each run, Pallas kernels for 0% -> 0%
where the time goes in v2:
time: 538 us; the launch traced here: 537 us
  Pallas kernels  515 us (96%)
  local copies, waits for them, and re-layouts  17 us (3%)
    pallas_call x13, Pallas kernels, call(): pl.pallas_call(kernel, out_shape=[jax.ShapeDtypeStruct(s, t) for s, t in...  198 us
    pallas_call x1, Pallas kernels, reduce_all(): pl.pallas_call(functools.partial(reduce_all_kernel, g), out_shape=jax.Sha...  164 us
    pallas_call x2, Pallas kernels, reduce_scatter_ctx(): pl.pallas_call(functools.partial(scatter_kernel, g), out_shape=jax.ShapeD...  83.7 us
    pallas_call x2, Pallas kernels, all_gather_ctx(): pl.pallas_call(functools.partial(gather_kernel, g, count, spots), out_sha...  66.2 us
    unnamed x8, local copies, waits for them, and re-layouts  14.3 us

profile of v2, /device:TPU:10, one launch (start us, length us, event | category | flops | bytes accessed | tf_op | source)
XLA Modules:
  0.0 536.8 jit_solution(16755157402362173348)
XLA Ops:
  1.3 1.9 copy.32
  3.2 1.9 copy.35
  6.6 2.6 exchange.1
  12.7 3.1 pre.2
  15.8 2.2 copy.34.refs_5_
  18.0 35.4 %ctx_gather.2 = (bf16[16,256,384]{2,1,0:T(8,128)(2,1)}, s32[16,2,128]{2,1,0:T(2,128)}, bf16[2,288,576]{2,1,0:T(8,128)(2,1)}, bf16[2,288,1536]{2,1,0:T(8,128)(2,1...) custom-call(bf16[256,384]{1,0:T(8,128)(2,1)} %get-tuple-element.76.r, ...), custom_call_target="tpu_custom_call" | custom-call | tf_op jit(solution)/shard_map/ctx_gather/pallas_call | solution.py:519
  53.5 28.2 %attend.2 = (f32[2,128,576]{2,1,0:T(8,128)}, f32[2,6,1,192]{3,2,1,0:T(1,128)}) custom-call(s32[16,2,128]{2,1,0:T(2,128)} %get-tuple-element.77.block_ref, s32[2,128]{1,0:T(2,128)} %mine_ref.7, bf16[2,128,576]{2,1,0:T(8,128)(2,1)} %bitcast.73, bf16[16,2,128,384]{3,2,1,0:T(8,128)(2,1)} %bitcast.42), custom_call_target="tpu_custom_call" | custom-call | tf_op jit(solution)/shard_map/attend/pallas_call | solution.py:621
  81.7 9.1 %post.2 = (f32[256,576]{1,0:T(8,128)}, bf16[256,576]{1,0:T(8,128)(2,1)}, f32[256,1536]{1,0:T(8,128)}, f32[256,1536]{1,0:T(8,128)}, f32[256,576]{1,0:T(8,128)}) custom-call(f32[256,576]{1,0:T(8,128)} %bitcast.56, bf16[256,576]{1,0:T(8,128)(2,1)} %bitcast.61, bf16[576,576]{1,0:T(8,128)(2,1)} %bitcast.71, f32[1,576]{1,0:T(1,128)} %squeeze.17.gain_ref.refs_6_, ...), custom_call_target="tpu_custom_call" | custom-call | tf_op jit(solution)/shard_map/post/pallas_call | solution.py:621
  90.8 3.2 pre.3
  94.0 30.7 %ctx_gather.3 = bf16[16,256,384]{2,1,0:T(8,128)(2,1)} custom-call(bf16[256,384]{1,0:T(8,128)(2,1)} %get-tuple-element.91.refs_0_), custom_call_target="tpu_custom_call" | custom-call | tf_op jit(solution)/shard_map/ctx_gather/pallas_call | solution.py:519
  124.7 28.2 %attend.3 = (f32[2,128,576]{2,1,0:T(8,128)}, f32[2,6,1,192]{3,2,1,0:T(1,128)}) custom-call(s32[16,2,128]{2,1,0:T(2,128)} %get-tuple-element.77.block_ref, s32[2,128]{1,0:T(2,128)} %mine_ref.7, bf16[2,128,576]{2,1,0:T(8,128)(2,1)} %bitcast.75, bf16[16,2,128,384]{3,2,1,0:T(8,128)(2,1)} %bitcast.40), custom_call_target="tpu_custom_call" | custom-call | tf_op jit(solution)/shard_map/attend/pallas_call | solution.py:621
  152.9 9.2 %post.3 = (f32[256,576]{1,0:T(8,128)}, bf16[256,576]{1,0:T(8,128)(2,1)}, f32[256,1536]{1,0:T(8,128)}, f32[256,1536]{1,0:T(8,128)}, f32[256,576]{1,0:T(8,128)}) custom-call(f32[256,576]{1,0:T(8,128)} %bitcast.58, f32[256,576]{1,0:T(8,128)} %get-tuple-element.86.x_ref.refs_3_, bf16[576,576]{1,0:T(8,128)(2,1)} %bitcast.69, f32[1,576]{1,0:T(1,128)} %squeeze.19.gain_ref.refs_6_, ...), custom_call_target="tpu_custom_call" | custom-call | tf_op jit(solution)/shard_map/post/pallas_call | solution.py:621
  164.1 14.5 %ffn_back.2 = (f32[256,576]{1,0:T(8,128)}, bf16[256,576]{1,0:T(8,128)(2,1)}, bf16[2,1856,16,128]{3,2,1,0:T(8,128)(2,1)}) custom-call(bf16[256,576]{1,0:T(8,128)(2,1)} %bitcast.77, f32[256,576]{1,0:T(8,128)} %get-tuple-element.98.refs_1_, bf16[256,576]{1,0:T(8,128)(2,1)} %get-tuple-element.99.refs_2_, f32[256,1536]{1,0:T(8,128)} %get-tuple-element.100.refs_3_, ...), custom_call_target="tpu_custom_call" | custom-call | tf_op jit(solution)/shard_map/ffn_back/pallas_call | solution.py:611
  178.6 33.9 %attend_back.2 = (f32[2,128,576]{2,1,0:T(8,128)}, bf16[16,2,128,384]{3,2,1,0:T(8,128)(2,1)}) custom-call(s32[16,2,128]{2,1,0:T(2,128)} %get-tuple-element.77.block_ref, s32[2,128]{1,0:T(2,128)} %mine_ref.7, bf16[2,128,576]{2,1,0:T(8,128)(2,1)} %bitcast.76, bf16[16,2,128,384]{3,2,1,0:T(8,128)(2,1)} %bitcast.41, bf16[2,128,576]{2,1,0:T(8,128)(2,1)} %bitcast.91, ...), custom_call_target="tpu_custom_call" | custom-call | tf_op jit(solution)/shard_map/attend_back/pallas_call | solution.py:621
  212.6 45.9 %ctx_reduce.2.refs_1_ = f32[256,384]{1,0:T(8,128)} custom-call(bf16[16,256,384]{2,1,0:T(8,128)(2,1)} %bitcast.64), custom_call_target="tpu_custom_call" | custom-call | tf_op jit(solution)/shard_map/ctx_reduce/pallas_call | solution.py:326
  258.5 5.6 %pre_back.2 = (f32[256,576]{1,0:T(8,128)}, bf16[2,1856,16,128]{3,2,1,0:T(8,128)(2,1)}) custom-call(f32[256,576]{1,0:T(8,128)} %bitcast.88, f32[256,384]{1,0:T(8,128)} %ctx_reduce.2.refs_1_, bf16[256,576]{1,0:T(8,128)(2,1)} %get-tuple-element.106.refs_2_, f32[256,576]{1,0:T(8,128)} %get-tuple-element.86.x_ref.refs_3_, ...), custom_call_target="tpu_custom_call", output_to_operand_aliasing={{1}: (11, {})} | custom-call | tf_op jit(solution)/shard_map/pre_back/pallas_call | solution.py:611
  264.0 14.8 %ffn_back.3 = (f32[256,576]{1,0:T(8,128)}, bf16[256,576]{1,0:T(8,128)(2,1)}, bf16[2,1856,16,128]{3,2,1,0:T(8,128)(2,1)}) custom-call(f32[256,576]{1,0:T(8,128)} %get-tuple-element.109.refs_0_, f32[256,576]{1,0:T(8,128)} %get-tuple-element.110.refs_1_, bf16[256,576]{1,0:T(8,128)(2,1)} %get-tuple-element.111.refs_2_, ...), custom_call_target="tpu_custom_call", output_to_operand_aliasing={{2}: (11, {})} | custom-call | tf_op jit(solution)/shard_map/ffn_back/pallas_call | solution.py:611
  278.9 33.8 %attend_back.3 = (f32[2,128,576]{2,1,0:T(8,128)}, bf16[16,2,128,384]{3,2,1,0:T(8,128)(2,1)}) custom-call(s32[16,2,128]{2,1,0:T(2,128)} %get-tuple-element.77.block_ref, s32[2,128]{1,0:T(2,128)} %mine_ref.7, bf16[2,128,576]{2,1,0:T(8,128)(2,1)} %bitcast.74, bf16[16,2,128,384]{3,2,1,0:T(8,128)(2,1)} %bitcast.43, bf16[2,128,576]{2,1,0:T(8,128)(2,1)} %bitcast.90, ...), custom_call_target="tpu_custom_call" | custom-call | tf_op jit(solution)/shard_map/attend_back/pallas_call | solution.py:621
  312.6 37.8 %ctx_reduce.3.refs_1_ = f32[256,384]{1,0:T(8,128)} custom-call(bf16[16,256,384]{2,1,0:T(8,128)(2,1)} %bitcast.63), custom_call_target="tpu_custom_call" | custom-call | tf_op jit(solution)/shard_map/ctx_reduce/pallas_call | solution.py:326
  350.5 5.6 %pre_back.3 = (f32[256,576]{1,0:T(8,128)}, bf16[2,1856,16,128]{3,2,1,0:T(8,128)(2,1)}) custom-call(f32[256,576]{1,0:T(8,128)} %bitcast.87, f32[256,384]{1,0:T(8,128)} %ctx_reduce.3.refs_1_, bf16[256,576]{1,0:T(8,128)(2,1)} %get-tuple-element.119.refs_2_, bf16[256,576]{1,0:T(8,128)(2,1)} %bitcast.62, ...), custom_call_target="tpu_custom_call", output_to_operand_aliasing={{1}: (11, {})} | custom-call | tf_op jit(solution)/shard_map/pre_back/pallas_call | solution.py:611
  356.1 2.1 copy.37
  358.2 164.4 %grad_reduce.1 = bf16[2,16,928,128]{3,2,1,0:T(8,128)(2,1)} custom-call(bf16[2,2,16,928,128]{4,3,2,1,0:T(8,128)(2,1)} %bitcast.38), custom_call_target="tpu_custom_call" | custom-call | tf_op jit(solution)/shard_map/grad_reduce/pallas_call | solution.py:408
  522.7 8.8 %unpack.1 = (f32[2,288]{1,0:T(2,128)}, f32[2,288,576]{2,1,0:T(8,128)}, f32[2,288,192]{2,1,0:T(8,128)}, f32[2,288,192]{2,1,0:T(8,128)}, f32[2,288,576]{2,1,0:T(8,...) custom-call(bf16[1856,16,128]{2,1,0:T(8,128)(2,1)} %bitcast.39), custom_call_target="tpu_custom_call" | custom-call | tf_op jit(solution)/shard_map/unpack/pallas_call | solution.py:621
  531.5 5.3 copy.38
  (15 shorter events, 7.6 us)
Async XLA Ops:
  5.6 10.2 %copy-start = (bf16[2,768,576]{1,2,0:T(8,128)(2,1)S(1)}, bf16[2,768,576]{1,2,0:T(8,128)(2,1)}, u32[]{:S(2)}) copy-start(bf16[2,768,576]{1,2,0:T(8,128)(2,1)} %param.22) | copy-start | bytes 5308420

commit v3 on v2

--- a/solution.py
+++ b/solution.py
@@ -1,4 +1,7 @@
-import functools, itertools
+import functools
+import itertools
+import math
+
 import jax
 import jax.numpy as jnp
 from jax import lax
@@ -8,7 +11,7 @@
 
 CTX, FSDP = "ctx", "fsdp"
 MESH = pl.DeviceIdType.MESH
-PARTS = 2
+SHARES = ((0, 6), (1, 6), (2, 2), (3, 2))
 
 
 def factors(n):
@@ -194,20 +197,39 @@
         ref = self.own if self.stage == 0 else self.acc
         return ref(self.g.index(delta))
 
-    def ship(self, src, label, axis, step, way, at_label):
-        g = self.g
+    @staticmethod
+    def room(g, order):
+        starts, total = [], 0
+        for stage, a in enumerate(order):
+            live = math.prod(g.dims[b] for b in order[stage:])
+            starts.append(total)
+            total += live // 2 if g.dims[a] == 2 else 2 * live
+        return starts, total
+
+    def spot(self, stage, way, label):
+        g, a = self.g, self.order[stage]
+        axes = self.order[stage + 1 :] if g.dims[a] == 2 else self.order[stage:]
+        rank, live = 0, 1
+        for b in axes:
+            rank = rank + label[b] * live
+            live *= g.dims[b]
+        return self.room(g, self.order)[0][stage] + way * live + rank
+
+    def ship(self, src, label, stage, step, way, at_label):
+        g, axis = self.g, self.order[stage]
+        spot = self.spot(stage, way, at_label)
         copy = pltpu.make_async_remote_copy(
-            src_ref=src, dst_ref=self.land.at[way, g.slot(at_label)], send_sem=self.send.at[g.slot(label)],
-            recv_sem=self.recv.at[way, g.slot(at_label)],
+            src_ref=src, dst_ref=self.land.at[spot], send_sem=self.send.at[g.slot(label)], recv_sem=self.recv.at[spot],
             device_id=(g.peer(axis, step), lax.axis_index(FSDP)), device_id_type=MESH)
         copy.start()
         self.sent.append(copy)
 
-    def landed(self, way, label):
+    def landed(self, stage, way, label):
         g = self.g
-        ref = self.land.at[way, g.slot(label)]
+        spot = self.spot(stage, way, label)
+        ref = self.land.at[spot]
         pltpu.make_async_remote_copy(
-            src_ref=ref, dst_ref=ref, send_sem=self.send.at[0], recv_sem=self.recv.at[way, g.slot(label)],
+            src_ref=ref, dst_ref=ref, send_sem=self.send.at[0], recv_sem=self.recv.at[spot],
             device_id=(g.peer(self.order[0], 1), lax.axis_index(FSDP)), device_id_type=MESH).wait_recv()
         return ref
 
@@ -224,7 +246,7 @@
         out = []
         if n == 2:
             if stage == 0:
-                out += [functools.partial(self.swap, put(1, d, a), a) for d in keep]
+                out += [functools.partial(self.swap, put(1, d, a)) for d in keep]
             out += [functools.partial(self.take, d, stage) for d in keep]
         else:
             if stage == 0:
@@ -242,20 +264,20 @@
             add_into(self.acc(i), [self.own(i)])
         self.stage = 1
 
-    def swap(self, d, axis):
-        self.ship(self.held(d), d, axis, 1, 0, put(1, d, axis))
+    def swap(self, d):
+        self.ship(self.held(d), d, 0, 1, 0, d)
 
     def next_ship(self, d, stage):
         if stage + 1 < len(self.order):
             a = self.order[stage + 1]
             if self.g.dims[a] == 2 and d[a]:
-                self.ship(self.acc(self.g.index(d)), d, a, 1, 0, d)
+                self.ship(self.acc(self.g.index(d)), d, stage + 1, 1, 0, d)
 
     def take(self, d, stage):
         a = self.order[stage]
         i = self.g.index(d)
         ref = self.own(i) if stage == 0 and self.stage == 0 else self.acc(i)
-        add_into(self.acc(i), [ref, self.landed(0, put(1, d, a))])
+        add_into(self.acc(i), [ref, self.landed(stage, 0, put(1, d, a))])
         self.next_ship(d, stage)
 
     def pass_on(self, d, stage):
@@ -268,9 +290,9 @@
 
         @pl.when(jnp.where(up, c > 0, c < n - 1))
         def _():
-            add_into(kept, [kept, self.landed(way, d)])
-
-        self.ship(kept, d, a, jnp.where(up, 1, n - 1), way, put(jnp.where(up, k - 1, lax.rem(k + 1, n)), d, a))
+            add_into(kept, [kept, self.landed(stage, way, d)])
+
+        self.ship(kept, d, stage, jnp.where(up, 1, n - 1), way, put(jnp.where(up, k - 1, lax.rem(k + 1, n)), d, a))
 
     def close(self, d, stage):
         g, a = self.g, self.order[stage]
@@ -279,11 +301,11 @@
 
         @pl.when(c > 0)
         def _():
-            add_into(kept, [kept, self.landed(0, d)])
+            add_into(kept, [kept, self.landed(stage, 0, d)])
 
         @pl.when(c < n - 1)
         def _():
-            add_into(kept, [kept, self.landed(1, d)])
+            add_into(kept, [kept, self.landed(stage, 1, d)])
 
         self.next_ship(d, stage)
 
@@ -322,6 +344,7 @@
 def reduce_scatter_ctx(x, n, cid):
     g = Grid(n)
     _, rows, cols = x.shape
+    room = max(Reduce.room(g, o[::-1])[1] for o in g.orders())
     dma = pltpu.SemaphoreType.DMA
     return pl.pallas_call(
         functools.partial(scatter_kernel, g),
@@ -330,66 +353,74 @@
         out_specs=pl.BlockSpec(memory_space=pltpu.VMEM),
         scratch_shapes=[
             pltpu.VMEM((n, rows, cols), x.dtype),
-            pltpu.VMEM((2, 2, n, rows // 2, cols), x.dtype),
+            pltpu.VMEM((2, room, rows // 2, cols), x.dtype),
             dma((2, n)),
-            dma((2, 2, n)),
+            dma((2, room)),
         ],
         compiler_params=pltpu.CompilerParams(collective_id=cid, has_side_effects=True, vmem_limit_bytes=60 << 20),
         name="ctx_reduce",
     )(x)
 
 
-def reduce_all_kernel(g, x_ref, o_ref, own, kept, land, send, recv, gsend, grecv, psend, precv, lsem):
+def row_cuts(rows, shares):
+    tiles, total, seen, out = rows // 16, sum(shares), 0, []
+    for s in shares:
+        start = tiles * seen // total
+        seen += s
+        out.append((start * 16, (tiles * seen // total - start) * 16))
+    return out
+
+
+def reduce_parts(g, rows):
+    rest = list(range(1, len(g.dims)))
+    orders = [[0] + rest, [0] + rest[::-1], rest + [0], rest[::-1] + [0]]
+    return [(*cut, orders[k]) for cut, (k, _) in zip(row_cuts(rows, [s for _, s in SHARES]), SHARES) if cut[1]]
+
+
+def reduce_all_kernel(g, x_ref, o_ref, own, kept, send, recv, gsend, grecv, psend, precv, lsem, *lands):
     g.locate()
     entry_barrier(g, True)
     f = lax.axis_index(FSDP)
-    parts = x_ref.shape[1]
-    orders = g.orders()
-    rs, gs, local = [], [], []
-    for p in range(parts):
-        order = orders[p % 2]
-        at = (lambda p: lambda i: kept.at[p, i])(p)
-        rs.append(Reduce(g, order[::-1], at, at, land.at[p], send.at[p], recv.at[p]))
-        gs.append(Gather(g, order, o_ref.at[p, g.me], (lambda p: lambda i: o_ref.at[p, i])(p), gsend.at[p], grecv.at[p]))
-        c = pltpu.make_async_copy(x_ref.at[f, p], own.at[p], lsem.at[p])
-        c.start()
-        local.append(c)
-    turns = [sorted(g.all, key=lambda d, a=r.order[0], r=r: (d[a] == 0, -sum(1 for v in d if v))) for r in rs]
+    cuts = reduce_parts(g, x_ref.shape[2])
+    rs, gs = [], []
+    for p, (r0, rn, order) in enumerate(cuts):
+        at = (lambda r: lambda i: kept.at[i, r])(pl.ds(r0, rn))
+        to = (lambda r: lambda i: o_ref.at[i, r])(pl.ds(r0, rn))
+        rs.append(Reduce(g, order[::-1], at, at, lands[p], send.at[p], recv.at[p]))
+        gs.append(Gather(g, order, to(g.me), to, gsend.at[p], grecv.at[p]))
+    local = pltpu.make_async_copy(x_ref.at[f], own, lsem)
+    local.start()
+    turns = [sorted(g.all, key=lambda d, a=r.order[0]: (d[a] == 0, -sum(1 for v in d if v))) for r in rs]
     pairs = {}
     for i in range(g.n):
-        for p in range(parts):
+        for p, (r0, rn, _) in enumerate(cuts):
             d = turns[p][i]
             k = g.index(d)
+            at = pl.ds(r0, rn)
             c = pltpu.make_async_remote_copy(
-                src_ref=x_ref.at[1 - f, p, k], dst_ref=kept.at[p, k], send_sem=psend.at[p, g.slot(d)],
+                src_ref=x_ref.at[1 - f, k, at], dst_ref=kept.at[k, at], send_sem=psend.at[p, g.slot(d)],
                 recv_sem=precv.at[p, g.slot(d)], device_id=(g.me, 1 - f), device_id_type=MESH)
             c.start()
             pairs[p, d] = c
-    for c in local:
-        c.wait()
-    first = [r.steps(0) for r in rs]
+    local.wait()
     for i in range(g.n):
         for p, r in enumerate(rs):
             d = turns[p][i]
             k = g.index(d)
             pairs[p, d].wait_recv()
-            add_into(kept.at[p, k], [kept.at[p, k], own.at[p, k]])
+            add_into(r.acc(k), [r.acc(k), own.at[k, pl.ds(cuts[p][0], cuts[p][1])]])
             a = r.order[0]
             if g.dims[a] == 2 and d[a]:
-                r.swap(d, a)
+                r.swap(d)
+    first = [[s for s in r.steps(0) if getattr(s, "func", s).__name__ in ("take", "pass_on", "close")] for r in rs]
     for r in rs:
         r.stage = 1
     for stage in range(len(g.dims)):
-        lists = []
-        for r, steps in zip(rs, first):
-            if stage == 0:
-                lists.append([s for s in steps if getattr(s, "func", s).__name__ in ("take", "pass_on", "close")])
-            else:
-                lists.append(r.steps(stage))
+        lists = first if stage == 0 else [r.steps(stage) for r in rs]
         for step in interleave(lists):
             step()
-    for p, q in enumerate(gs):
-        add_into(o_ref.at[p, g.me], [kept.at[p, g.me]])
+    for r, q in zip(rs, gs):
+        add_into(q.own, [r.acc(g.me)])
         q.begin()
     run_gathers(g, gs)
     for c in pairs.values():
@@ -402,26 +433,28 @@
 
 def reduce_all(x, n, cid):
     g = Grid(n)
-    _, parts, _, rows, cols = x.shape
-    blk = (parts, n, rows, cols)
+    _, _, rows, cols = x.shape
+    cuts = reduce_parts(g, rows)
+    parts = len(cuts)
+    rooms = [Reduce.room(g, order[::-1])[1] for _, _, order in cuts]
     dma = pltpu.SemaphoreType.DMA
     return pl.pallas_call(
         functools.partial(reduce_all_kernel, g),
-        out_shape=jax.ShapeDtypeStruct(blk, x.dtype),
+        out_shape=jax.ShapeDtypeStruct((n, rows, cols), x.dtype),
         in_specs=[pl.BlockSpec(memory_space=pl.ANY)],
         out_specs=pl.BlockSpec(memory_space=pltpu.VMEM),
         scratch_shapes=[
-            pltpu.VMEM(blk, x.dtype),
-            pltpu.VMEM(blk, x.dtype),
-            pltpu.VMEM((parts, 2, n, rows, cols), x.dtype),
+            pltpu.VMEM((n, rows, cols), x.dtype),
+            pltpu.VMEM((n, rows, cols), x.dtype),
             dma((parts, n)),
-            dma((parts, 2, n)),
+            dma((parts, max(rooms))),
             dma((parts, 2, n)),
             dma((parts, n)),
             dma((parts, n)),
             dma((parts, n)),
-            dma((parts,)),
-        ],
+            dma(()),
+        ]
+        + [pltpu.VMEM((room, rn, cols), x.dtype) for room, (_, rn, _) in zip(rooms, cuts)],
         compiler_params=pltpu.CompilerParams(collective_id=cid, has_side_effects=True, vmem_limit_bytes=64 << 20),
         name="grad_reduce",
     )(x)
@@ -629,8 +662,27 @@
     )(*args)
 
 
-def pre_kernel(x_ref, gain_ref, wq_ref, wk_ref, wv_ref, cos_ref, sin_ref, a_ref, q_ref, kv_ref):
-    a = rms(x_ref[...].astype(F32), gain_ref[...]).astype(BF16)
+def gain_of(ref, l):
+    return jnp.concatenate([ref[0, l : l + 1].astype(F32), ref[1, l : l + 1].astype(F32)], axis=1)
+
+
+def rows_of(ref):
+    return jnp.concatenate([ref[s].astype(F32).T for s in range(ref.shape[0])], axis=0)
+
+
+def put_turned(ref, value):
+    r = ref.shape[2]
+    for s in range(ref.shape[0]):
+        ref[s] = value[s * r : (s + 1) * r].T.astype(ref.dtype)
+
+
+def pre_kernel(l, x_ref, gain_ref, wq_ref, wk_ref, wv_ref, cos_ref, sin_ref, a_ref, q_ref, kv_ref, *turned):
+    if turned:
+        x = rows_of(x_ref)
+        turned[0][...] = x
+    else:
+        x = x_ref[...]
+    a = rms(x, gain_of(gain_ref, l)).astype(BF16)
     a_ref[...] = a
     cos, sin = cos_ref[...], sin_ref[...]
     for lo, w, piece in rope(nn(a, wq_ref[...]), cos, sin):
@@ -639,10 +691,10 @@
     kv_ref[...] = jnp.concatenate([keys, nn(a, wv_ref[...])], axis=1).astype(BF16)
 
 
-def pre(x, gain, wq, wk, wv, cos, sin):
-    m, d = x.shape
-    e = wk.shape[1]
-    return call(pre_kernel, [((m, d), BF16), ((m, d), BF16), ((m, 2 * e), BF16)], (x, gain, wq, wk, wv, cos, sin), "pre")
+def pre(l, x, gain, wq, wk, wv, cos, sin):
+    m, d, e = cos.shape[0], wq.shape[0], wk.shape[1]
+    outs = [((m, d), BF16), ((m, d), BF16), ((m, 2 * e), BF16)] + ([((m, d), F32)] if x.ndim == 3 else [])
+    return call(functools.partial(pre_kernel, l), outs, (x, gain, wq, wk, wv, cos, sin), "pre")
 
 
 def half_of(u, src, dst):
@@ -694,45 +746,68 @@
     return ((KV_HEADS + g) // 2) * 128, (KV_HEADS + g) % 2
 
 
-def attend_kernel(n, block_ref, mine_ref, q_ref, kv_ref, o_ref, lse_ref, sorted_ref, qp_ref, st_ref):
+def turn_rows(src, lo, dst, count):
+    def one(c, carry):
+        at = pl.ds(pl.multiple_of(c * CHUNK, CHUNK), CHUNK)
+        dst[:, at] = src[at, lo : lo + 256].astype(F32).T.astype(BF16)
+        return carry
+
+    lax.fori_loop(0, count, one, 0)
+
+
+def attend_kernel(
+    n, block_ref, mine_ref, q_ref, kv_ref, o_ref, lse_ref, sorted_ref, turned_ref, qp_ref, st_ref, acc_ref, stat_ref
+):
     rows = q_ref.shape[1] // 2
     wide = GROUP * rows
+    groups = range(KV_HEADS)
+    vlo = HEAD * KV_HEADS // 128 * 128
+    voff = HEAD * KV_HEADS - vlo
 
     def sequence(s, carry):
         sort_rows(block_ref, s, kv_ref, sorted_ref, n, rows)
-        for g in range(KV_HEADS):
+        turn_rows(sorted_ref, vlo, turned_ref, n * 2 * rows // CHUNK)
+        for g in groups:
             pack_heads(q_ref, s, qp_ref, g, key_lanes(g)[1], HEAD**-0.5)
         low = mine_ref[s, 0] // rows
-        for g in range(KV_HEADS):
-            klo, _ = key_lanes(g)
-            vlo, vhalf = value_lanes(g)
-            for part in range(2):
-                block = low if part == 0 else 2 * n - 1 - low
-                last = block * rows // CHUNK
-                qp = qp_ref[g * 2 + part]
-
-                def score(c, top, masked):
-                    at = pl.ds(pl.multiple_of(c * CHUNK, CHUNK), CHUNK)
-                    st = nt(sorted_ref[at, klo : klo + 128], qp)
+        for part in range(2):
+            block = low if part == 0 else 2 * n - 1 - low
+            last = block * rows // CHUNK
+            stat_ref[...] = jnp.full_like(stat_ref, -1e30)
+
+            def score(c, masked):
+                at = pl.ds(pl.multiple_of(c * CHUNK, CHUNK), CHUNK)
+                for g in groups:
+                    klo, _ = key_lanes(g)
+                    st = nt(sorted_ref[at, klo : klo + 128], qp_ref[g * 2 + part])
                     if masked:
                         st = jnp.where(visible(c, block, rows, st.shape), st, -1e30)
-                    st_ref[at, :] = st
-                    return jnp.maximum(top, jnp.max(st.reshape(CHUNK // 8, 8, wide), axis=0))
-
-                top = lax.fori_loop(0, last, lambda c, t: score(c, t, False), jnp.full((8, wide), -1e30, F32))
-                top = jnp.max(score(last, top, True), axis=0, keepdims=True)
-
-                def mix(c, state):
-                    total, acc = state
-                    at = pl.ds(pl.multiple_of(c * CHUNK, CHUNK), CHUNK)
-                    p = jnp.exp(st_ref[at, :] - top)
-                    total = total + jnp.sum(p.reshape(CHUNK // 8, 8, wide), axis=0)
-                    return total, acc + tn(sorted_ref[at, vlo : vlo + 128], p.astype(BF16))
-
-                total, acc = lax.fori_loop(0, last + 1, mix, (jnp.zeros((8, wide), F32), jnp.zeros((128, wide), F32)))
-                total = jnp.sum(total, axis=0, keepdims=True)
-                lse_ref[s, g * 2 + part] = top + jnp.log(total)
-                out = (acc[vhalf * HEAD : (vhalf + 1) * HEAD] / total).T
+                    st_ref[g, at, :] = st
+                    stat_ref[g] = jnp.maximum(stat_ref[g], jnp.max(st.reshape(CHUNK // 8, 8, wide), axis=0))
+
+            def scores(c, carry):
+                score(c, False)
+                return carry
+
+            lax.fori_loop(0, last, scores, 0)
+            score(last, True)
+            tops = [jnp.max(stat_ref[g], axis=0, keepdims=True) for g in groups]
+            stat_ref[...] = jnp.zeros_like(stat_ref)
+            acc_ref[...] = jnp.zeros_like(acc_ref)
+
+            def mix(c, tops):
+                at = pl.ds(pl.multiple_of(c * CHUNK, CHUNK), CHUNK)
+                for g in groups:
+                    p = jnp.exp(st_ref[g, at, :] - tops[g])
+                    stat_ref[g] += jnp.sum(p.reshape(CHUNK // 8, 8, wide), axis=0)
+                    acc_ref[g] += nn(turned_ref[voff + g * HEAD : voff + (g + 1) * HEAD, at], p.astype(BF16))
+                return tops
+
+            tops = lax.fori_loop(0, last + 1, mix, tuple(tops))
+            for g in groups:
+                total = jnp.sum(stat_ref[g], axis=0, keepdims=True)
+                lse_ref[s, g * 2 + part] = tops[g] + jnp.log(total)
+                out = (acc_ref[g] / total).T
                 for i in range(GROUP):
                     h = g * GROUP + i
                     o_ref[s, part * rows : (part + 1) * rows, h * HEAD : (h + 1) * HEAD] = out[i * rows : (i + 1) * rows]
@@ -747,35 +822,37 @@
     wide = GROUP * r // 2
     scratch = [
         pltpu.VMEM((n * r, kv.shape[-1]), BF16),
+        pltpu.VMEM((256, n * r), BF16),
         pltpu.VMEM((2 * KV_HEADS, wide, 128), BF16),
-        pltpu.VMEM((n * r, wide), F32),
+        pltpu.VMEM((KV_HEADS, n * r, wide), F32),
+        pltpu.VMEM((KV_HEADS, HEAD, wide), F32),
+        pltpu.VMEM((KV_HEADS, 8, wide), F32),
     ]
     outs = [((seqs, r, d), F32), ((seqs, 2 * KV_HEADS, 1, wide), F32)]
     return call(functools.partial(attend_kernel, n), outs, (blocks, mine, q, kv), "attend", scratch, 2)
 
 
 def attend_back_kernel(
-    n, block_ref, mine_ref, q_ref, kv_ref, do_ref, o_ref, lse_ref, dq_ref, dkv_ref, sorted_ref, qp_ref, dop_ref, acc_ref, delta_ref
+    n, block_ref, mine_ref, q_ref, kv_ref, do_ref, o_ref, lse_ref, dq_ref, dkv_ref,
+    sorted_ref, turned_ref, qp_ref, dop_ref, acc_ref, delta_ref, dqt_ref,
 ):
     rows = q_ref.shape[1] // 2
     wide = GROUP * rows
+    groups = range(KV_HEADS)
 
     def sequence(s, carry):
         sort_rows(block_ref, s, kv_ref, sorted_ref, n, rows)
-        for g in range(KV_HEADS):
+        turn_rows(sorted_ref, 0, turned_ref, n * 2 * rows // CHUNK)
+        for g in groups:
             pack_heads(q_ref, s, qp_ref, g, key_lanes(g)[1], HEAD**-0.5)
             pack_heads(do_ref, s, dop_ref, g, value_lanes(g)[1], 1.0)
         acc_ref[...] = jnp.zeros_like(acc_ref)
         low = mine_ref[s, 0] // rows
-        for g in range(KV_HEADS):
-            klo, khalf = key_lanes(g)
-            vlo, vhalf = value_lanes(g)
-            pieces = []
-            for part in range(2):
-                block = low if part == 0 else 2 * n - 1 - low
-                last = block * rows // CHUNK
-                qp, dop = qp_ref[g * 2 + part], dop_ref[g * 2 + part]
-                lse = lse_ref[s, g * 2 + part]
+        for part in range(2):
+            block = low if part == 0 else 2 * n - 1 - low
+            last = block * rows // CHUNK
+            deltas = []
+            for g in groups:
                 sums = []
                 for i in range(GROUP):
                     h = g * GROUP + i
@@ -784,27 +861,35 @@
                     both = do_ref[s, at, lanes].astype(F32) * o_ref[s, at, lanes]
                     sums.append(jnp.sum(both, axis=1, keepdims=True))
                 delta_ref[...] = jnp.concatenate(sums, axis=0) + jnp.zeros((wide, 128), F32)
-                delta = delta_ref[...].T[0:1]
-
-                def step(c, dq, masked):
-                    at = pl.ds(pl.multiple_of(c * CHUNK, CHUNK), CHUNK)
-                    keys = sorted_ref[at, klo : klo + 128]
-                    p = jnp.exp(nt(keys, qp) - lse)
+                deltas.append(delta_ref[...].T[0:1])
+            dqt_ref[...] = jnp.zeros_like(dqt_ref)
+
+            def step(c, deltas, masked):
+                at = pl.ds(pl.multiple_of(c * CHUNK, CHUNK), CHUNK)
+                sums = [None] * (2 * KV_HEADS * HEAD // 128)
+                for g in groups:
+                    klo, _ = key_lanes(g)
+                    vlo, _ = value_lanes(g)
+                    qp, dop = qp_ref[g * 2 + part], dop_ref[g * 2 + part]
+                    p = jnp.exp(nt(sorted_ref[at, klo : klo + 128], qp) - lse_ref[s, g * 2 + part])
                     if masked:
                         p = jnp.where(visible(c, block, rows, p.shape), p, 0.0)
                     dp = nt(sorted_ref[at, vlo : vlo + 128], dop)
-                    ds = (p * (dp - delta)).astype(BF16)
-                    acc_ref[at, vlo : vlo + 128] += nn(p.astype(BF16), dop)
-                    acc_ref[at, klo : klo + 128] += nn(ds, qp)
-                    return dq + tn(ds, keys)
-
-                dq = lax.fori_loop(0, last, lambda c, t: step(c, t, False), jnp.zeros((wide, 128), F32))
-                dq = step(last, dq, True) * HEAD**-0.5
+                    ds = (p * (dp - deltas[g])).astype(BF16)
+                    for lo, v in ((vlo // 128, nn(p.astype(BF16), dop)), (klo // 128, nn(ds, qp))):
+                        sums[lo] = v if sums[lo] is None else sums[lo] + v
+                    dqt_ref[g] += nn(turned_ref[g * HEAD : (g + 1) * HEAD, at], ds)
+                for k, v in enumerate(sums):
+                    acc_ref[at, k * 128 : (k + 1) * 128] += v
+                return deltas
+
+            deltas = lax.fori_loop(0, last, lambda c, t: step(c, t, False), tuple(deltas))
+            step(last, deltas, True)
+            for g in groups:
+                dq = dqt_ref[g].T * HEAD**-0.5
                 for i in range(GROUP):
                     h = g * GROUP + i
-                    dq_ref[s, part * rows : (part + 1) * rows, h * HEAD : (h + 1) * HEAD] = dq[
-                        i * rows : (i + 1) * rows, khalf * HEAD : (khalf + 1) * HEAD
-                    ]
+                    dq_ref[s, part * rows : (part + 1) * rows, h * HEAD : (h + 1) * HEAD] = dq[i * rows : (i + 1) * rows]
 
         def one(j, carry):
             b = block_ref[j, s, 0] // rows
@@ -826,21 +911,30 @@
     wide = GROUP * r // 2
     scratch = [
         pltpu.VMEM((n * r, kv.shape[-1]), BF16),
+        pltpu.VMEM((256, n * r), BF16),
         pltpu.VMEM((2 * KV_HEADS, wide, 128), BF16),
         pltpu.VMEM((2 * KV_HEADS, wide, 128), BF16),
         pltpu.VMEM((n * r, kv.shape[-1]), F32),
         pltpu.VMEM((wide, 128), F32),
+        pltpu.VMEM((KV_HEADS, HEAD, wide), F32),
     ]
     outs = [((seqs, r, d), F32), (kv.shape, BF16)]
     args = (blocks, mine, q, kv, do, o, lse)
     return call(functools.partial(attend_back_kernel, n), outs, args, "attend_back", scratch, 2)
 
 
-def post_kernel(o_ref, x_ref, wo_ref, gain_ref, wg_ref, wu_ref, wd_ref, h_ref, b_ref, gate_ref, up_ref, y_ref):
-    h = x_ref[...].astype(F32) + nn(o_ref[...].astype(BF16), wo_ref[...])
+def down_at(wd_ref, i):
+    per = wd_ref.shape[2] // CHUNK
+    f = i // per
+    return f, pl.ds(pl.multiple_of((i - f * per) * CHUNK, CHUNK), CHUNK)
+
+
+def post_kernel(l, o_ref, x_ref, wo_ref, gain_ref, wg_ref, wu_ref, wd_ref, h_ref, b_ref, gate_ref, up_ref, y_ref, *turned):
+    sum_ref = turned[0] if turned else y_ref
+    h = x_ref[...] + nn(o_ref[...].astype(BF16), wo_ref[...])
     h_ref[...] = h
-    y_ref[...] = h
-    b_ref[...] = rms(h, gain_ref[...]).astype(BF16)
+    sum_ref[...] = h
+    b_ref[...] = rms(h, gain_of(gain_ref, l)).astype(BF16)
 
     def some(i, carry):
         at = pl.ds(pl.multiple_of(i * CHUNK, CHUNK), CHUNK)
@@ -848,17 +942,21 @@
         gate, up = nn(b, wg_ref[:, at]), nn(b, wu_ref[:, at])
         gate_ref[:, at], up_ref[:, at] = gate, up
         m = (gate * jax.nn.sigmoid(gate) * up).astype(BF16)
-        y_ref[...] += nn(m, wd_ref[at, :])
+        f, spot = down_at(wd_ref, i)
+        sum_ref[...] += nt(m, wd_ref[f, :, spot])
         return carry
 
     lax.fori_loop(0, wg_ref.shape[1] // CHUNK, some, 0)
-
-
-def post(o, x, wo, gain, wg, wu, wd):
+    if turned:
+        put_turned(y_ref, sum_ref[...])
+
+
+def post(l, o, x, wo, gain, wg, wu, wd, turned=None):
     m, d = x.shape
     ff = wg.shape[1]
-    outs = [((m, d), F32), ((m, d), BF16), ((m, ff), F32), ((m, ff), F32), ((m, d), F32)]
-    return call(post_kernel, outs, (o, x, wo, gain, wg, wu, wd), "post")
+    outs = [((m, d), F32), ((m, d), BF16), ((m, ff), F32), ((m, ff), F32), (turned, BF16) if turned else ((m, d), F32)]
+    scratch = [pltpu.VMEM((m, d), F32)] if turned else []
+    return call(functools.partial(post_kernel, l), outs, (o, x, wo, gain, wg, wu, wd), "post", scratch)
 
 
 def put_tiles(blob, base, value, count):
@@ -884,25 +982,27 @@
     return -(-cols // 128)
 
 
-def ffn_back_kernel(base, new, *refs):
+def ffn_back_kernel(l, base, new, *refs):
     dy_ref, h_ref, b_ref, gate_ref, up_ref, o_ref, gain_ref, wo_ref, wg_ref, wu_ref, wd_ref = refs[:11]
-    dh_ref, do_ref, out_ref, blob_ref, dyb_ref, db_ref, bt_ref, sem = refs[11 if new else 12 :]
+    dh_ref, do_ref, out_ref, blob_ref, dyb_ref, dyt_ref, db_ref, bt_ref, sem = refs[11 if new else 12 :]
     m, d = h_ref.shape
     ff = wg_ref.shape[1]
     half = d // 2 // 16
-    gate_at, up_at = 0, (ff // 128) * half
-    down_at = 2 * up_at
-    down_rows = ff // 2 // 16
-    out_at = down_at + wide_of(d) * down_rows
+    up_at = (ff // 128) * half
+    low_at = 2 * up_at
+    out_at = low_at + (ff // 256) * (d // 16)
     norm_at = out_at + wide_of(d) * half
-    dyb_ref[...] = dy_ref[...].astype(BF16)
+    dy = rows_of(dy_ref) if len(dy_ref.shape) == 3 else dy_ref[...]
+    dh_ref[...] = dy
+    dyb_ref[...] = dy.astype(BF16)
+    dyt_ref[...] = dyb_ref[...].T
     db_ref[...] = jnp.zeros_like(db_ref)
     bt_ref[...] = b_ref[...].T
 
     def some(i, carry):
         at = pl.ds(pl.multiple_of(i * CHUNK, CHUNK), CHUNK)
-        dyb = dyb_ref[...]
-        dm = nt(dyb, wd_ref[at, :])
+        f, spot = down_at(wd_ref, i)
+        dm = nn(dyb_ref[...], wd_ref[f, :, spot])
         gate, up = gate_ref[:, at], up_ref[:, at]
         sig = jax.nn.sigmoid(gate)
         silu = gate * sig
@@ -911,22 +1011,20 @@
         dup = (dm * silu).astype(BF16)
         db_ref[...] += nt(dgate, wg_ref[:, at]) + nt(dup, wu_ref[:, at])
         bt = bt_ref[...]
-        put_tiles(blob_ref, gate_at + i * (CHUNK // 128) * half, nn(bt, dgate).astype(BF16), CHUNK // 128)
+        put_tiles(blob_ref, i * (CHUNK // 128) * half, nn(bt, dgate).astype(BF16), CHUNK // 128)
         put_tiles(blob_ref, up_at + i * (CHUNK // 128) * half, nn(bt, dup).astype(BF16), CHUNK // 128)
-        gd = tn(mid, dyb).astype(BF16)
-        gd = jnp.concatenate([gd, jnp.zeros((CHUNK, wide_of(d) * 128 - d), BF16)], axis=1)
-        per = ff // 2 // CHUNK
-        f = i // per
-        for j in range(wide_of(d)):
-            start = down_at + j * down_rows + (i - f * per) * (CHUNK // 16)
-            blob_ref[f, pl.ds(start, CHUNK // 16)] = gd[:, j * 128 : (j + 1) * 128].reshape(CHUNK // 16, 16, 128)
+        gd = nn(dyt_ref[...], mid).astype(BF16)
+        per = wd_ref.shape[2] // CHUNK
+        for j in range(CHUNK // 128):
+            start = low_at + ((i - f * per) * (CHUNK // 128) + j) * (d // 16)
+            blob_ref[f, pl.ds(start, d // 16)] = gd[:, j * 128 : (j + 1) * 128].reshape(d // 16, 16, 128)
         return carry
 
     lax.fori_loop(0, ff // CHUNK, some, 0)
     first = pltpu.make_async_copy(blob_ref.at[:, pl.ds(0, out_at)], out_ref.at[:, pl.ds(base, out_at)], sem.at[0])
     first.start()
-    dv, dg = rms_back(h_ref[...], gain_ref[...], db_ref[...])
-    dh = dy_ref[...].astype(F32) + dv
+    dv, dg = rms_back(h_ref[...], gain_of(gain_ref, l), db_ref[...])
+    dh = dh_ref[...] + dv
     dh_ref[...] = dh
     dhb = dh.astype(BF16)
     do_ref[...] = nt(dhb, wo_ref[...]).astype(BF16)
@@ -942,29 +1040,30 @@
 
 
 def ffn_tiles(d, ff):
-    return 2 * (ff // 128) * (d // 32) + wide_of(d) * (ff // 32) + wide_of(d) * (d // 32) + 1
-
-
-def pre_tiles(d, e):
-    return wide_of(d) * (d // 32) + wide_of(2 * e) * (d // 32) + 1
-
-
-def ffn_back(blob, base, dy, h, b, gate, up, o, gain, wo, wg, wu, wd):
+    return 2 * (ff // 128) * (d // 32) + (ff // 256) * (d // 16) + wide_of(d) * (d // 32) + 1
+
+
+def ffn_back(l, blob, base, dy, h, b, gate, up, o, gain, wo, wg, wu, wd):
     m, d = h.shape
     ff = wg.shape[1]
     scratch = [
         pltpu.VMEM((2, ffn_tiles(d, ff), 16, 128), BF16),
         pltpu.VMEM((m, d), BF16),
+        pltpu.VMEM((d, m), BF16),
         pltpu.VMEM((m, d), F32),
         pltpu.VMEM((d, m), BF16),
         pltpu.SemaphoreType.DMA((2,)),
     ]
-    kernel = functools.partial(ffn_back_kernel, base, isinstance(blob, tuple))
+    kernel = functools.partial(ffn_back_kernel, l, base, isinstance(blob, tuple))
     args = (dy, h, b, gate, up, o, gain, wo, wg, wu, wd)
     return call(kernel, [((m, d), F32), ((m, d), BF16)], args, "ffn_back", scratch, blob=blob)
 
 
-def pre_back_kernel(base, *refs):
+def pre_tiles(d, e):
+    return wide_of(d) * (d // 32) + wide_of(2 * e) * (d // 32) + 1
+
+
+def pre_back_kernel(l, base, *refs):
     dq_ref, dkv_ref, a_ref, x_ref, dh_ref, gain_ref, wq_ref, wk_ref, wv_ref, cos_ref, sin_ref = refs[:11]
     dx_ref, out_ref, blob_ref, dqp_ref, sem = refs[12:]
     d = x_ref.shape[1]
@@ -978,7 +1077,7 @@
     dkp = jnp.concatenate([piece for _, _, piece in rope(dkv[:, :e], cos, sin)], axis=1).astype(BF16)
     dvr = dkv[:, e:].astype(BF16)
     da = nt(dqp, wq_ref[...]) + nt(dkp, wk_ref[...]) + nt(dvr, wv_ref[...])
-    dv, dg = rms_back(x_ref[...].astype(F32), gain_ref[...], da)
+    dv, dg = rms_back(x_ref[...], gain_of(gain_ref, l), da)
     kv_at = wide_of(d) * half
     norm_at = kv_at + wide_of(2 * e) * half
     put_norm(blob_ref, norm_at, dg)
@@ -990,15 +1089,18 @@
     put_tiles(blob_ref, kv_at, jnp.concatenate([nn(at, dkp), nn(at, dvr)], axis=1).astype(BF16), wide_of(2 * e))
     done = pltpu.make_async_copy(blob_ref, out_ref.at[:, pl.ds(base, blob_ref.shape[1])], sem)
     done.start()
-    dx_ref[...] = dh_ref[...] + dv
+    if len(dx_ref.shape) == 3:
+        put_turned(dx_ref, dh_ref[...] + dv)
+    else:
+        dx_ref[...] = dh_ref[...] + dv
     done.wait()
 
 
-def pre_back(blob, base, tiles, dq, dkv, a, x, dh, gain, wq, wk, wv, cos, sin):
+def pre_back(l, shape, blob, base, tiles, dq, dkv, a, x, dh, gain, wq, wk, wv, cos, sin):
     m, d = x.shape
     scratch = [pltpu.VMEM((2, tiles, 16, 128), BF16), pltpu.VMEM((m, d), BF16), pltpu.SemaphoreType.DMA(())]
     args = (dq, dkv, a, x, dh, gain, wq, wk, wv, cos, sin)
-    return call(functools.partial(pre_back_kernel, base), [((m, d), F32)], args, "pre_back", scratch, blob=blob)
+    return call(functools.partial(pre_back_kernel, l, base), [(shape, F32)], args, "pre_back", scratch, blob=blob)
 
 
 def unpack_kernel(places, blob, *outs):
@@ -1026,11 +1128,11 @@
 
     for l, (ffn, att) in enumerate(places):
         up_at = (ff // 128) * t
-        down_at = 2 * up_at
-        out_at = down_at + wide_of(d) * (gd.shape[1] // 16)
+        low_at = 2 * up_at
+        out_at = low_at + (ff // 256) * (d // 16)
         take(ffn, 0, half, ff, gg, l)
         take(ffn, up_at, half, ff, gu, l)
-        take(ffn, down_at, gd.shape[1], d, gd, l)
+        take(ffn, low_at, d, ff // 2, gd, l)
         take(ffn, out_at, half, d, go, l)
         norm(ffn, out_at + wide_of(d) * t, g_ffn, l)
         take(att, 0, half, d, gq, l)
@@ -1050,17 +1152,16 @@
     seqs, r, d = tokens.shape
     m = seqs * r
     e, ff = w_key.shape[2], w_gate.shape[2]
-    own = (w_query, w_key, w_value, w_out, w_gate, w_up, w_down)
+    own = (w_query, w_key, w_value, w_out, w_gate, w_up, jnp.swapaxes(w_down, 1, 2))
     shards = [(w, l) for l in range(layers) for w in own]
     full = exchange([(norm_attn, None), (norm_ffn, None), *shards[:3]], 0)
-    gains = [jnp.swapaxes(v, 0, 1).reshape(layers, 1, d).astype(F32) for v in full[:2]]
-    full = full[2:]
+    gain_attn, gain_ffn, *full = full
     frequency = jnp.exp(jnp.arange(HEAD // 2, dtype=F32) * (-jnp.log(ROPE_BASE) / (HEAD // 2)))
     angles = positions.reshape(m, 1).astype(F32) * frequency
     cos, sin = jnp.cos(angles), jnp.sin(angles)
     cos = jnp.concatenate([cos] * 4, axis=1)
     sin = jnp.concatenate([-sin, sin] * 2, axis=1)
-    x = tokens.reshape(m, d)
+    x = jnp.swapaxes(tokens, 1, 2)
     kept = []
     weights = []
 
@@ -1069,24 +1170,28 @@
 
     for l in range(layers):
         wq, wk, wv = (joined(w) for w in full[l * len(own) : l * len(own) + 3])
-        a, q, kv = pre(x, gains[0][l], wq, wk, wv, cos, sin)
+        a, q, kv, *turned = pre(l, x, gain_attn, wq, wk, wv, cos, sin)
+        if turned:
+            (x,) = turned
         q = q.reshape(seqs, r, d)
         if l == 0:
             kv, places, *rest = all_gather_ctx(kv, n, 1, positions, shards[3:])
             full = [*full, *rest]
         else:
             (kv,) = all_gather_ctx(kv, n, 1 + l)
-        wo, wg, wu, wd = (joined(w) for w in full[l * len(own) + 3 : (l + 1) * len(own)])
+        wo, wg, wu = (joined(w) for w in full[l * len(own) + 3 : l * len(own) + 6])
+        wd = full[l * len(own) + 6]
         weights.append((wq, wk, wv, wo, wg, wu, wd))
         kv = kv.reshape(n, seqs, r, 2 * e)
         o, lse = attend(places, positions, q, kv)
-        h, b, gate, up, y = post(o.reshape(m, d), x, wo, gains[1][l], wg, wu, wd)
+        turned = (seqs, d, r) if l == layers - 1 else None
+        h, b, gate, up, y = post(l, o.reshape(m, d), x, wo, gain_ffn, wg, wu, wd, turned)
         kept.append((x, a, q, kv, o, lse, h, b, gate, up))
         x = y
-    output = x.reshape(seqs, r, d).astype(BF16)
-    dy = cotangent.reshape(m, d)
+    output = jnp.swapaxes(x, 1, 2)
+    dy = jnp.swapaxes(cotangent, 1, 2)
     one, two = ffn_tiles(d, ff), pre_tiles(d, e)
-    unit = 2 * PARTS * n
+    unit = 2 * n
     whole = -(-layers * (one + two) // unit) * unit
     blob = (2, whole, 16, 128)
     spots = []
@@ -1095,17 +1200,18 @@
         x, a, q, kv, o, lse, h, b, gate, up = kept[l]
         start = (layers - 1 - l) * (one + two)
         spots.insert(0, (start, start + one))
-        dh, do, blob = ffn_back(blob, start, dy, h, b, gate, up, o.reshape(m, d), gains[1][l], wo, wg, wu, wd)
+        dh, do, blob = ffn_back(l, blob, start, dy, h, b, gate, up, o.reshape(m, d), gain_ffn, wo, wg, wu, wd)
         dq, dkv = attend_back(places, positions, q, kv, do.reshape(seqs, r, d), o, lse)
         dkv = reduce_scatter_ctx(dkv.reshape(n, m, 2 * e), n, 1 + layers + l)
         tiles = two if l else whole - start - one
+        shape = (m, d) if l else (seqs, d, r)
         dy, blob = pre_back(
-            blob, start + one, tiles, dq.reshape(m, d), dkv, a, x, dh, gains[0][l], wq, wk, wv, cos, sin
+            l, shape, blob, start + one, tiles, dq.reshape(m, d), dkv, a, x, dh, gain_attn, wq, wk, wv, cos, sin
         )
-    total = reduce_all(blob.reshape(2, PARTS, n, -1, 128), n, 1 + 2 * layers)
+    total = reduce_all(blob.reshape(2, n, -1, 128), n, 1 + 2 * layers)
     shapes = [norm_attn.shape, *[w.shape for w in own[:4]], norm_ffn.shape, *[w.shape for w in own[4:]]]
     grads = unpack(total.reshape(whole, 16, 128), spots, shapes)
-    return (output, dy.reshape(seqs, r, d), *grads)
+    return (output, jnp.swapaxes(dy, 1, 2), *grads[:-1], jnp.swapaxes(grads[-1], 1, 2))
 
 
 def solution(mesh):

time: 538 us -> 460 us (0.86)
  Pallas kernels: 515 us -> 451 us
  local copies, waits for them, and re-layouts: 17 us -> 0 us
    pallas_call x13, Pallas kernels: 198 us -> 160 us  [call(): pl.pallas_call(kernel, out_shape=[jax.ShapeDtypeStruct(s, t) for s, t in...]
    pallas_call x1, Pallas kernels: 164 us -> 139 us  [reduce_all(): pl.pallas_call(functools.partial(reduce_all_kernel, g), out_shape=jax.Sha...]
    unnamed x8 -> x0, local copies, waits for them, and re-layouts: 14.3 us -> none
where the time goes in v3:
time: 460 us; the launch traced here: 454 us
  Pallas kernels  451 us (98%)
    pallas_call x13, Pallas kernels, call(): pl.pallas_call(kernel, out_shape=[jax.ShapeDtypeStruct(s, t) for s, t in...  160 us
    pallas_call x1, Pallas kernels, reduce_all(): pl.pallas_call(functools.partial(reduce_all_kernel, g), out_shape=jax.Sha...  139 us
    pallas_call x2, Pallas kernels, reduce_scatter_ctx(): pl.pallas_call(functools.partial(scatter_kernel, g), out_shape=jax.ShapeD...  84 us
    pallas_call x2, Pallas kernels, all_gather_ctx(): pl.pallas_call(functools.partial(gather_kernel, g, count, spots), out_sha...  66 us

profile of v3, /device:TPU:10, one launch (start us, length us, event | category | flops | bytes accessed | tf_op | source)
XLA Modules:
  0.0 454.2 jit_solution(10210016478293781949)
XLA Ops:
  0.7 0.7 convert_bitcast_fusion
  1.3 0.5 fusion
  1.9 1.0 pad_maximum_fusion
  2.9 2.6 exchange.1
  5.5 3.5 pre.2
  9.0 35.4 %ctx_gather.2 = (bf16[16,256,384]{2,1,0:T(8,128)(2,1)}, s32[16,2,128]{2,1,0:T(2,128)}, bf16[2,288,576]{2,1,0:T(8,128)(2,1)}, bf16[2,288,1536]{2,1,0:T(8,128)(2,1...) custom-call(bf16[256,384]{1,0:T(8,128)(2,1)} %get-tuple-element.77.r, ...), custom_call_target="tpu_custom_call" | custom-call | tf_op jit(solution)/shard_map/ctx_gather/pallas_call | solution.py:552
  44.3 16.4 %attend.2 = (f32[2,128,576]{2,1,0:T(8,128)}, f32[2,6,1,192]{3,2,1,0:T(1,128)}) custom-call(s32[16,2,128]{2,1,0:T(2,128)} %get-tuple-element.78.block_ref, s32[2,128]{1,0:T(2,128)} %mine_ref.7, bf16[2,128,576]{2,1,0:T(8,128)(2,1)} %bitcast.63, bf16[16,2,128,384]{3,2,1,0:T(8,128)(2,1)} %bitcast.38), custom_call_target="tpu_custom_call" | custom-call | tf_op jit(solution)/shard_map/attend/pallas_call | solution.py:654
  60.8 9.2 %post.2 = (f32[256,576]{1,0:T(8,128)}, bf16[256,576]{1,0:T(8,128)(2,1)}, f32[256,1536]{1,0:T(8,128)}, f32[256,1536]{1,0:T(8,128)}, f32[256,576]{1,0:T(8,128)}) custom-call(f32[256,576]{1,0:T(8,128)} %bitcast.48, f32[256,576]{1,0:T(8,128)} %get-tuple-element.82.x_ref.refs_3_, bf16[576,576]{1,0:T(8,128)(2,1)} %bitcast.56, ...), custom_call_target="tpu_custom_call" | custom-call | tf_op jit(solution)/shard_map/post/pallas_call | solution.py:654
  69.9 3.2 pre.3
  73.1 30.6 %ctx_gather.3 = bf16[16,256,384]{2,1,0:T(8,128)(2,1)} custom-call(bf16[256,384]{1,0:T(8,128)(2,1)} %get-tuple-element.93.refs_0_), custom_call_target="tpu_custom_call" | custom-call | tf_op jit(solution)/shard_map/ctx_gather/pallas_call | solution.py:552
  103.8 16.5 %attend.3 = (f32[2,128,576]{2,1,0:T(8,128)}, f32[2,6,1,192]{3,2,1,0:T(1,128)}) custom-call(s32[16,2,128]{2,1,0:T(2,128)} %get-tuple-element.78.block_ref, s32[2,128]{1,0:T(2,128)} %mine_ref.7, bf16[2,128,576]{2,1,0:T(8,128)(2,1)} %bitcast.65, bf16[16,2,128,384]{3,2,1,0:T(8,128)(2,1)} %bitcast.36), custom_call_target="tpu_custom_call" | custom-call | tf_op jit(solution)/shard_map/attend/pallas_call | solution.py:654
  120.2 9.0 %post.3 = (f32[256,576]{1,0:T(8,128)}, bf16[256,576]{1,0:T(8,128)(2,1)}, f32[256,1536]{1,0:T(8,128)}, f32[256,1536]{1,0:T(8,128)}, bf16[2,576,128]{2,1,0:T(8,128)(2,1)}) custom-call(f32[256,576]{1,0:T(8,128)} %bitcast.50, f32[256,576]{1,0:T(8,128)} %get-tuple-element.88.x_ref.refs_3_, bf16[576,576]{1,0:T(8,128)(2,1)} %bitcast.54, ...), custom_call_target="tpu_custom_call" | custom-call | tf_op jit(solution)/shard_map/post/pallas_call | solution.py:654
  129.2 13.7 %ffn_back.2 = (f32[256,576]{1,0:T(8,128)}, bf16[256,576]{1,0:T(8,128)(2,1)}, bf16[2,1792,16,128]{3,2,1,0:T(8,128)(2,1)}) custom-call(bf16[2,576,128]{2,1,0:T(8,128)(2,1)} %bitcast.79, f32[256,576]{1,0:T(8,128)} %get-tuple-element.100.refs_1_, bf16[256,576]{1,0:T(8,128)(2,1)} %get-tuple-element.101.refs_2_, f32[256,1536]{1,0:T(8,128)} %get-tuple-element.102.refs_3_, ...), custom_call_target="tpu_custom_call" | custom-call | tf_op jit(solution)/shard_map/ffn_back/pallas_call | solution.py:644
  142.9 27.3 %attend_back.2 = (f32[2,128,576]{2,1,0:T(8,128)}, bf16[16,2,128,384]{3,2,1,0:T(8,128)(2,1)}) custom-call(s32[16,2,128]{2,1,0:T(2,128)} %get-tuple-element.78.block_ref, s32[2,128]{1,0:T(2,128)} %mine_ref.7, bf16[2,128,576]{2,1,0:T(8,128)(2,1)} %bitcast.66, bf16[16,2,128,384]{3,2,1,0:T(8,128)(2,1)} %bitcast.37, bf16[2,128,576]{2,1,0:T(8,128)(2,1)} %bitcast.78, ...), custom_call_target="tpu_custom_call" | custom-call | tf_op jit(solution)/shard_map/attend_back/pallas_call | solution.py:654
  170.2 45.9 %ctx_reduce.2.refs_1_ = f32[256,384]{1,0:T(8,128)} custom-call(bf16[16,256,384]{2,1,0:T(8,128)(2,1)} %bitcast.53), custom_call_target="tpu_custom_call" | custom-call | tf_op jit(solution)/shard_map/ctx_reduce/pallas_call | solution.py:349
  216.1 5.6 %pre_back.2 = (f32[256,576]{1,0:T(8,128)}, bf16[2,1792,16,128]{3,2,1,0:T(8,128)(2,1)}) custom-call(f32[256,576]{1,0:T(8,128)} %bitcast.76, f32[256,384]{1,0:T(8,128)} %ctx_reduce.2.refs_1_, bf16[256,576]{1,0:T(8,128)(2,1)} %get-tuple-element.108.refs_2_, f32[256,576]{1,0:T(8,128)} %get-tuple-element.88.x_ref.refs_3_, ...), custom_call_target="tpu_custom_call", output_to_operand_aliasing={{1}: (11, {})} | custom-call | tf_op jit(solution)/shard_map/pre_back/pallas_call | solution.py:644
  221.7 14.0 %ffn_back.3 = (f32[256,576]{1,0:T(8,128)}, bf16[256,576]{1,0:T(8,128)(2,1)}, bf16[2,1792,16,128]{3,2,1,0:T(8,128)(2,1)}) custom-call(f32[256,576]{1,0:T(8,128)} %get-tuple-element.111.refs_0_, f32[256,576]{1,0:T(8,128)} %get-tuple-element.112.refs_1_, bf16[256,576]{1,0:T(8,128)(2,1)} %get-tuple-element.113.refs_2_, ...), custom_call_target="tpu_custom_call", output_to_operand_aliasing={{2}: (11, {})} | custom-call | tf_op jit(solution)/shard_map/ffn_back/pallas_call | solution.py:644
  235.7 27.1 %attend_back.3 = (f32[2,128,576]{2,1,0:T(8,128)}, bf16[16,2,128,384]{3,2,1,0:T(8,128)(2,1)}) custom-call(s32[16,2,128]{2,1,0:T(2,128)} %get-tuple-element.78.block_ref, s32[2,128]{1,0:T(2,128)} %mine_ref.7, bf16[2,128,576]{2,1,0:T(8,128)(2,1)} %bitcast.64, bf16[16,2,128,384]{3,2,1,0:T(8,128)(2,1)} %bitcast.39, bf16[2,128,576]{2,1,0:T(8,128)(2,1)} %bitcast.77, ...), custom_call_target="tpu_custom_call" | custom-call | tf_op jit(solution)/shard_map/attend_back/pallas_call | solution.py:654
  262.8 38.2 %ctx_reduce.3.refs_1_ = f32[256,384]{1,0:T(8,128)} custom-call(bf16[16,256,384]{2,1,0:T(8,128)(2,1)} %bitcast.52), custom_call_target="tpu_custom_call" | custom-call | tf_op jit(solution)/shard_map/ctx_reduce/pallas_call | solution.py:349
  301.0 5.6 %pre_back.3 = (f32[2,576,128]{2,1,0:T(8,128)}, bf16[2,1792,16,128]{3,2,1,0:T(8,128)(2,1)}) custom-call(f32[256,576]{1,0:T(8,128)} %bitcast.75, f32[256,384]{1,0:T(8,128)} %ctx_reduce.3.refs_1_, bf16[256,576]{1,0:T(8,128)(2,1)} %get-tuple-element.121.refs_2_, f32[256,576]{1,0:T(8,128)} %get-tuple-element.82.x_ref.refs_3_, ...), custom_call_target="tpu_custom_call", output_to_operand_aliasing={{1}: (11, {})} | custom-call | tf_op jit(solution)/shard_map/pre_back/pallas_call | solution.py:644
  306.6 138.9 %grad_reduce.1 = bf16[16,1792,128]{2,1,0:T(8,128)(2,1)} custom-call(bf16[2,16,1792,128]{3,2,1,0:T(8,128)(2,1)} %bitcast.34), custom_call_target="tpu_custom_call" | custom-call | tf_op jit(solution)/shard_map/grad_reduce/pallas_call | solution.py:441
  445.5 8.6 %unpack.1 = (f32[2,288]{1,0:T(2,128)}, f32[2,288,576]{2,1,0:T(8,128)}, f32[2,288,192]{2,1,0:T(8,128)}, f32[2,288,192]{2,1,0:T(8,128)}, f32[2,288,576]{2,1,0:T(8,...) custom-call(bf16[1792,16,128]{2,1,0:T(8,128)(2,1)} %bitcast.35), custom_call_target="tpu_custom_call" | custom-call | tf_op jit(solution)/shard_map/unpack/pallas_call | solution.py:654
  (1 shorter events, 0.0 us)

commit v4 on v3

--- a/solution.py
+++ b/solution.py
@@ -321,16 +321,15 @@
                 yield l[i]
 
 
-def scatter_kernel(g, x_ref, o_ref, acc, land, send, recv):
+def scatter_kernel(g, x_ref, o_ref, acc, send, recv, *lands):
     g.locate()
     entry_barrier(g, False)
-    rows = x_ref.shape[1] // 2
     rs = []
-    for p, order in enumerate(g.orders()):
-        at = pl.ds(p * rows, rows)
+    for p, (r0, rn, order) in enumerate(reduce_parts(g, x_ref.shape[1])):
+        at = pl.ds(r0, rn)
         own = (lambda at: lambda i: x_ref.at[i, at])(at)
         kept = (lambda at: lambda i: acc.at[i, at])(at)
-        rs.append(Reduce(g, order[::-1], own, kept, land.at[p], send.at[p], recv.at[p]))
+        rs.append(Reduce(g, order[::-1], own, kept, lands[p], send.at[p], recv.at[p]))
     for stage in range(len(g.dims)):
         for step in interleave([r.steps(stage) for r in rs]):
             step()
@@ -344,20 +343,21 @@
 def reduce_scatter_ctx(x, n, cid):
     g = Grid(n)
     _, rows, cols = x.shape
-    room = max(Reduce.room(g, o[::-1])[1] for o in g.orders())
+    cuts = reduce_parts(g, rows)
+    rooms = [Reduce.room(g, order[::-1])[1] for _, _, order in cuts]
     dma = pltpu.SemaphoreType.DMA
+    scratch = [pltpu.VMEM((n, rows, cols), x.dtype), dma((len(cuts), n)), dma((len(cuts), max(rooms)))]
+    scratch += [pltpu.VMEM((room, rn, cols), x.dtype) for room, (_, rn, _) in zip(rooms, cuts)]
+    out = ((rows, cols), jnp.float32)
     return pl.pallas_call(
         functools.partial(scatter_kernel, g),
-        out_shape=jax.ShapeDtypeStruct((rows, cols), jnp.float32),
+        out_shape=jax.ShapeDtypeStruct(*out),
         in_specs=[pl.BlockSpec(memory_space=pltpu.VMEM)],
         out_specs=pl.BlockSpec(memory_space=pltpu.VMEM),
-        scratch_shapes=[
-            pltpu.VMEM((n, rows, cols), x.dtype),
-            pltpu.VMEM((2, room, rows // 2, cols), x.dtype),
-            dma((2, n)),
-            dma((2, room)),
-        ],
-        compiler_params=pltpu.CompilerParams(collective_id=cid, has_side_effects=True, vmem_limit_bytes=60 << 20),
+        scratch_shapes=scratch,
+        compiler_params=pltpu.CompilerParams(
+            collective_id=cid, has_side_effects=True, vmem_limit_bytes=grant([(x.shape, x.dtype), out], scratch)
+        ),
         name="ctx_reduce",
     )(x)
 
@@ -377,7 +377,7 @@
     return [(*cut, orders[k]) for cut, (k, _) in zip(row_cuts(rows, [s for _, s in SHARES]), SHARES) if cut[1]]
 
 
-def reduce_all_kernel(g, x_ref, o_ref, own, kept, send, recv, gsend, grecv, psend, precv, lsem, *lands):
+def reduce_all_kernel(g, x_ref, o_ref, kept, send, recv, gsend, grecv, psend, precv, *lands):
     g.locate()
     entry_barrier(g, True)
     f = lax.axis_index(FSDP)
@@ -388,8 +388,6 @@
         to = (lambda r: lambda i: o_ref.at[i, r])(pl.ds(r0, rn))
         rs.append(Reduce(g, order[::-1], at, at, lands[p], send.at[p], recv.at[p]))
         gs.append(Gather(g, order, to(g.me), to, gsend.at[p], grecv.at[p]))
-    local = pltpu.make_async_copy(x_ref.at[f], own, lsem)
-    local.start()
     turns = [sorted(g.all, key=lambda d, a=r.order[0]: (d[a] == 0, -sum(1 for v in d if v))) for r in rs]
     pairs = {}
     for i in range(g.n):
@@ -402,13 +400,12 @@
                 recv_sem=precv.at[p, g.slot(d)], device_id=(g.me, 1 - f), device_id_type=MESH)
             c.start()
             pairs[p, d] = c
-    local.wait()
     for i in range(g.n):
         for p, r in enumerate(rs):
             d = turns[p][i]
             k = g.index(d)
             pairs[p, d].wait_recv()
-            add_into(r.acc(k), [r.acc(k), own.at[k, pl.ds(cuts[p][0], cuts[p][1])]])
+            add_into(r.acc(k), [r.acc(k), x_ref.at[f, k, pl.ds(cuts[p][0], cuts[p][1])]])
             a = r.order[0]
             if g.dims[a] == 2 and d[a]:
                 r.swap(d)
@@ -438,24 +435,25 @@
     parts = len(cuts)
     rooms = [Reduce.room(g, order[::-1])[1] for _, _, order in cuts]
     dma = pltpu.SemaphoreType.DMA
+    scratch = [
+        pltpu.VMEM((n, rows, cols), x.dtype),
+        dma((parts, n)),
+        dma((parts, max(rooms))),
+        dma((parts, 2, n)),
+        dma((parts, n)),
+        dma((parts, n)),
+        dma((parts, n)),
+    ] + [pltpu.VMEM((room, rn, cols), x.dtype) for room, (_, rn, _) in zip(rooms, cuts)]
+    out = ((n, rows, cols), x.dtype)
     return pl.pallas_call(
         functools.partial(reduce_all_kernel, g),
-        out_shape=jax.ShapeDtypeStruct((n, rows, cols), x.dtype),
-        in_specs=[pl.BlockSpec(memory_space=pl.ANY)],
+        out_shape=jax.ShapeDtypeStruct(*out),
+        in_specs=[pl.BlockSpec(memory_space=pltpu.VMEM)],
         out_specs=pl.BlockSpec(memory_space=pltpu.VMEM),
-        scratch_shapes=[
-            pltpu.VMEM((n, rows, cols), x.dtype),
-            pltpu.VMEM((n, rows, cols), x.dtype),
-            dma((parts, n)),
-            dma((parts, max(rooms))),
-            dma((parts, 2, n)),
-            dma((parts, n)),
-            dma((parts, n)),
-            dma((parts, n)),
-            dma(()),
-        ]
-        + [pltpu.VMEM((room, rn, cols), x.dtype) for room, (_, rn, _) in zip(rooms, cuts)],
-        compiler_params=pltpu.CompilerParams(collective_id=cid, has_side_effects=True, vmem_limit_bytes=64 << 20),
+        scratch_shapes=scratch,
+        compiler_params=pltpu.CompilerParams(
+            collective_id=cid, has_side_effects=True, vmem_limit_bytes=grant([out], scratch)
+        ),
         name="grad_reduce",
     )(x)
 
@@ -503,15 +501,17 @@
                 pltpu.make_async_remote_copy(
                     src_ref=s, dst_ref=d.at[f], send_sem=send.at[i], recv_sem=recv.at[i], device_id=(c, 1 - f),
                     device_id_type=MESH))
-            self.loads.append(pltpu.make_async_copy(s, v, load.at[i]))
-            self.stores.append(pltpu.make_async_copy(v, d.at[f], store.at[i]))
+            self.loads.append(pltpu.make_async_copy(s, d.at[f] if v is None else v, load.at[i]))
+            if v is not None:
+                self.stores.append(pltpu.make_async_copy(v, d.at[f], store.at[i]))
 
     def begin(self):
         for c in self.remote + self.loads:
             c.start()
-        for a, b in zip(self.loads, self.stores):
+        for i, a in enumerate(self.loads):
             a.wait()
-            b.start()
+            if self.stores:
+                self.stores[i].start()
 
     def end(self):
         for c in self.stores + self.remote:
@@ -520,6 +520,10 @@
     @staticmethod
     def scratch(picks):
         return [pltpu.SemaphoreType.DMA((len(picks),))] * 4 + [pltpu.VMEM(shape_of(a, l), a.dtype) for a, l in picks]
+
+
+def in_hbm(arrays):
+    return [pltpu.with_memory_space_constraint(a, pltpu.HBM) for a in arrays]
 
 
 def distinct(picks):
@@ -549,16 +553,18 @@
     dma = pltpu.SemaphoreType.DMA
     vmem, anywhere = pl.BlockSpec(memory_space=pltpu.VMEM), pl.BlockSpec(memory_space=pl.ANY)
     parts = len(xs) + 1
+    scratch = [dma((parts, 2, n)), dma((parts, n)), dma((2,))] + (Swap.scratch(weights) if count else [])
+    arrays_in_vmem = [(v.shape, v.dtype) for v in xs] + [((n, *v.shape), v.dtype) for v in xs]
     return pl.pallas_call(
         functools.partial(gather_kernel, g, count, spots),
         out_shape=[jax.ShapeDtypeStruct((n, *v.shape), v.dtype) for v in xs]
         + [jax.ShapeDtypeStruct((2, *shape_of(a, l)), a.dtype) for a, l in weights],
-        in_specs=[vmem] * len(xs) + [anywhere] * count,
+        in_specs=[vmem] * len(xs) + [pl.BlockSpec(memory_space=pltpu.HBM)] * count,
         out_specs=[vmem] * len(xs) + [anywhere] * len(weights),
-        scratch_shapes=[dma((parts, 2, n)), dma((parts, n)), dma((2,))] + (Swap.scratch(weights) if count else []),
-        compiler_params=pltpu.CompilerParams(collective_id=cid, has_side_effects=True, vmem_limit_bytes=60 << 20),
+        scratch_shapes=scratch,
+        compiler_params=pltpu.CompilerParams(collective_id=cid, has_side_effects=True, vmem_limit_bytes=grant(arrays_in_vmem, scratch)),
         name="ctx_gather",
-    )(*xs, *arrays)
+    )(*xs, *in_hbm(arrays))
 
 
 def exchange_kernel(count, spots, *refs):
@@ -567,23 +573,24 @@
     sem = pltpu.get_barrier_semaphore()
     pl.semaphore_signal(sem, inc=1, device_id=(c, 1 - f), device_id_type=MESH)
     pl.semaphore_wait(sem, 1)
-    swap = Swap(srcs, dsts, *refs[count + len(spots) :])
+    swap = Swap(srcs, dsts, *refs[count + len(spots) :], *[None] * len(spots))
     swap.begin()
     swap.end()
 
 
 def exchange(picks, cid):
     arrays, spots = distinct(picks)
-    anywhere = pl.BlockSpec(memory_space=pl.ANY)
+    vmem = pl.BlockSpec(memory_space=pltpu.VMEM)
+    outs = [((2, *shape_of(a, l)), a.dtype) for a, l in picks]
     return pl.pallas_call(
         functools.partial(exchange_kernel, len(arrays), spots),
-        out_shape=[jax.ShapeDtypeStruct((2, *shape_of(a, l)), a.dtype) for a, l in picks],
-        in_specs=[anywhere] * len(arrays),
-        out_specs=[anywhere] * len(picks),
-        scratch_shapes=Swap.scratch(picks),
-        compiler_params=pltpu.CompilerParams(collective_id=cid, has_side_effects=True),
+        out_shape=[jax.ShapeDtypeStruct(*o) for o in outs],
+        in_specs=[pl.BlockSpec(memory_space=pltpu.HBM)] * len(arrays),
+        out_specs=[vmem] * len(picks),
+        scratch_shapes=[pltpu.SemaphoreType.DMA((len(picks),))] * 4,
+        compiler_params=pltpu.CompilerParams(collective_id=cid, has_side_effects=True, vmem_limit_bytes=grant(outs)),
         name="exchange",
-    )(*arrays)
+    )(*in_hbm(arrays))
 
 
 HEADS = 9
@@ -594,7 +601,7 @@
 ROPE_BASE = 100000.0
 F32, BF16 = jnp.float32, jnp.bfloat16
 CHUNK = 256
-ROOM = 62 << 20
+SLACK = 1 << 20
 
 
 def nn(a, b):
@@ -635,10 +642,27 @@
     return out
 
 
+def padded(shape, dtype):
+    size = jnp.dtype(dtype).itemsize
+    dims = [1, 1, *shape]
+    tile = 32 // size
+    dims[-1], dims[-2] = -(-dims[-1] // 128) * 128, -(-dims[-2] // tile) * tile
+    return size * math.prod(dims)
+
+
+def grant(arrays, scratch=()):
+    total = sum(padded(s, t) for s, t in arrays)
+    for v in scratch:
+        if getattr(v, "memory_space", None) == pltpu.VMEM:
+            total += padded(v.shape, v.dtype)
+    return min(total + SLACK, 62 << 20)
+
+
 def call(kernel, outs, args, name, scratch=(), prefetch=0, blob=None):
     vmem = pl.BlockSpec(memory_space=pltpu.VMEM)
     smem = pl.BlockSpec(memory_space=pltpu.SMEM)
     anywhere = pl.BlockSpec(memory_space=pl.ANY)
+    room = grant([(a.shape, a.dtype) for a in args[prefetch:]] + list(outs), scratch)
     if blob is not None:
         new = isinstance(blob, tuple)
         return pl.pallas_call(
@@ -648,7 +672,7 @@
             out_specs=[vmem] * len(outs) + [anywhere],
             scratch_shapes=list(scratch),
             input_output_aliases={} if new else {len(args): len(outs)},
-            compiler_params=pltpu.CompilerParams(vmem_limit_bytes=ROOM),
+            compiler_params=pltpu.CompilerParams(vmem_limit_bytes=room),
             name=name,
         )(*args, *([] if new else [blob]))
     return pl.pallas_call(
@@ -657,7 +681,7 @@
         in_specs=[smem] * prefetch + [vmem] * (len(args) - prefetch),
         out_specs=[vmem] * len(outs),
         scratch_shapes=list(scratch),
-        compiler_params=pltpu.CompilerParams(vmem_limit_bytes=ROOM),
+        compiler_params=pltpu.CompilerParams(vmem_limit_bytes=room),
         name=name,
     )(*args)
 

time: 460 us -> 397 us (0.86)
  Pallas kernels: 451 us -> 388 us
    pallas_call x13, Pallas kernels: 160 us -> 114 us  [call(): pl.pallas_call(kernel, out_shape=[jax.ShapeDtypeStruct(s, t) for s, t in...]
    pallas_call x2, Pallas kernels: 84 us -> 67.7 us  [reduce_scatter_ctx(): pl.pallas_call(functools.partial(scatter_kernel, g), out_shape=jax.ShapeD...]
    pallas_call x2, Pallas kernels: 66 us -> 60.7 us  [all_gather_ctx(): pl.pallas_call(functools.partial(gather_kernel, g, count, spots), out_sha...]
    pallas_call x1, Pallas kernels: 139 us -> 144 us  [reduce_all(): pl.pallas_call(functools.partial(reduce_all_kernel, g), out_shape=jax.Sha...]
where the time goes in v4:
time: 397 us; the launch traced here: 392 us
  Pallas kernels  388 us (98%)
    pallas_call x1, Pallas kernels, reduce_all(): pl.pallas_call(functools.partial(reduce_all_kernel, g), out_shape=jax.Sha...  144 us
    pallas_call x13, Pallas kernels, call(): pl.pallas_call(kernel, out_shape=[jax.ShapeDtypeStruct(s, t) for s, t in...  114 us
    pallas_call x2, Pallas kernels, reduce_scatter_ctx(): pl.pallas_call(functools.partial(scatter_kernel, g), out_shape=jax.ShapeD...  67.7 us
    pallas_call x2, Pallas kernels, all_gather_ctx(): pl.pallas_call(functools.partial(gather_kernel, g, count, spots), out_sha...  60.7 us

profile of v4, /device:TPU:10, one launch (start us, length us, event | category | flops | bytes accessed | tf_op | source)
XLA Modules:
  0.0 392.4 jit_solution(3777145057458645332)
XLA Ops:
  0.7 0.7 convert_bitcast_fusion
  1.4 0.5 fusion
  1.9 0.3 pad_maximum_fusion
  2.2 2.5 exchange.1
  4.8 1.2 pre.2
  6.0 0.7 copy-done.14
  6.7 32.5 %ctx_gather.2 = (bf16[16,256,384]{2,1,0:T(8,128)(2,1)S(1)}, s32[16,2,128]{2,1,0:T(2,128)S(1)}, bf16[2,288,576]{2,1,0:T(8,128)(2,1)S(1)}, bf16[2,288,1536]{2,1,0:...) custom-call(bf16[256,384]{1,0:T(8,128)(2,1)S(1)} %get-tuple-element., ...), custom_call_target="tpu_custom_call" | custom-call | tf_op jit(solution)/shard_map/ctx_gather/pallas_call | solution.py:558
  39.3 14.4 %attend.2 = (f32[2,128,576]{2,1,0:T(8,128)S(1)}, f32[2,6,1,192]{3,2,1,0:T(1,128)S(1)}) custom-call(s32[16,2,128]{2,1,0:T(2,128)S(1)} %get-tuple-element.78.block_ref, s32[2,128]{1,0:T(2,128)S(1)} %copy-done.20, bf16[2,128,576]{2,1,0:T(8,128)(2,1)S(1)} %bitcast.62, bf16[16,2,128,384]{3,2,1,0:T(8,128)(2,1)S(1)} %bitcast.38), custom_call_target="tpu_custom_call" | custom-call | tf_op jit(solution)/shard_map/attend/pallas_call | solution.py:678
  53.7 4.4 %post.2 = (f32[256,576]{1,0:T(8,128)S(1)}, bf16[256,576]{1,0:T(8,128)(2,1)S(1)}, f32[256,1536]{1,0:T(8,128)S(1)}, f32[256,1536]{1,0:T(8,128)S(1)}, f32[256,576]{1,0:T(8,128)S(1)}) custom-call(f32[256,576]{1,0:T(8,128)S(1)} %bitcast.48, f32[256,576]{1,0:T(8,128)S(1)} %get-tuple-element.82.x_ref.refs_3_, bf16[576,576]{1,0:T(8,128)(2,1)S(1)} %bitcast.56, ...), custom_call_target="tpu_custom_call" | custom-call | tf_op jit(solution)/shard_map/post/pallas_call | solution.py:678
  58.0 0.7 copy-done.16
  58.8 1.0 pre.3
  59.7 28.2 %ctx_gather.3 = bf16[16,256,384]{2,1,0:T(8,128)(2,1)S(1)} custom-call(bf16[256,384]{1,0:T(8,128)(2,1)S(1)} %get-tuple-element.93.refs_0_), custom_call_target="tpu_custom_call" | custom-call | tf_op jit(solution)/shard_map/ctx_gather/pallas_call | solution.py:558
  87.9 14.4 %attend.3 = (f32[2,128,576]{2,1,0:T(8,128)S(1)}, f32[2,6,1,192]{3,2,1,0:T(1,128)S(1)}) custom-call(s32[16,2,128]{2,1,0:T(2,128)S(1)} %get-tuple-element.78.block_ref, s32[2,128]{1,0:T(2,128)S(1)} %copy-done.20, bf16[2,128,576]{2,1,0:T(8,128)(2,1)S(1)} %bitcast.64, bf16[16,2,128,384]{3,2,1,0:T(8,128)(2,1)S(1)} %bitcast.36), custom_call_target="tpu_custom_call" | custom-call | tf_op jit(solution)/shard_map/attend/pallas_call | solution.py:678
  102.3 5.2 %post.3 = (f32[256,576]{1,0:T(8,128)S(1)}, bf16[256,576]{1,0:T(8,128)(2,1)S(1)}, f32[256,1536]{1,0:T(8,128)S(1)}, f32[256,1536]{1,0:T(8,128)S(1)}, bf16[2,576,128]{2,1,0:T(8,128)(2,1)}) custom-call(f32[256,576]{1,0:T(8,128)S(1)} %bitcast.50, f32[256,576]{1,0:T(8,128)S(1)} %get-tuple-element.88.x_ref.refs_3_, bf16[576,576]{1,0:T(8,128)(2,1)S(1)} %bitcast.54, ...), custom_call_target="tpu_custom_call" | custom-call | tf_op jit(solution)/shard_map/post/pallas_call | solution.py:678
  107.5 7.6 %ffn_back.2 = (f32[256,576]{1,0:T(8,128)S(1)}, bf16[256,576]{1,0:T(8,128)(2,1)S(1)}, bf16[2,1792,16,128]{3,2,1,0:T(8,128)(2,1)S(1)}) custom-call(bf16[2,576,128]{2,1,0:T(8,128)(2,1)S(1)} %bitcast.78, f32[256,576]{1,0:T(8,128)S(1)} %get-tuple-element.100.refs_1_, bf16[256,576]{1,0:T(8,128)(2,1)S(1)} %get-tuple-element.101.refs_2_, ...), custom_call_target="tpu_custom_call" | custom-call | tf_op jit(solution)/shard_map/ffn_back/pallas_call | solution.py:668
  115.1 24.0 %attend_back.2 = (f32[2,128,576]{2,1,0:T(8,128)S(1)}, bf16[16,2,128,384]{3,2,1,0:T(8,128)(2,1)S(1)}) custom-call(s32[16,2,128]{2,1,0:T(2,128)S(1)} %get-tuple-element.78.block_ref, s32[2,128]{1,0:T(2,128)S(1)} %copy-done.20, bf16[2,128,576]{2,1,0:T(8,128)(2,1)S(1)} %bitcast.65, bf16[16,2,128,384]{3,2,1,0:T(8,128)(2,1)S(1)} %bitcast.37, ...), custom_call_target="tpu_custom_call" | custom-call | tf_op jit(solution)/shard_map/attend_back/pallas_call | solution.py:678
  139.1 36.9 %ctx_reduce.2.refs_1_ = f32[256,384]{1,0:T(8,128)S(1)} custom-call(bf16[16,256,384]{2,1,0:T(8,128)(2,1)S(1)} %bitcast.53), custom_call_target="tpu_custom_call" | custom-call | tf_op jit(solution)/shard_map/ctx_reduce/pallas_call | solution.py:352
  176.1 2.0 pre_back.2
  178.3 7.5 %ffn_back.3 = (f32[256,576]{1,0:T(8,128)S(1)}, bf16[256,576]{1,0:T(8,128)(2,1)S(1)}, bf16[2,1792,16,128]{3,2,1,0:T(8,128)(2,1)S(1)}) custom-call(f32[256,576]{1,0:T(8,128)S(1)} %get-tuple-element.111.refs_0_, f32[256,576]{1,0:T(8,128)S(1)} %copy-done.13, bf16[256,576]{1,0:T(8,128)(2,1)S(1)} %copy-done.17, ...), custom_call_target="tpu_custom_call", output_to_operand_aliasing={{2}: (11, {})} | custom-call | tf_op jit(solution)/shard_map/ffn_back/pallas_call | solution.py:668
  185.8 23.8 %attend_back.3 = (f32[2,128,576]{2,1,0:T(8,128)S(1)}, bf16[16,2,128,384]{3,2,1,0:T(8,128)(2,1)S(1)}) custom-call(s32[16,2,128]{2,1,0:T(2,128)S(1)} %get-tuple-element.78.block_ref, s32[2,128]{1,0:T(2,128)S(1)} %copy-done.20, bf16[2,128,576]{2,1,0:T(8,128)(2,1)S(1)} %bitcast.63, bf16[16,2,128,384]{3,2,1,0:T(8,128)(2,1)S(1)} %bitcast.39, ...), custom_call_target="tpu_custom_call" | custom-call | tf_op jit(solution)/shard_map/attend_back/pallas_call | solution.py:678
  209.7 30.8 %ctx_reduce.3.refs_1_ = f32[256,384]{1,0:T(8,128)S(1)} custom-call(bf16[16,256,384]{2,1,0:T(8,128)(2,1)S(1)} %bitcast.52), custom_call_target="tpu_custom_call" | custom-call | tf_op jit(solution)/shard_map/ctx_reduce/pallas_call | solution.py:352
  240.5 2.8 pre_back.3
  243.3 143.5 %grad_reduce.1 = bf16[16,1792,128]{2,1,0:T(8,128)(2,1)S(1)} custom-call(bf16[2,16,1792,128]{3,2,1,0:T(8,128)(2,1)S(1)} %bitcast.34), custom_call_target="tpu_custom_call" | custom-call | tf_op jit(solution)/shard_map/grad_reduce/pallas_call | solution.py:448
  386.8 5.6 %unpack.1 = (f32[2,288]{1,0:T(2,128)}, f32[2,288,576]{2,1,0:T(8,128)}, f32[2,288,192]{2,1,0:T(8,128)}, f32[2,288,192]{2,1,0:T(8,128)}, f32[2,288,576]{2,1,0:T(8,...) custom-call(bf16[1792,16,128]{2,1,0:T(8,128)(2,1)S(1)} %bitcast.35), custom_call_target="tpu_custom_call" | custom-call | tf_op jit(solution)/shard_map/unpack/pallas_call | solution.py:678
  (41 shorter events, 0.3 us)
Async XLA Ops:
  0.6 4.1 %copy-start.19 = (bf16[2,128,576]{1,2,0:T(8,128)(2,1)S(1)}, bf16[2,128,576]{1,2,0:T(8,128)(2,1)}, u32[]{:S(2)}) copy-start(bf16[2,128,576]{1,2,0:T(8,128)(2,1)} %param.12) | copy-start | bytes 884740
  2.2 4.5 %copy-start.20 = (s32[2,128]{1,0:T(2,128)S(1)}, s32[2,128]{1,0:T(2,128)}, u32[]{:S(2)}) copy-start(s32[2,128]{1,0:T(2,128)} %mine_ref.7) | copy-start | bytes 3076
  4.7 1.9 copy-start.2
  6.0 0.7 copy-start.14
  6.7 47.0 %copy-start.6 = (f32[256,576]{1,0:T(8,128)}, f32[256,576]{1,0:T(8,128)S(1)}, u32[]{:S(2)}) copy-start(f32[256,576]{1,0:T(8,128)S(1)} %get-tuple-element.82.x_ref.refs_3_) | copy-start | bytes 1769476
  39.2 14.4 %copy-start = (bf16[2,288,576]{2,1,0:T(8,128)(2,1)}, bf16[2,288,576]{2,1,0:T(8,128)(2,1)S(1)}, u32[]{:S(2)}) copy-start(bf16[2,288,576]{2,1,0:T(8,128)(2,1)S(1)} %get-tuple-element.83) | copy-start | bytes 1990660
  39.3 19.5 %copy-start.4 = (bf16[2,288,576]{2,1,0:T(8,128)(2,1)}, bf16[2,288,576]{2,1,0:T(8,128)(2,1)S(1)}, u32[]{:S(2)}) copy-start(bf16[2,288,576]{2,1,0:T(8,128)(2,1)S(1)} %get-tuple-element.89) | copy-start | bytes 1990660
  58.0 0.7 copy-start.16
  58.8 29.1 %copy-start.8 = (f32[256,1536]{1,0:T(8,128)}, f32[256,1536]{1,0:T(8,128)S(1)}, u32[]{:S(2)}) copy-start(f32[256,1536]{1,0:T(8,128)S(1)} %get-tuple-element.114.refs_3_) | copy-start | bytes 4718596
  58.8 29.2 %copy-start.10 = (f32[256,1536]{1,0:T(8,128)}, f32[256,1536]{1,0:T(8,128)S(1)}, u32[]{:S(2)}) copy-start(f32[256,1536]{1,0:T(8,128)S(1)} %get-tuple-element.115.refs_4_) | copy-start | bytes 4718596
  58.8 29.2 %copy-start.12 = (f32[256,576]{1,0:T(8,128)}, f32[256,576]{1,0:T(8,128)S(1)}, u32[]{:S(2)}) copy-start(f32[256,576]{1,0:T(8,128)S(1)} %get-tuple-element.112.refs_1_) | copy-start | bytes 1769476
  102.3 5.2 %copy-start.18 = (bf16[2,128,576]{1,2,0:T(8,128)(2,1)S(1)}, bf16[2,128,576]{1,2,0:T(8,128)(2,1)}, u32[]{:S(2)}) copy-start(bf16[2,128,576]{1,2,0:T(8,128)(2,1)} %param.23) | copy-start | bytes 884740
  139.1 36.9 %copy-start.5 = (bf16[2,288,576]{2,1,0:T(8,128)(2,1)S(1)}, bf16[2,288,576]{2,1,0:T(8,128)(2,1)}, u32[]{:S(2)}) copy-start(bf16[2,288,576]{2,1,0:T(8,128)(2,1)} %copy-done.4) | copy-start | bytes 1990660
  176.0 2.1 copy-start.1
  176.0 2.1 copy-start.9
  176.0 2.1 copy-start.11
  176.0 2.2 copy-start.13
  176.0 2.3 copy-start.17
  209.6 30.9 %copy-start.3 = (bf16[2,288,576]{2,1,0:T(8,128)(2,1)S(1)}, bf16[2,288,576]{2,1,0:T(8,128)(2,1)}, u32[]{:S(2)}) copy-start(bf16[2,288,576]{2,1,0:T(8,128)(2,1)} %copy-done.2) | copy-start | bytes 1990660
  209.6 30.9 %copy-start.7 = (f32[256,576]{1,0:T(8,128)S(1)}, f32[256,576]{1,0:T(8,128)}, u32[]{:S(2)}) copy-start(f32[256,576]{1,0:T(8,128)} %copy-done.6) | copy-start | bytes 1769476
  209.6 30.9 %copy-start.15 = (bf16[256,576]{1,0:T(8,128)(2,1)S(1)}, bf16[256,576]{1,0:T(8,128)(2,1)}, u32[]{:S(2)}) copy-start(bf16[256,576]{1,0:T(8,128)(2,1)} %copy-done.14) | copy-start | bytes 884740

commit v5 on v4

--- a/solution.py
+++ b/solution.py
@@ -12,6 +12,7 @@
 CTX, FSDP = "ctx", "fsdp"
 MESH = pl.DeviceIdType.MESH
 SHARES = ((0, 6), (1, 6), (2, 2), (3, 2))
+SUM_SHARES = ((0, 6), (1, 6), (2, 2), (3, 2))
 
 
 def factors(n):
@@ -159,13 +160,17 @@
                 pl.when(cond)(copy.wait_send)
 
 
-def run_gathers(g, gs, stages=None):
-    for stage in range(len(g.dims)):
-        lists = [q.labels(stage) for q in gs]
-        for i in range(max(map(len, lists))):
-            for q, l in zip(gs, lists):
-                if i < len(l):
-                    q.arrive(l[i], stage)
+def run_gathers(g, gs):
+    courses = [[(q, d, stage) for stage in range(len(g.dims)) for d in q.labels(stage)] for q in gs]
+    for q, d, stage in interleave(courses):
+        q.arrive(d, stage)
+
+
+def interleave(lists):
+    for i in range(max(map(len, lists))):
+        for l in lists:
+            if i < len(l):
+                yield l[i]
 
 
 def add_into(out, refs):
@@ -191,11 +196,6 @@
     def __init__(self, g, order, own, acc, land, send, recv):
         self.g, self.order, self.own, self.acc, self.land, self.send, self.recv = g, order, own, acc, land, send, recv
         self.sent = []
-        self.stage = 0
-
-    def held(self, delta):
-        ref = self.own if self.stage == 0 else self.acc
-        return ref(self.g.index(delta))
 
     @staticmethod
     def room(g, order):
@@ -258,14 +258,16 @@
             out += [functools.partial(self.close, d, stage) for d in keep]
         return out
 
+    def course(self):
+        return [step for stage in range(len(self.order)) for step in self.steps(stage)]
+
     def copy_all(self):
         for d in self.g.all:
             i = self.g.index(d)
             add_into(self.acc(i), [self.own(i)])
-        self.stage = 1
 
     def swap(self, d):
-        self.ship(self.held(d), d, 0, 1, 0, d)
+        self.ship(self.own(self.g.index(d)), d, 0, 1, 0, d)
 
     def next_ship(self, d, stage):
         if stage + 1 < len(self.order):
@@ -276,7 +278,7 @@
     def take(self, d, stage):
         a = self.order[stage]
         i = self.g.index(d)
-        ref = self.own(i) if stage == 0 and self.stage == 0 else self.acc(i)
+        ref = self.own(i) if stage == 0 else self.acc(i)
         add_into(self.acc(i), [ref, self.landed(stage, 0, put(1, d, a))])
         self.next_ship(d, stage)
 
@@ -314,27 +316,17 @@
             copy.wait_send()
 
 
-def interleave(lists):
-    for i in range(max(map(len, lists))):
-        for l in lists:
-            if i < len(l):
-                yield l[i]
-
-
 def scatter_kernel(g, x_ref, o_ref, acc, send, recv, *lands):
     g.locate()
     entry_barrier(g, False)
     rs = []
-    for p, (r0, rn, order) in enumerate(reduce_parts(g, x_ref.shape[1])):
+    for p, (r0, rn, order) in enumerate(reduce_parts(g, x_ref.shape[1], SUM_SHARES)):
         at = pl.ds(r0, rn)
         own = (lambda at: lambda i: x_ref.at[i, at])(at)
         kept = (lambda at: lambda i: acc.at[i, at])(at)
         rs.append(Reduce(g, order[::-1], own, kept, lands[p], send.at[p], recv.at[p]))
-    for stage in range(len(g.dims)):
-        for step in interleave([r.steps(stage) for r in rs]):
-            step()
-        for r in rs:
-            r.stage = 1
+    for step in interleave([r.course() for r in rs]):
+        step()
     o_ref[...] = acc[g.me].astype(jnp.float32)
     for r in rs:
         r.end()
@@ -343,7 +335,7 @@
 def reduce_scatter_ctx(x, n, cid):
     g = Grid(n)
     _, rows, cols = x.shape
-    cuts = reduce_parts(g, rows)
+    cuts = reduce_parts(g, rows, SUM_SHARES)
     rooms = [Reduce.room(g, order[::-1])[1] for _, _, order in cuts]
     dma = pltpu.SemaphoreType.DMA
     scratch = [pltpu.VMEM((n, rows, cols), x.dtype), dma((len(cuts), n)), dma((len(cuts), max(rooms)))]
@@ -371,17 +363,17 @@
     return out
 
 
-def reduce_parts(g, rows):
+def reduce_parts(g, rows, shares):
     rest = list(range(1, len(g.dims)))
     orders = [[0] + rest, [0] + rest[::-1], rest + [0], rest[::-1] + [0]]
-    return [(*cut, orders[k]) for cut, (k, _) in zip(row_cuts(rows, [s for _, s in SHARES]), SHARES) if cut[1]]
+    return [(*cut, orders[k]) for cut, (k, _) in zip(row_cuts(rows, [s for _, s in shares]), shares) if cut[1]]
 
 
 def reduce_all_kernel(g, x_ref, o_ref, kept, send, recv, gsend, grecv, psend, precv, *lands):
     g.locate()
     entry_barrier(g, True)
     f = lax.axis_index(FSDP)
-    cuts = reduce_parts(g, x_ref.shape[2])
+    cuts = reduce_parts(g, x_ref.shape[2], SHARES)
     rs, gs = [], []
     for p, (r0, rn, order) in enumerate(cuts):
         at = (lambda r: lambda i: kept.at[i, r])(pl.ds(r0, rn))
@@ -409,16 +401,14 @@
             a = r.order[0]
             if g.dims[a] == 2 and d[a]:
                 r.swap(d)
-    first = [[s for s in r.steps(0) if getattr(s, "func", s).__name__ in ("take", "pass_on", "close")] for r in rs]
-    for r in rs:
-        r.stage = 1
-    for stage in range(len(g.dims)):
-        lists = first if stage == 0 else [r.steps(stage) for r in rs]
-        for step in interleave(lists):
-            step()
-    for r, q in zip(rs, gs):
-        add_into(q.own, [r.acc(g.me)])
-        q.begin()
+    def begin(p):
+        add_into(gs[p].own, [rs[p].acc(g.me)])
+        gs[p].begin()
+
+    skip = ("swap", "copy_all")
+    courses = [[s for s in r.course() if getattr(s, "func", s).__name__ not in skip] for r in rs]
+    for step in interleave([course + [functools.partial(begin, p)] for p, course in enumerate(courses)]):
+        step()
     run_gathers(g, gs)
     for c in pairs.values():
         c.wait_send()
@@ -431,7 +421,7 @@
 def reduce_all(x, n, cid):
     g = Grid(n)
     _, _, rows, cols = x.shape
-    cuts = reduce_parts(g, rows)
+    cuts = reduce_parts(g, rows, SHARES)
     parts = len(cuts)
     rooms = [Reduce.room(g, order[::-1])[1] for _, _, order in cuts]
     dma = pltpu.SemaphoreType.DMA
@@ -467,14 +457,13 @@
     send, recv, local = refs[:3]
     g.locate()
     entry_barrier(g, bool(count))
-    rows = xs[0].shape[0] // 2
     gs = []
-    for p, order in enumerate(g.orders()):
-        at = pl.ds(p * rows, rows)
+    for p, (r0, rn, order) in enumerate(reduce_parts(g, xs[0].shape[0], SHARES)):
+        at = pl.ds(r0, rn)
         slot = (lambda at: lambda i: os[0].at[i, at])(at)
         gs.append(Gather(g, order, xs[0].at[at], slot, send.at[p], recv.at[p]))
     if count:
-        gs.append(Gather(g, g.orders()[0], xs[1], lambda i: os[1].at[i], send.at[2], recv.at[2]))
+        gs.append(Gather(g, g.orders()[0], xs[1], lambda i: os[1].at[i], send.at[len(gs)], recv.at[len(gs)]))
     for q in gs:
         q.begin()
     mine = [pltpu.make_async_copy(x, o.at[g.me], local.at[i]) for i, (x, o) in enumerate(zip(xs, os))]
@@ -552,7 +541,7 @@
     xs = [x] if places is None else [x, places]
     dma = pltpu.SemaphoreType.DMA
     vmem, anywhere = pl.BlockSpec(memory_space=pltpu.VMEM), pl.BlockSpec(memory_space=pl.ANY)
-    parts = len(xs) + 1
+    parts = len(SHARES) + 1
     scratch = [dma((parts, 2, n)), dma((parts, n)), dma((2,))] + (Swap.scratch(weights) if count else [])
     arrays_in_vmem = [(v.shape, v.dtype) for v in xs] + [((n, *v.shape), v.dtype) for v in xs]
     return pl.pallas_call(

time: 397 us -> 391 us (0.985)
  Pallas kernels: 388 us -> 383 us
    pallas_call x1, Pallas kernels: 144 us -> 139 us  [reduce_all(): pl.pallas_call(functools.partial(reduce_all_kernel, g), out_shape=jax.Sha...]
where the time goes in v5:
time: 391 us; the launch traced here: 387 us
  Pallas kernels  383 us (98%)
    pallas_call x1, Pallas kernels, reduce_all(): pl.pallas_call(functools.partial(reduce_all_kernel, g), out_shape=jax.Sha...  139 us
    pallas_call x13, Pallas kernels, call(): pl.pallas_call(kernel, out_shape=[jax.ShapeDtypeStruct(s, t) for s, t in...  114 us
    pallas_call x2, Pallas kernels, reduce_scatter_ctx(): pl.pallas_call(functools.partial(scatter_kernel, g), out_shape=jax.ShapeD...  67.8 us
    pallas_call x2, Pallas kernels, all_gather_ctx(): pl.pallas_call(functools.partial(gather_kernel, g, count, spots), out_sha...  59.3 us

profile of v5, /device:TPU:10, one launch (start us, length us, event | category | flops | bytes accessed | tf_op | source)
XLA Modules:
  0.0 386.9 jit_solution(9668054129132370040)
XLA Ops:
  0.7 0.7 convert_bitcast_fusion
  1.4 0.5 fusion
  1.9 0.3 pad_maximum_fusion
  2.2 2.5 exchange.1
  4.8 1.2 pre.2
  6.0 0.7 copy-done.14
  6.7 31.2 %ctx_gather.2 = (bf16[16,256,384]{2,1,0:T(8,128)(2,1)S(1)}, s32[16,2,128]{2,1,0:T(2,128)S(1)}, bf16[2,288,576]{2,1,0:T(8,128)(2,1)S(1)}, bf16[2,288,1536]{2,1,0:...) custom-call(bf16[256,384]{1,0:T(8,128)(2,1)S(1)} %get-tuple-element., ...), custom_call_target="tpu_custom_call" | custom-call | tf_op jit(solution)/shard_map/ctx_gather/pallas_call | solution.py:547
  37.9 14.4 %attend.2 = (f32[2,128,576]{2,1,0:T(8,128)S(1)}, f32[2,6,1,192]{3,2,1,0:T(1,128)S(1)}) custom-call(s32[16,2,128]{2,1,0:T(2,128)S(1)} %get-tuple-element.78.block_ref, s32[2,128]{1,0:T(2,128)S(1)} %copy-done.20, bf16[2,128,576]{2,1,0:T(8,128)(2,1)S(1)} %bitcast.62, bf16[16,2,128,384]{3,2,1,0:T(8,128)(2,1)S(1)} %bitcast.38), custom_call_target="tpu_custom_call" | custom-call | tf_op jit(solution)/shard_map/attend/pallas_call | solution.py:667
  52.3 4.4 %post.2 = (f32[256,576]{1,0:T(8,128)S(1)}, bf16[256,576]{1,0:T(8,128)(2,1)S(1)}, f32[256,1536]{1,0:T(8,128)S(1)}, f32[256,1536]{1,0:T(8,128)S(1)}, f32[256,576]{1,0:T(8,128)S(1)}) custom-call(f32[256,576]{1,0:T(8,128)S(1)} %bitcast.48, f32[256,576]{1,0:T(8,128)S(1)} %get-tuple-element.82.x_ref.refs_3_, bf16[576,576]{1,0:T(8,128)(2,1)S(1)} %bitcast.56, ...), custom_call_target="tpu_custom_call" | custom-call | tf_op jit(solution)/shard_map/post/pallas_call | solution.py:667
  56.7 0.7 copy-done.16
  57.4 1.0 pre.3
  58.4 28.1 %ctx_gather.3 = bf16[16,256,384]{2,1,0:T(8,128)(2,1)S(1)} custom-call(bf16[256,384]{1,0:T(8,128)(2,1)S(1)} %get-tuple-element.93.refs_0_), custom_call_target="tpu_custom_call" | custom-call | tf_op jit(solution)/shard_map/ctx_gather/pallas_call | solution.py:547
  86.5 14.4 %attend.3 = (f32[2,128,576]{2,1,0:T(8,128)S(1)}, f32[2,6,1,192]{3,2,1,0:T(1,128)S(1)}) custom-call(s32[16,2,128]{2,1,0:T(2,128)S(1)} %get-tuple-element.78.block_ref, s32[2,128]{1,0:T(2,128)S(1)} %copy-done.20, bf16[2,128,576]{2,1,0:T(8,128)(2,1)S(1)} %bitcast.64, bf16[16,2,128,384]{3,2,1,0:T(8,128)(2,1)S(1)} %bitcast.36), custom_call_target="tpu_custom_call" | custom-call | tf_op jit(solution)/shard_map/attend/pallas_call | solution.py:667
  100.9 5.2 %post.3 = (f32[256,576]{1,0:T(8,128)S(1)}, bf16[256,576]{1,0:T(8,128)(2,1)S(1)}, f32[256,1536]{1,0:T(8,128)S(1)}, f32[256,1536]{1,0:T(8,128)S(1)}, bf16[2,576,128]{2,1,0:T(8,128)(2,1)}) custom-call(f32[256,576]{1,0:T(8,128)S(1)} %bitcast.50, f32[256,576]{1,0:T(8,128)S(1)} %get-tuple-element.88.x_ref.refs_3_, bf16[576,576]{1,0:T(8,128)(2,1)S(1)} %bitcast.54, ...), custom_call_target="tpu_custom_call" | custom-call | tf_op jit(solution)/shard_map/post/pallas_call | solution.py:667
  106.1 7.6 %ffn_back.2 = (f32[256,576]{1,0:T(8,128)S(1)}, bf16[256,576]{1,0:T(8,128)(2,1)S(1)}, bf16[2,1792,16,128]{3,2,1,0:T(8,128)(2,1)S(1)}) custom-call(bf16[2,576,128]{2,1,0:T(8,128)(2,1)S(1)} %bitcast.78, f32[256,576]{1,0:T(8,128)S(1)} %get-tuple-element.100.refs_1_, bf16[256,576]{1,0:T(8,128)(2,1)S(1)} %get-tuple-element.101.refs_2_, ...), custom_call_target="tpu_custom_call" | custom-call | tf_op jit(solution)/shard_map/ffn_back/pallas_call | solution.py:657
  113.7 24.0 %attend_back.2 = (f32[2,128,576]{2,1,0:T(8,128)S(1)}, bf16[16,2,128,384]{3,2,1,0:T(8,128)(2,1)S(1)}) custom-call(s32[16,2,128]{2,1,0:T(2,128)S(1)} %get-tuple-element.78.block_ref, s32[2,128]{1,0:T(2,128)S(1)} %copy-done.20, bf16[2,128,576]{2,1,0:T(8,128)(2,1)S(1)} %bitcast.65, bf16[16,2,128,384]{3,2,1,0:T(8,128)(2,1)S(1)} %bitcast.37, ...), custom_call_target="tpu_custom_call" | custom-call | tf_op jit(solution)/shard_map/attend_back/pallas_call | solution.py:667
  137.7 36.4 %ctx_reduce.2.refs_1_ = f32[256,384]{1,0:T(8,128)S(1)} custom-call(bf16[16,256,384]{2,1,0:T(8,128)(2,1)S(1)} %bitcast.53), custom_call_target="tpu_custom_call" | custom-call | tf_op jit(solution)/shard_map/ctx_reduce/pallas_call | solution.py:344
  174.3 2.0 pre_back.2
  176.5 7.5 %ffn_back.3 = (f32[256,576]{1,0:T(8,128)S(1)}, bf16[256,576]{1,0:T(8,128)(2,1)S(1)}, bf16[2,1792,16,128]{3,2,1,0:T(8,128)(2,1)S(1)}) custom-call(f32[256,576]{1,0:T(8,128)S(1)} %get-tuple-element.111.refs_0_, f32[256,576]{1,0:T(8,128)S(1)} %copy-done.13, bf16[256,576]{1,0:T(8,128)(2,1)S(1)} %copy-done.17, ...), custom_call_target="tpu_custom_call", output_to_operand_aliasing={{2}: (11, {})} | custom-call | tf_op jit(solution)/shard_map/ffn_back/pallas_call | solution.py:657
  184.0 23.8 %attend_back.3 = (f32[2,128,576]{2,1,0:T(8,128)S(1)}, bf16[16,2,128,384]{3,2,1,0:T(8,128)(2,1)S(1)}) custom-call(s32[16,2,128]{2,1,0:T(2,128)S(1)} %get-tuple-element.78.block_ref, s32[2,128]{1,0:T(2,128)S(1)} %copy-done.20, bf16[2,128,576]{2,1,0:T(8,128)(2,1)S(1)} %bitcast.63, bf16[16,2,128,384]{3,2,1,0:T(8,128)(2,1)S(1)} %bitcast.39, ...), custom_call_target="tpu_custom_call" | custom-call | tf_op jit(solution)/shard_map/attend_back/pallas_call | solution.py:667
  207.9 31.3 %ctx_reduce.3.refs_1_ = f32[256,384]{1,0:T(8,128)S(1)} custom-call(bf16[16,256,384]{2,1,0:T(8,128)(2,1)S(1)} %bitcast.52), custom_call_target="tpu_custom_call" | custom-call | tf_op jit(solution)/shard_map/ctx_reduce/pallas_call | solution.py:344
  239.2 2.8 pre_back.3
  242.0 139.3 %grad_reduce.1 = bf16[16,1792,128]{2,1,0:T(8,128)(2,1)S(1)} custom-call(bf16[2,16,1792,128]{3,2,1,0:T(8,128)(2,1)S(1)} %bitcast.34), custom_call_target="tpu_custom_call" | custom-call | tf_op jit(solution)/shard_map/grad_reduce/pallas_call | solution.py:438
  381.3 5.6 %unpack.1 = (f32[2,288]{1,0:T(2,128)}, f32[2,288,576]{2,1,0:T(8,128)}, f32[2,288,192]{2,1,0:T(8,128)}, f32[2,288,192]{2,1,0:T(8,128)}, f32[2,288,576]{2,1,0:T(8,...) custom-call(bf16[1792,16,128]{2,1,0:T(8,128)(2,1)S(1)} %bitcast.35), custom_call_target="tpu_custom_call" | custom-call | tf_op jit(solution)/shard_map/unpack/pallas_call | solution.py:667
  (41 shorter events, 0.3 us)
Async XLA Ops:
  0.6 4.1 %copy-start.19 = (bf16[2,128,576]{1,2,0:T(8,128)(2,1)S(1)}, bf16[2,128,576]{1,2,0:T(8,128)(2,1)}, u32[]{:S(2)}) copy-start(bf16[2,128,576]{1,2,0:T(8,128)(2,1)} %param.12) | copy-start | bytes 884740
  2.2 4.5 %copy-start.20 = (s32[2,128]{1,0:T(2,128)S(1)}, s32[2,128]{1,0:T(2,128)}, u32[]{:S(2)}) copy-start(s32[2,128]{1,0:T(2,128)} %mine_ref.7) | copy-start | bytes 3076
  4.7 1.9 copy-start.2
  6.0 0.7 copy-start.14
  6.7 45.6 %copy-start.6 = (f32[256,576]{1,0:T(8,128)}, f32[256,576]{1,0:T(8,128)S(1)}, u32[]{:S(2)}) copy-start(f32[256,576]{1,0:T(8,128)S(1)} %get-tuple-element.82.x_ref.refs_3_) | copy-start | bytes 1769476
  37.9 14.4 %copy-start = (bf16[2,288,576]{2,1,0:T(8,128)(2,1)}, bf16[2,288,576]{2,1,0:T(8,128)(2,1)S(1)}, u32[]{:S(2)}) copy-start(bf16[2,288,576]{2,1,0:T(8,128)(2,1)S(1)} %get-tuple-element.83) | copy-start | bytes 1990660
  37.9 19.5 %copy-start.4 = (bf16[2,288,576]{2,1,0:T(8,128)(2,1)}, bf16[2,288,576]{2,1,0:T(8,128)(2,1)S(1)}, u32[]{:S(2)}) copy-start(bf16[2,288,576]{2,1,0:T(8,128)(2,1)S(1)} %get-tuple-element.89) | copy-start | bytes 1990660
  56.7 0.7 copy-start.16
  57.4 29.1 %copy-start.8 = (f32[256,1536]{1,0:T(8,128)}, f32[256,1536]{1,0:T(8,128)S(1)}, u32[]{:S(2)}) copy-start(f32[256,1536]{1,0:T(8,128)S(1)} %get-tuple-element.114.refs_3_) | copy-start | bytes 4718596
  57.4 29.1 %copy-start.10 = (f32[256,1536]{1,0:T(8,128)}, f32[256,1536]{1,0:T(8,128)S(1)}, u32[]{:S(2)}) copy-start(f32[256,1536]{1,0:T(8,128)S(1)} %get-tuple-element.115.refs_4_) | copy-start | bytes 4718596
  57.4 29.1 %copy-start.12 = (f32[256,576]{1,0:T(8,128)}, f32[256,576]{1,0:T(8,128)S(1)}, u32[]{:S(2)}) copy-start(f32[256,576]{1,0:T(8,128)S(1)} %get-tuple-element.112.refs_1_) | copy-start | bytes 1769476
  100.9 5.2 %copy-start.18 = (bf16[2,128,576]{1,2,0:T(8,128)(2,1)S(1)}, bf16[2,128,576]{1,2,0:T(8,128)(2,1)}, u32[]{:S(2)}) copy-start(bf16[2,128,576]{1,2,0:T(8,128)(2,1)} %param.23) | copy-start | bytes 884740
  137.7 36.5 %copy-start.5 = (bf16[2,288,576]{2,1,0:T(8,128)(2,1)S(1)}, bf16[2,288,576]{2,1,0:T(8,128)(2,1)}, u32[]{:S(2)}) copy-start(bf16[2,288,576]{2,1,0:T(8,128)(2,1)} %copy-done.4) | copy-start | bytes 1990660
  174.2 2.1 copy-start.1
  174.2 2.1 copy-start.9
  174.2 2.1 copy-start.11
  174.2 2.2 copy-start.13
  174.2 2.3 copy-start.17
  207.8 31.4 %copy-start.3 = (bf16[2,288,576]{2,1,0:T(8,128)(2,1)S(1)}, bf16[2,288,576]{2,1,0:T(8,128)(2,1)}, u32[]{:S(2)}) copy-start(bf16[2,288,576]{2,1,0:T(8,128)(2,1)} %copy-done.2) | copy-start | bytes 1990660
  207.8 31.4 %copy-start.7 = (f32[256,576]{1,0:T(8,128)S(1)}, f32[256,576]{1,0:T(8,128)}, u32[]{:S(2)}) copy-start(f32[256,576]{1,0:T(8,128)} %copy-done.6) | copy-start | bytes 1769476
  207.9 31.4 %copy-start.15 = (bf16[256,576]{1,0:T(8,128)(2,1)S(1)}, bf16[256,576]{1,0:T(8,128)(2,1)}, u32[]{:S(2)}) copy-start(bf16[256,576]{1,0:T(8,128)(2,1)} %copy-done.14) | copy-start | bytes 884740
